TPU v7x, 32 devices: a whole 2x2x4 slice. The times are simulated.
32 devices in a mesh: ctx: 8 (over y, x, core), mp: 4 (over z).
Axes of the slice: x: 2, y: 2, z: 4, core: 2. Of those that a mesh axis runs over, the one named last changes fastest.
Arguments:
- tokens: bfloat16 [4096, 8192], P('ctx', 'mp'), may hold values from -12 to 12
- norm_gain: bfloat16 [8192], replicated, may hold values from 0.099609375 to 1.8984375
- router_weight: bfloat16 [8192], replicated, may hold values from -0.0625 to 0.0625
- query_weight: bfloat16 [8192, 4096], P('ctx', 'mp'), may hold values from -2 to 2
- key_weight: bfloat16 [8192, 1024], P('ctx', 'mp'), may hold values from -1 to 1
- value_weight: bfloat16 [8192, 1024], P('ctx', 'mp'), may hold values from -0.0625 to 0.0625
- out_weight: bfloat16 [4096, 8192], P('mp', 'ctx'), may hold values from -0.1875 to 0.1875
- mlp_gain: bfloat16 [8192], P('mp'), may hold values from 0.099609375 to 1.8984375
- gate_weight: bfloat16 [8192, 28672], P('mp', 'ctx'), may hold values from -0.0625 to 0.0625
- up_weight: bfloat16 [8192, 28672], P('mp', 'ctx'), may hold values from -0.0625 to 0.0625
- down_weight: bfloat16 [28672, 8192], P('ctx', 'mp'), may hold values from -0.0625 to 0.0625
- destination: int32 [4096], P('ctx'), may hold values from -1 to 511, as said below
- kept_pos: int32 [512], P('ctx'), may hold values from 0 to 4095, as said below
Outputs:
- layer_out: bfloat16 [4096, 8192], P('ctx', 'mp')
Inputs may be any that keep to these rules, and one draw needn't show every extreme that they name: A token that skips the block has -1. The kept tokens, counted in sequence order as k = 0, 1, ..., 511, have destination (k mod 8) * 64 + (k div 8): owner k mod 8, slot k div 8 of that owner. Each shard of 512 tokens keeps from 32 to 96 tokens, and in every draw some shard keeps exactly 96; so at most 12 kept tokens of one shard have one owner, and that most is reached in every draw. kept_pos[destination[t]] = t for every kept token t.
All inputs are finite; a program needn't handle non-finite values.
Results may differ from a plain program's by a relative error of at most 0.0055.
Values may be sent and summed in bfloat16 or wider, within the bound.
No kernel may reach another device: no remote copies, remote signals or barrier semaphores. Data moves between devices by JAX's collectives and lax.ppermute only.
A program may use at most 128 MiB of HBM per device.

v0:
```python
import jax
import jax.numpy as jnp
from jax import lax
from jax.sharding import PartitionSpec as P

HEAD_DIM = 128


def rotate(values, positions):
    half_dim = values.shape[-1] // 2
    exponent = jnp.arange(half_dim, dtype=jnp.float32) * (2.0 / values.shape[-1])
    frequency = 500000.0 ** (-exponent)
    angles = positions.astype(jnp.float32)[:, None] * frequency[None, :]
    cosine = jnp.cos(angles)[:, None, :]
    sine_part = jnp.sin(angles)[:, None, :]
    first_half = values[..., :half_dim]
    second_half = values[..., half_dim:]
    return jnp.concatenate(
        [
            first_half * cosine - second_half * sine_part,
            second_half * cosine + first_half * sine_part,
        ],
        axis=-1,
    )


def body(
    tokens,
    norm_gain,
    router_weight,
    query_weight,
    key_weight,
    value_weight,
    out_weight,
    mlp_gain,
    gate_weight,
    up_weight,
    down_weight,
    destination,
    kept_pos,
):
    ctx_count = lax.axis_size("ctx")
    mp_count = lax.axis_size("mp")
    my_index = lax.axis_index("ctx")
    tok_dev = tokens.shape[0]
    kept_dev = kept_pos.shape[0]
    feature_cols = tokens.shape[1]
    feature_total = feature_cols * mp_count
    capacity = (3 * kept_dev // 2 + ctx_count - 1) // ctx_count
    slots_all = ctx_count * capacity
    head_dim = HEAD_DIM
    query_cols = query_weight.shape[1]
    key_cols = key_weight.shape[1]
    kv_local = key_cols // head_dim
    q_local = query_cols // head_dim
    group_size = q_local // kv_local
    peer_ids = jnp.arange(ctx_count, dtype=jnp.int32)
    is_kept = destination >= 0
    owner_ids = destination // kept_dev
    slot_ids = destination % kept_dev
    kept_order = slot_ids * ctx_count + owner_ids
    first_order = jnp.min(jnp.where(is_kept, kept_order, ctx_count * kept_dev))
    first_slots = (first_order - peer_ids + ctx_count - 1) // ctx_count
    owner_match = owner_ids[:, None] == peer_ids[None, :]
    send_index = (
        owner_ids * capacity
        + slot_ids
        - jnp.sum(jnp.where(owner_match, first_slots[None, :], 0), axis=1)
    )
    send_index = jnp.where(is_kept, send_index, slots_all)
    token_ids = jnp.arange(tok_dev, dtype=jnp.int32)
    picked = jnp.full((slots_all,), tok_dev, jnp.int32).at[send_index].set(token_ids, mode="drop")
    outgoing = jnp.take(tokens, picked, axis=0, mode="fill", fill_value=0).reshape(
        ctx_count, capacity, feature_cols
    )
    incoming = lax.all_to_all(outgoing, "ctx", split_axis=0, concat_axis=0, tiled=True).reshape(
        slots_all, feature_cols
    )
    slot_range = jnp.arange(kept_dev, dtype=jnp.int32)
    source_ids = kept_pos // tok_dev
    source_match = source_ids[:, None] == peer_ids[None, :]
    first_from = jnp.min(jnp.where(source_match, slot_range[:, None], kept_dev), axis=0)
    recv_index = (
        source_ids * capacity
        + slot_range
        - jnp.sum(jnp.where(source_match, first_from[None, :], 0), axis=1)
    )
    local_rows = incoming[recv_index]
    full_rows = lax.all_gather(local_rows, "mp", axis=1, tiled=True)
    raw_rows = full_rows.astype(jnp.float32)
    mean_square = jnp.mean(raw_rows * raw_rows, axis=-1, keepdims=True)
    normed = (raw_rows * lax.rsqrt(mean_square + 1e-05) * norm_gain.astype(jnp.float32)).astype(
        jnp.bfloat16
    )
    router_score = jax.nn.sigmoid(
        jnp.dot(full_rows, router_weight, preferred_element_type=jnp.float32)
    )
    slices = lax.all_to_all(normed, "ctx", split_axis=1, concat_axis=0, tiled=True)
    stacked = jnp.concatenate([query_weight, key_weight, value_weight], axis=1)
    projected = lax.psum_scatter(
        jnp.dot(slices, stacked, preferred_element_type=jnp.float32),
        "ctx",
        scatter_dimension=0,
        tiled=True,
    )
    query_proj = projected[:, :query_cols]
    key_proj = projected[:, query_cols : query_cols + key_cols]
    value_proj = projected[:, query_cols + key_cols :]
    queries = rotate(query_proj.reshape(kept_dev, q_local, head_dim), kept_pos).astype(jnp.bfloat16)
    queries = queries.reshape(kept_dev, kv_local, group_size, head_dim)
    key_rows = (
        rotate(key_proj.reshape(kept_dev, kv_local, head_dim), kept_pos)
        .astype(jnp.bfloat16)
        .reshape(kept_dev, key_cols)
    )
    value_rows = value_proj.astype(jnp.bfloat16)
    query_order = slot_range * ctx_count + my_index
    softmax_scale = head_dim ** (-0.5)
    running_max = jnp.full((kept_dev, kv_local, group_size), -1e30, jnp.float32)
    key_piece = lax.all_gather(key_rows, "ctx", axis=0, tiled=True)
    value_piece = lax.all_gather(value_rows, "ctx", axis=0, tiled=True)
    piece_rows = key_piece.shape[0]
    key_piece = key_piece.reshape(piece_rows, kv_local, head_dim)
    value_piece = value_piece.reshape(piece_rows, kv_local, head_dim).astype(jnp.float32)
    row_ids = jnp.arange(piece_rows, dtype=jnp.int32)
    key_order = row_ids % kept_dev * ctx_count + row_ids // kept_dev
    allowed = (key_order[None, :] <= query_order[:, None])[:, None, None, :]
    scores = (
        jnp.einsum("qhgd,khd->qhgk", queries, key_piece, preferred_element_type=jnp.float32)
        * softmax_scale
    )
    scores = jnp.where(allowed, scores, -1e30)
    new_max = jnp.maximum(running_max, jnp.max(scores, axis=-1))
    weights = jnp.where(allowed, jnp.exp(scores - new_max[..., None]), 0.0)
    running_sum = jnp.sum(weights, axis=-1)
    weighted = jnp.einsum("qhgk,khd->qhgd", weights, value_piece)
    attended = (
        (weighted / running_sum[..., None]).reshape(kept_dev, query_cols).astype(jnp.bfloat16)
    )
    every_head = lax.all_gather(attended, "ctx", axis=0, tiled=True)
    partial_cols = jnp.dot(every_head, out_weight, preferred_element_type=jnp.float32)
    head_delta = lax.all_to_all(
        partial_cols.astype(jnp.bfloat16), "ctx", split_axis=0, concat_axis=1, tiled=True
    ).astype(partial_cols.dtype)
    head_share = lax.psum_scatter(
        head_delta.astype(jnp.bfloat16), "mp", scatter_dimension=1, tiled=True
    ).astype(jnp.float32)
    mixed_share = local_rows.astype(jnp.float32) + head_share
    square_sum = lax.psum(jnp.sum(mixed_share * mixed_share, axis=1), "mp")
    second_normed = (
        mixed_share
        * lax.rsqrt(square_sum / feature_total + 1e-05)[:, None]
        * mlp_gain.astype(jnp.float32)
    ).astype(jnp.bfloat16)
    every_normed = lax.all_gather(second_normed, "ctx", axis=0, tiled=True)
    hidden_cols = gate_weight.shape[1]
    gate_block = jnp.dot(every_normed, gate_weight, preferred_element_type=jnp.float32)
    up_block = jnp.dot(every_normed, up_weight, preferred_element_type=jnp.float32)
    gate_up = lax.psum_scatter(
        jnp.concatenate([gate_block, up_block], axis=1).astype(jnp.bfloat16),
        "mp",
        scatter_dimension=0,
        tiled=True,
    ).astype(jnp.float32)
    hidden = (jax.nn.silu(gate_up[:, :hidden_cols]) * gate_up[:, hidden_cols:]).astype(jnp.bfloat16)
    mlp_partial = jnp.dot(
        lax.all_gather(hidden, "mp", axis=0, tiled=True),
        down_weight,
        preferred_element_type=jnp.float32,
    )
    mlp_share = lax.psum_scatter(
        mlp_partial.astype(jnp.bfloat16), "ctx", scatter_dimension=0, tiled=True
    ).astype(jnp.float32)
    update = (router_score[:, None] * (head_share + mlp_share)).astype(jnp.bfloat16)
    returning = (
        jnp.zeros((slots_all, feature_cols), jnp.bfloat16)
        .at[recv_index]
        .set(update)
        .reshape(ctx_count, capacity, feature_cols)
    )
    returned = lax.all_to_all(returning, "ctx", split_axis=0, concat_axis=0, tiled=True).reshape(
        slots_all, feature_cols
    )
    arriving = jnp.take(returned, send_index, axis=0, mode="fill", fill_value=0)
    return (tokens.astype(jnp.float32) + arriving.astype(jnp.float32)).astype(jnp.bfloat16)


def solution(mesh):
    in_specs = (
        P("ctx", "mp"),
        P(),
        P(),
        P("ctx", "mp"),
        P("ctx", "mp"),
        P("ctx", "mp"),
        P("mp", "ctx"),
        P("mp"),
        P("mp", "ctx"),
        P("mp", "ctx"),
        P("ctx", "mp"),
        P("ctx"),
        P("ctx"),
    )
    out_specs = P("ctx", "mp")
    return jax.shard_map(body, mesh=mesh, in_specs=in_specs, out_specs=out_specs, check_vma=False)
```

profile of v0, /device:TPU:0, one launch (start us, length us, event | category | flops | bytes accessed | tf_op | source)
XLA Modules:
  0.0 584.7 jit_solution(6739190528111375991)
XLA Ops:
  9.5 2.4 scatter_custom_fusion
  12.0 3.1 gather_fusion
  16.1 5.2 all-to-all-start
  21.6 9.4 %all-to-all-done = bf16[8,12,2048]{2,1,0:T(8,128)(2,1)S(1)} async-done(((bf16[8,12,2048]{2,1,0:T(8,128)(2,1)}), bf16[8,12,2048]{2,1,0:T(8,128)(2,1)S(1)}, u32[]{:S(2)}, u32[]{:S(2)}) %all-to-all-start) | async-done | bytes 393248 | tf_op jit(solution)/shard_map/all_to_all | solution.py:76
  32.7 27.4 %all-gather.12.cloned.1.call-done = bf16[64,8192]{1,0:T(8,128)(2,1)} async-done(((bf16[64,2048]{1,0:T(8,128)(2,1)}), bf16[64,8192]{1,0:T(8,128)(2,1)}) %all-gather.12.cloned.1.call-update) | async-done | bytes 1048592 | tf_op jit(solution)/shard_map/all_gather | solution.py:89
  60.1 1.5 fusion.6
  61.7 1.7 fusion.8
  63.5 18.8 %all_to_all.48 = bf16[64,8,1024]{2,0,1:T(8,128)(2,1)S(1)} all-to-all(bf16[64,8,1024]{2,0,1:T(8,128)(2,1)S(1)} %bitcast.62), channel_id=1, replica_groups=mesh['ctx'=8,'mp'=4] {'ctx'}, dimensions={1} | all-to-all | bytes 2097152 | tf_op jit(solution)/shard_map/all_to_all | solution.py:98
  82.3 3.5 fusion
  86.1 43.4 %reduce-scatter.5.cloned.1.call-done = f32[64,1536]{1,0:T(8,128)} async-done(((f32[512,1536]{1,0:T(8,128)}), f32[64,1536]{1,0:T(8,128)}) %reduce-scatter.5.cloned.1.call-update) | async-done | bytes 393232 | tf_op jit(solution)/shard_map/reduce_scatter | solution.py:100
  132.0 9.3 %all_gather.20 = bf16[512,256]{1,0:T(8,128)(2,1)S(1)} all-gather(bf16[64,256]{1,0:T(8,128)(2,1)S(1)} %bitcast.71), channel_id=1, replica_groups=mesh['ctx'=8,'mp'=4] {'ctx'}, dimensions={0}, use_global_device_ids=true | all-gather | bytes 294912 | tf_op jit(solution)/shard_map/all_gather | solution.py:120
  142.2 8.3 %all_gather.19 = bf16[512,256]{1,0:T(8,128)(2,1)S(1)} all-gather(bf16[64,256]{1,0:T(8,128)(2,1)S(1)} %slice.66), channel_id=1, replica_groups=mesh['ctx'=8,'mp'=4] {'ctx'}, dimensions={0}, use_global_device_ids=true | all-gather | bytes 294912 | tf_op jit(solution)/shard_map/all_gather | solution.py:121
  152.7 23.5 %all-gather.6.cloned.1.call-done = bf16[512,1024]{1,0:T(8,128)(2,1)} async-done(((bf16[64,1024]{1,0:T(8,128)(2,1)}), bf16[512,1024]{1,0:T(8,128)(2,1)}) %all-gather.6.cloned.1.call-update) | async-done | bytes 1048592 | tf_op jit(solution)/shard_map/all_gather | solution.py:140
  176.2 2.5 convolution_convert_fusion.3
  178.7 18.0 %all_to_all.49 = bf16[8,64,1024]{2,1,0:T(8,128)(2,1)S(1)} all-to-all(bf16[8,64,1024]{2,1,0:T(8,128)(2,1)S(1)} %bitcast.67), channel_id=1, replica_groups=mesh['ctx'=8,'mp'=4] {'ctx'}, dimensions={0} | all-to-all | bytes 2097152 | tf_op jit(solution)/shard_map/all_to_all | solution.py:142
  197.9 26.5 %reduce-scatter.7.cloned.1.call-done = bf16[64,2048]{1,0:T(8,128)(2,1)} async-done(((bf16[64,8192]{1,0:T(8,128)(2,1)}), bf16[64,2048]{1,0:T(8,128)(2,1)}) %reduce-scatter.7.cloned.1.call-update) | async-done | bytes 262160 | tf_op jit(solution)/shard_map/reduce_scatter | solution.py:145
  225.5 9.3 %psum.7 = f32[64]{0:T(128)S(1)} all-reduce(f32[64]{0:T(128)S(1)} %multiply_reduce_fusion), channel_id=1, replica_groups=mesh['ctx'=8,'mp'=4] {'mp'}, use_global_device_ids=true, to_apply=%region_11.12 | all-reduce | flops 64 | bytes 512 | tf_op jit(solution)/shard_map/psum | solution.py:149
  234.8 1.8 multiply_convert_fusion
  236.8 26.4 %all-gather.8.cloned.1.call-done = bf16[512,2048]{1,0:T(8,128)(2,1)} async-done(((bf16[64,2048]{1,0:T(8,128)(2,1)}), bf16[512,2048]{1,0:T(8,128)(2,1)}) %all-gather.8.cloned.1.call-update) | async-done | bytes 2097168 | tf_op jit(solution)/shard_map/all_gather | solution.py:155
  263.2 15.1 %convolution_convert_fusion = bf16[512,3584]{1,0:T(8,128)(2,1)} fusion(bf16[512,2048]{1,0:T(8,128)(2,1)} %all-gather.8.cloned.1.call-done, bf16[2048,3584]{1,0:T(8,128)(2,1)} %param.22), kind=kOutput, calls=%fused_computation.6 | convolution fusion | flops 7518027776 | bytes 20447232 | tf_op jit(solution)/shard_map/dot_general | solution.py:158
  278.3 12.4 %convolution_convert_fusion.1 = bf16[512,3584]{1,0:T(8,128)(2,1)} fusion(bf16[512,2048]{1,0:T(8,128)(2,1)S(1)} %copy-done.9, bf16[2048,3584]{1,0:T(8,128)(2,1)} %param.21), kind=kOutput, calls=%fused_computation.7 | convolution fusion | flops 7518027776 | bytes 20447232 | tf_op jit(solution)/shard_map/dot_general | solution.py:157
  290.7 6.9 %pad_maximum_fusion = bf16[512,7168]{1,0:T(8,128)(2,1)} fusion(bf16[512,3584]{1,0:T(8,128)(2,1)} %convolution_convert_fusion, bf16[512,3584]{1,0:T(8,128)(2,1)} %convolution_convert_fusion.1), kind=kLoop, calls=%fused_computation.5 | loop fusion | flops 14680064 | bytes 14680064 | tf_op jit(solution)/shard_map/concatenate | solution.py:160
  297.7 127.9 %reduce-scatter.9.cloned.1.call-done = bf16[128,7168]{1,0:T(8,128)(2,1)} async-done(((bf16[512,7168]{1,0:T(8,128)(2,1)}), bf16[128,7168]{1,0:T(8,128)(2,1)}) %reduce-scatter.9.cloned.1.call-update) | async-done | bytes 1835024 | tf_op jit(solution)/shard_map/reduce_scatter | solution.py:159
  425.5 1.9 convert_element_type.83
  428.9 72.7 %all-gather.10.cloned.1.call-done = bf16[512,3584]{1,0:T(8,128)(2,1)} async-done(((bf16[128,3584]{1,0:T(8,128)(2,1)}), bf16[512,3584]{1,0:T(8,128)(2,1)}) %all-gather.10.cloned.1.call-update) | async-done | bytes 3670032 | tf_op jit(solution)/shard_map/all_gather | solution.py:167
  501.6 13.0 %convolution_convert_fusion.2 = bf16[512,2048]{1,0:T(8,128)(2,1)} fusion(bf16[512,3584]{1,0:T(8,128)(2,1)} %all-gather.10.cloned.1.call-done, bf16[3584,2048]{1,0:T(8,128)(2,1)} %param.23), kind=kOutput, calls=%fused_computation.15 | convolution fusion | flops 7517241344 | bytes 20447232 | tf_op jit(solution)/shard_map/dot_general | solution.py:166
  515.1 39.4 %reduce-scatter.11.cloned.1.call-done = bf16[64,2048]{1,0:T(8,128)(2,1)} async-done(((bf16[512,2048]{1,0:T(8,128)(2,1)}), bf16[64,2048]{1,0:T(8,128)(2,1)}) %reduce-scatter.11.cloned.1.call-update) | async-done | bytes 262160 | tf_op jit(solution)/shard_map/reduce_scatter | solution.py:171
  554.5 1.6 scatter_custom_fusion.1
  557.0 3.5 all-to-all-start.3
  560.5 9.6 %all-to-all-done.3 = bf16[8,12,2048]{2,1,0:T(8,128)(2,1)S(1)} async-done(((bf16[8,12,2048]{2,1,0:T(8,128)(2,1)}), bf16[8,12,2048]{2,1,0:T(8,128)(2,1)S(1)}, u32[]{:S(2)}, u32[]{:S(2)}) %all-to-all-start.3) | async-done | bytes 393248 | tf_op jit(solution)/shard_map/all_to_all | solution.py:181
  570.2 3.3 gather_fusion.2
  573.5 4.4 add_convert_fusion
  (97 shorter events, 17.4 us)
Async XLA Ops:
  6.5 169.7 %copy-start = (bf16[1024,1024]{1,0:T(8,128)(2,1)S(1)}, bf16[1024,1024]{1,0:T(8,128)(2,1)}, u32[]{:S(2)}) copy-start(bf16[1024,1024]{1,0:T(8,128)(2,1)} %param.19) | copy-start | bytes 6291460
  12.0 9.4 %copy-start.12 = (s32[64]{0:T(128)S(1)}, s32[64]{0:T(128)}, u32[]{:S(2)}) copy-start(s32[64]{0:T(128)} %param.25) | copy-start | bytes 772
  15.1 17.5 %copy-start.5 = (bf16[8192]{0:T(1024)(128)(2,1)S(1)}, bf16[8192]{0:T(1024)(128)(2,1)}, u32[]{:S(2)}) copy-start(bf16[8192]{0:T(1024)(128)(2,1)} %param.14) | copy-start | bytes 49156
  16.1 14.9 %all-to-all-start = ((bf16[8,12,2048]{2,1,0:T(8,128)(2,1)}), bf16[8,12,2048]{2,1,0:T(8,128)(2,1)S(1)}, u32[]{:S(2)}, u32[]{:S(2)}) async-start(bf16[8,12,2048]{2,1,0:T(8,128)(2,1)} %broadcast_select_fusion), calls=%async_computation | async-start | bytes 1048576 | tf_op jit(solution)/shard_map/all_to_all | solution.py:76
  21.3 38.8 %all-gather.12.cloned.1.call-start = ((), (), s32[]{:S(2)}) async-start(), calls=%async_computation.15 | async-start | bytes 1310720 | tf_op jit(solution)/shard_map/all_gather | solution.py:89
  32.6 96.9 %reduce-scatter.5.cloned.1.call-start = ((), (), s32[]{:S(2)}) async-start(), calls=%async_computation.8 | async-start | bytes 3538944 | tf_op jit(solution)/shard_map/reduce_scatter | solution.py:100
  61.7 20.6 %copy-start.8 = (bf16[1024,1024]{1,0:T(8,128)(2,1)S(1)}, bf16[1024,1024]{1,0:T(8,128)(2,1)}, u32[]{:S(2)}) copy-start(bf16[1024,1024]{1,0:T(8,128)(2,1)} %param.16) | copy-start | bytes 6291460
  61.7 20.6 %copy-start.10 = (bf16[1024,256]{1,0:T(8,128)(2,1)S(1)}, bf16[1024,256]{1,0:T(8,128)(2,1)}, u32[]{:S(2)}) copy-start(bf16[1024,256]{1,0:T(8,128)(2,1)} %param.18) | copy-start | bytes 1572868
  61.7 20.6 %copy-start.11 = (bf16[1024,256]{1,0:T(8,128)(2,1)S(1)}, bf16[1024,256]{1,0:T(8,128)(2,1)}, u32[]{:S(2)}) copy-start(bf16[1024,256]{1,0:T(8,128)(2,1)} %param.17) | copy-start | bytes 1572868
  85.8 90.4 %all-gather.6.cloned.1.call-start = ((), (), s32[]{:S(2)}) async-start(), calls=%async_computation.9 | async-start | bytes 1179648 | tf_op jit(solution)/shard_map/all_gather | solution.py:140
  152.7 71.7 %reduce-scatter.7.cloned.1.call-start = ((), (), s32[]{:S(2)}) async-start(), calls=%async_computation.10 | async-start | bytes 1310720 | tf_op jit(solution)/shard_map/reduce_scatter | solution.py:145
  178.7 19.2 %copy-start.7 = (bf16[2048]{0:T(1024)(128)(2,1)S(1)}, bf16[2048]{0:T(1024)(128)(2,1)}, u32[]{:S(2)}) copy-start(bf16[2048]{0:T(1024)(128)(2,1)} %param.20) | copy-start | bytes 12292
  178.7 45.6 %copy-start.3 = (bf16[64,2048]{1,0:T(8,128)(2,1)S(1)}, bf16[64,2048]{1,0:T(8,128)(2,1)}, u32[]{:S(2)}) copy-start(bf16[64,2048]{1,0:T(8,128)(2,1)} %gather_fusion.1) | copy-start | bytes 786436
  197.8 65.4 %all-gather.8.cloned.1.call-start = ((), (), s32[]{:S(2)}) async-start(), calls=%async_computation.11 | async-start | bytes 2359296 | tf_op jit(solution)/shard_map/all_gather | solution.py:155
  236.6 189.0 %reduce-scatter.9.cloned.1.call-start = ((), (), s32[]{:S(2)}) async-start(), calls=%async_computation.12 | async-start | bytes 9175040 | tf_op jit(solution)/shard_map/reduce_scatter | solution.py:159
  263.2 15.1 %copy-start.9 = (bf16[512,2048]{1,0:T(8,128)(2,1)S(1)}, bf16[512,2048]{1,0:T(8,128)(2,1)}, u32[]{:S(2)}) copy-start(bf16[512,2048]{1,0:T(8,128)(2,1)} %all-gather.8.cloned.1.call-done) | copy-start | bytes 6291460
  297.6 204.0 %all-gather.10.cloned.1.call-start = ((), (), s32[]{:S(2)}) async-start(), calls=%async_computation.13 | async-start | bytes 4587520 | tf_op jit(solution)/shard_map/all_gather | solution.py:167
  428.8 85.8 %copy-start.6 = (bf16[8192]{0:T(1024)(128)(2,1)S(1)}, bf16[8192]{0:T(1024)(128)(2,1)}, u32[]{:S(2)}) copy-start(bf16[8192]{0:T(1024)(128)(2,1)} %param.15) | copy-start | bytes 49156
  428.9 85.8 %copy-start.2 = (bf16[64,8192]{1,0:T(8,128)(2,1)S(1)}, bf16[64,8192]{1,0:T(8,128)(2,1)}, u32[]{:S(2)}) copy-start(bf16[64,8192]{1,0:T(8,128)(2,1)} %all-gather.12.cloned.1.call-done) | copy-start | bytes 3145732
  428.9 125.6 %reduce-scatter.11.cloned.1.call-start = ((), (), s32[]{:S(2)}) async-start(), calls=%async_computation.14 | async-start | bytes 2359296 | tf_op jit(solution)/shard_map/reduce_scatter | solution.py:171
  514.6 39.9 %copy-start.4 = (bf16[64,2048]{1,0:T(8,128)(2,1)S(1)}, bf16[64,2048]{1,0:T(8,128)(2,1)}, u32[]{:S(2)}) copy-start(bf16[64,2048]{1,0:T(8,128)(2,1)} %reduce-scatter.7.cloned.1.call-done) | copy-start | bytes 786436
  557.0 13.2 %all-to-all-start.3 = ((bf16[8,12,2048]{2,1,0:T(8,128)(2,1)}), bf16[8,12,2048]{2,1,0:T(8,128)(2,1)S(1)}, u32[]{:S(2)}, u32[]{:S(2)}) async-start(bf16[8,12,2048]{2,1,0:T(8,128)(2,1)} %reshape.199), calls=%async_computation.7 | async-start | bytes 1048576 | tf_op jit(solution)/shard_map/all_to_all | solution.py:181
  573.5 4.4 copy-start.1
Sparse Core Ops, SparseCore 0:
  32.7 27.3 all-gather.11
  85.9 43.6 reduce-scatter.4
  152.8 23.3 all-gather.5
  197.9 26.3 reduce-scatter.6
  236.7 26.4 all-gather.7
  297.7 127.7 reduce-scatter.8
  429.0 72.5 all-gather.9
  514.8 39.6 reduce-scatter.10
where the time goes:
time: 586 us; the launch traced here: 585 us
  waiting for transfers between devices  406 us (69%)
  blocking collectives  63.6 us (11%)
  matrix products  47.6 us (8%)
  other arithmetic  27.4 us (5%)
  local copies, waits for them, and re-layouts  16.6 us (3%)
  between operations  13.9 us (2%)
  starting transfers between devices  9.2 us (2%)
    reduce_scatter x1, waiting for transfers between devices, body(): lax.psum_scatter(jnp.concatenate([gate_block, up_block], axis=1).astype(j...  128 us
    all_gather x1, waiting for transfers between devices, body(): lax.all_gather(hidden, 'mp', axis=0, tiled=True)  72.7 us
    reduce_scatter x1, waiting for transfers between devices, body(): lax.psum_scatter(jnp.dot(slices, stacked, preferred_element_type=jnp.floa...  43.4 us
    reduce_scatter x1, waiting for transfers between devices, body(): lax.psum_scatter(mlp_partial.astype(jnp.bfloat16), 'ctx', scatter_dimensi...  39.4 us
    all_gather x1, waiting for transfers between devices, body(): full_rows = lax.all_gather(local_rows, 'mp', axis=1, tiled=True)  27.4 us
    reduce_scatter x1, waiting for transfers between devices, body(): lax.psum_scatter(head_delta.astype(jnp.bfloat16), 'mp', scatter_dimension...  26.5 us
    all_gather x1, waiting for transfers between devices, body(): every_normed = lax.all_gather(second_normed, 'ctx', axis=0, tiled=True)  26.4 us
    all_gather x1, waiting for transfers between devices, body(): every_head = lax.all_gather(attended, 'ctx', axis=0, tiled=True)  23.5 us
  transfers between devices with their start and end apart: 10, of which 10 were waited for; matrix products, arithmetic and copies ran while one was open for 0% of the time, Pallas kernels for 0%

commit v1 on v0

v1 whole, which is shorter than its diff:
```python
import jax
import jax.numpy as jnp
from jax import lax
from jax.sharding import PartitionSpec as P


HEAD_DIM = 128
BF = jnp.bfloat16
F32 = jnp.float32
WIDTH = 256
GROUP = 4


def rotate(values, positions):
    half_dim = values.shape[-1] // 2
    exponent = jnp.arange(half_dim, dtype=F32) * (2.0 / values.shape[-1])
    frequency = 500000.0 ** (-exponent)
    angles = positions.astype(F32)[:, None] * frequency[None, :]
    cosine = jnp.cos(angles)
    sine_part = jnp.sin(angles)
    first_half = values[..., :half_dim]
    second_half = values[..., half_dim:]
    return jnp.concatenate(
        [
            first_half * cosine - second_half * sine_part,
            second_half * cosine + first_half * sine_part,
        ],
        axis=-1,
    )


def pick(array, index, axis):
    return lax.dynamic_index_in_dim(array, index, axis, keepdims=False)


class Grid:
    def __init__(self):
        self.C = lax.axis_size("ctx")
        self.M = lax.axis_size("mp")
        self.c = lax.axis_index("ctx")
        self.m = lax.axis_index("mp")
        self.H = self.C // self.M
        self.far_bits = []
        bit = 2
        while bit < self.C:
            self.far_bits.append(bit)
            bit *= 2

    def bit(self, b):
        return (self.c // b) % 2

    def swap(self, x, b):
        return lax.ppermute(x, "ctx", [(i, i ^ b) for i in range(self.C)])

    def flat(self, pairs):
        return [(a * self.M + b, d * self.M + e) for (a, b), (d, e) in pairs]

    def mp_sum(self, x):
        total = x
        for step in range(1, self.M):
            total = total + lax.ppermute(x, "mp", [(i, (i + step) % self.M) for i in range(self.M)])
        return total

    def far_gather(self, x, bits):
        have = []
        out = x[None]
        for b in bits:
            other = self.swap(out, b)
            zero = self.bit(b) == 0
            lo = jnp.where(zero, out, other)
            hi = jnp.where(zero, other, out)
            pos = sum(1 for g in have if g > b)
            lead = [2] * len(have)
            rest = x.shape
            lo = lo.reshape(*lead, *rest)
            hi = hi.reshape(*lead, *rest)
            out = jnp.stack([lo, hi], axis=pos)
            have.append(b)
            out = out.reshape(2 ** len(have), *rest)
        return out

    def gather(self, parts):
        a = self.far_gather(parts[0], self.far_bits)
        b = self.far_gather(parts[1], self.far_bits[::-1])
        near = jnp.concatenate([a, b], axis=-1)
        other = self.swap(near, 1)
        zero = self.bit(1) == 0
        lo = jnp.where(zero, near, other)
        hi = jnp.where(zero, other, near)
        out = jnp.stack([lo, hi], axis=1)
        return out.reshape(self.C, *near.shape[1:])

    def small_gather(self, x):
        out = self.far_gather(x, self.far_bits)
        other = self.swap(out, 1)
        zero = self.bit(1) == 0
        lo = jnp.where(zero, out, other)
        hi = jnp.where(zero, other, out)
        return jnp.stack([lo, hi], axis=1).reshape(self.C, *x.shape)

    def far_halve(self, x, bits):
        left = sorted(self.far_bits, reverse=True)
        rest = x.shape[1:]
        out = x
        for b in bits:
            pos = left.index(b)
            view = out.reshape(*([2] * len(left)), *rest)
            keep = pick(view, self.bit(b), pos)
            send = pick(view, 1 - self.bit(b), pos)
            left.remove(b)
            out = keep + self.swap(send.astype(BF), b).astype(F32)
        return out.reshape(rest)

    def near_halve(self, x):
        view = x.reshape(self.C // 2, 2, *x.shape[1:])
        keep = pick(view, self.bit(1), 1)
        send = pick(view, 1 - self.bit(1), 1)
        return keep + self.swap(send.astype(BF), 1).astype(F32)

    def scatter_sum(self, x):
        near = self.near_halve(x)
        half = x.shape[-1] // 2
        a = self.far_halve(near[..., :half], self.far_bits[::-1])
        b = self.far_halve(near[..., half:], self.far_bits)
        return jnp.concatenate([a, b], axis=-1)

    def rows_to_slices(self, local_rows):
        n = local_rows.shape[0]
        f = local_rows.shape[1] // self.H
        payload = [
            lax.dynamic_slice(local_rows, (0, ((self.c % self.H) ^ i) * f), (n, f))
            for i in range(self.H)
        ]
        q = self.c % self.H + self.H * self.m
        out = jnp.zeros((self.C * n, f), local_rows.dtype)
        for r in range(self.C):
            pairs = [
                ((a, b), (self.H * b + (a ^ r) % self.H, (a ^ r) // self.H))
                for a in range(self.C)
                for b in range(self.M)
            ]
            got = lax.ppermute(payload[r % self.H], ("ctx", "mp"), self.flat(pairs))
            out = lax.dynamic_update_slice(out, got, ((q ^ r) * n, 0))
        return out

    def slices_to_rows(self, partial):
        n = partial.shape[0] // self.C
        f = partial.shape[1]
        half = partial.astype(BF)
        q = self.c % self.H + self.H * self.m
        sums = [None] * self.H
        for r in range(self.C):
            pairs = [
                ((self.H * b + (a ^ r) % self.H, (a ^ r) // self.H), (a, b))
                for a in range(self.C)
                for b in range(self.M)
            ]
            block = lax.dynamic_slice(half, ((q ^ r) * n, 0), (n, f))
            got = lax.ppermute(block, ("ctx", "mp"), self.flat(pairs)).astype(F32)
            i = r % self.H
            sums[i] = got if sums[i] is None else sums[i] + got
        out = jnp.zeros((n, self.H * f), F32)
        for i in range(self.H):
            out = lax.dynamic_update_slice(out, sums[i], (0, ((self.c % self.H) ^ i) * f))
        return out


def head_reduce(grid, partial, rows, q_local, kv_local):
    heads = partial.reshape(rows, q_local + 2 * kv_local, HEAD_DIM).transpose(1, 0, 2)
    group_span = grid.C // kv_local
    queries = grid.near_halve(heads[:q_local])
    pair = heads[q_local:].reshape(2, kv_local, rows, HEAD_DIM)
    keep = pick(pair, grid.bit(1), 0)
    send = pick(pair, 1 - grid.bit(1), 0)
    stored = keep + grid.swap(send.astype(BF), 1).astype(F32)
    half = rows // 2
    halves = []
    for span, order in ((slice(0, half), grid.far_bits[::-1]), (slice(half, rows), grid.far_bits)):
        q = queries[:, span]
        kv = stored[:, span]
        left = sorted(grid.far_bits, reverse=True)
        left_kv = [b for b in left if b >= group_span]
        for b in order:
            view = q.reshape(*([2] * len(left)), half, HEAD_DIM)
            pos = left.index(b)
            q_keep = pick(view, grid.bit(b), pos)
            q_send = pick(view, 1 - grid.bit(b), pos).reshape(-1, half, HEAD_DIM)
            left.remove(b)
            if b >= group_span:
                kv_view = kv.reshape(*([2] * len(left_kv)), half, HEAD_DIM)
                kv_pos = left_kv.index(b)
                kv_keep = pick(kv_view, grid.bit(b), kv_pos).reshape(-1, half, HEAD_DIM)
                kv_send = pick(kv_view, 1 - grid.bit(b), kv_pos).reshape(-1, half, HEAD_DIM)
                left_kv.remove(b)
            else:
                kv_keep = kv
                kv_send = kv
            got = grid.swap(jnp.concatenate([q_send, kv_send], axis=0).astype(BF), b).astype(F32)
            count = q_send.shape[0]
            q = q_keep.reshape(-1, half, HEAD_DIM) + got[:count]
            kv = kv_keep + got[count:]
        halves.append((q.reshape(half, HEAD_DIM), kv.reshape(half, HEAD_DIM)))
    query = jnp.concatenate([halves[0][0], halves[1][0]], axis=0)
    own = jnp.concatenate([halves[0][1], halves[1][1]], axis=0)
    return query, own


def feed_forward(grid, normed, gate_weight, up_weight, down_weight):
    C, M = grid.C, grid.M
    rows = normed.shape[0]
    hidden_cols = gate_weight.shape[1]
    width = WIDTH if hidden_cols % WIDTH == 0 else HEAD_DIM
    count = hidden_cols // width
    streams = 2
    place = jnp.where(grid.c % 2 == 1, grid.m, M - 1 - grid.m)

    def at(a, p):
        return (a, p if a % 2 == 1 else M - 1 - p)

    inward = grid.flat([(at(a, p), at(a, p + 1)) for a in range(C) for p in range(M - 1)])
    outward = grid.flat([(at(a, p + 1), at(a, p)) for a in range(C) for p in range(M - 1)])

    def choose(options):
        return lax.select_n(place, *options)

    partial = {}

    def part(k):
        if k not in partial:
            lo, hi = k * width, (k + 1) * width
            g = jnp.dot(normed, gate_weight[:, lo:hi], preferred_element_type=F32)
            u = jnp.dot(normed, up_weight[:, lo:hi], preferred_element_type=F32)
            partial[k] = jnp.concatenate([g.astype(BF), u.astype(BF)], axis=1)
        return partial[k]

    lists = [list(range(s, count, streams)) for s in range(streams)]
    got = [None] * streams
    passed = [None] * streams
    hist = [[] for _ in range(streams)]
    hids = [[] for _ in range(streams)]
    waiting = []
    total = None
    zero = jnp.zeros((rows, 2 * width), BF)
    tick = normed[:8, :128].astype(F32) * 0.0
    last = max(len(ks) for ks in lists) + 2 * (M - 1) - 1
    for t in range(last + 1):
        for s in range(streams):
            ks = lists[s]
            n = len(ks)
            came = got[s]
            if t < n + M - 2:
                options = [part(ks[t - p]) if 0 <= t - p < n else zero for p in range(M - 1)]
                own = choose(options + [zero])
                send = own if came is None else (own.astype(F32) + came.astype(F32)).astype(BF)
                got[s] = lax.ppermute(send, ("ctx", "mp"), inward)
            i = t - (M - 1)
            if 0 <= i < n + M - 2:
                if i < n:
                    full = came.astype(F32) + part(ks[i]).astype(F32)
                    g, u = full[:, :width], full[:, width:]
                    hids[s].append((jax.nn.silu(g) * u).astype(BF))
                fresh = hids[s][i] if i < n else jnp.zeros((rows, width), BF)
                send = fresh if passed[s] is None else jnp.where(place == M - 1, fresh, passed[s])
                passed[s] = lax.ppermute(send, ("ctx", "mp"), outward)
                hist[s].append(passed[s])
            j = i - (M - 2) - 1
            if 0 <= j < n:
                waiting.append(
                    (ks[j], choose([hist[s][j + M - 2 - p] for p in range(M - 1)] + [hids[s][j]]))
                )
            tick = tick * 0.5
            tick = lax.optimization_barrier(tick)
            final = t == last and s == streams - 1
            if len(waiting) >= GROUP or (final and waiting):
                waiting.sort(key=lambda kv: kv[0])
                k0, k1 = waiting[0][0], waiting[-1][0] + 1
                assert k1 - k0 == len(waiting)
                block = lax.optimization_barrier(jnp.concatenate([b for _, b in waiting], axis=1))
                waiting.clear()
                piece = jnp.dot(
                    block, down_weight[k0 * width : k1 * width], preferred_element_type=F32
                )
                total = lax.optimization_barrier(piece if total is None else total + piece)
    return total, jnp.sum(tick)


def body(
    tokens,
    norm_gain,
    router_weight,
    query_weight,
    key_weight,
    value_weight,
    out_weight,
    mlp_gain,
    gate_weight,
    up_weight,
    down_weight,
    destination,
    kept_pos,
):
    grid = Grid()
    ctx_count, mp_count = grid.C, grid.M
    my_index = grid.c
    tok_dev = tokens.shape[0]
    kept_dev = kept_pos.shape[0]
    rows = kept_dev * ctx_count
    feature_cols = tokens.shape[1]
    feature_total = feature_cols * mp_count
    slice_cols = feature_total // ctx_count
    capacity = (3 * kept_dev // 2 + ctx_count - 1) // ctx_count
    slots_all = ctx_count * capacity
    head_dim = HEAD_DIM
    query_cols = query_weight.shape[1]
    key_cols = key_weight.shape[1]
    kv_local = key_cols // head_dim
    q_local = query_cols // head_dim
    group_size = q_local // kv_local
    peer_ids = jnp.arange(ctx_count, dtype=jnp.int32)
    is_kept = destination >= 0
    owner_ids = destination // kept_dev
    slot_ids = destination % kept_dev
    kept_order = slot_ids * ctx_count + owner_ids
    first_order = jnp.min(jnp.where(is_kept, kept_order, ctx_count * kept_dev))
    first_slots = (first_order - peer_ids + ctx_count - 1) // ctx_count
    owner_match = owner_ids[:, None] == peer_ids[None, :]
    send_index = (
        owner_ids * capacity
        + slot_ids
        - jnp.sum(jnp.where(owner_match, first_slots[None, :], 0), axis=1)
    )
    send_index = jnp.where(is_kept, send_index, slots_all)
    token_ids = jnp.arange(tok_dev, dtype=jnp.int32)
    picked = jnp.full((slots_all,), tok_dev, jnp.int32).at[send_index].set(token_ids, mode="drop")
    outgoing = jnp.take(tokens, picked, axis=0, mode="fill", fill_value=0).reshape(
        ctx_count, capacity, feature_cols
    )
    incoming = lax.all_to_all(outgoing, "ctx", split_axis=0, concat_axis=0, tiled=True).reshape(
        slots_all, feature_cols
    )
    slot_range = jnp.arange(kept_dev, dtype=jnp.int32)
    source_ids = kept_pos // tok_dev
    source_match = source_ids[:, None] == peer_ids[None, :]
    first_from = jnp.min(jnp.where(source_match, slot_range[:, None], kept_dev), axis=0)
    recv_index = (
        source_ids * capacity
        + slot_range
        - jnp.sum(jnp.where(source_match, first_from[None, :], 0), axis=1)
    )
    local_rows = incoming[recv_index]
    raw_share = local_rows.astype(F32)
    slices = grid.rows_to_slices(local_rows)
    my_router = lax.dynamic_slice(router_weight, (grid.m * feature_cols,), (feature_cols,))
    sums = grid.mp_sum(
        jnp.stack(
            [
                jnp.sum(raw_share * raw_share, axis=1),
                jnp.sum(raw_share * my_router.astype(F32)[None, :], axis=1),
            ]
        )
    )
    router_score = jax.nn.sigmoid(sums[1])
    inverse = lax.rsqrt(sums[0] / feature_total + 1e-05)
    shared = grid.small_gather(jnp.stack([inverse, kept_pos.astype(F32)]))
    inverse_all = shared[:, 0].reshape(rows)
    pos_all = shared[:, 1].reshape(rows)
    my_gain = lax.dynamic_slice(norm_gain, (my_index * slice_cols,), (slice_cols,))
    scaled = (slices.astype(F32) * my_gain.astype(F32)[None, :]).astype(BF)
    stacked = jnp.concatenate([query_weight, key_weight, value_weight], axis=1)
    projected = jnp.dot(scaled, stacked, preferred_element_type=F32)
    row_ids = jnp.arange(rows, dtype=jnp.int32)
    row_order = row_ids % kept_dev * ctx_count + row_ids // kept_dev
    softmax_scale = head_dim ** (-0.5)
    if q_local == ctx_count and kv_local <= ctx_count // 2:
        query, own = head_reduce(grid, projected, rows, q_local, kv_local)
        query = rotate(query * inverse_all[:, None], pos_all).astype(BF)
        own = own * inverse_all[:, None]
        own = jnp.where(grid.bit(1) == 0, rotate(own, pos_all), own).astype(BF)
        other = grid.swap(own, 1)
        keys = jnp.where(grid.bit(1) == 0, own, other)
        values = jnp.where(grid.bit(1) == 0, other, own)
        allowed = row_order[None, :] <= row_order[:, None]
        scores = (
            lax.dot_general(query, keys, (((1,), (1,)), ((), ())), preferred_element_type=F32)
            * softmax_scale
        )
        scores = jnp.where(allowed, scores, -1e30)
        peak = jnp.max(scores, axis=-1, keepdims=True)
        weights = jnp.where(allowed, jnp.exp(scores - peak), 0.0)
        weighted = jnp.dot(weights, values.astype(F32))
        attended = (weighted / jnp.sum(weights, axis=-1, keepdims=True)).astype(BF)
        half = rows // 2
        first = grid.far_gather(attended[:half], grid.far_bits)
        second = grid.far_gather(attended[half:], grid.far_bits[::-1])
        near = jnp.concatenate([first, second], axis=1)
        other = grid.swap(near, 1)
        zero = grid.bit(1) == 0
        pair = jnp.stack([jnp.where(zero, near, other), jnp.where(zero, other, near)], axis=1)
        every_head = pair.reshape(q_local, rows, head_dim).transpose(1, 0, 2).reshape(rows, query_cols)
    else:
        mine = lax.psum_scatter(projected, "ctx", scatter_dimension=0, tiled=True)
        mine = mine * inverse[:, None]
        by_head = mine.reshape(kept_dev, q_local + 2 * kv_local, head_dim).transpose(1, 0, 2)
        queries = rotate(by_head[:q_local], kept_pos).astype(BF)
        queries = queries.reshape(kv_local, group_size, kept_dev, head_dim)
        keys = rotate(by_head[q_local : q_local + kv_local], kept_pos).astype(BF)
        values = by_head[q_local + kv_local :].astype(BF)
        keys = lax.all_gather(keys, "ctx", axis=1, tiled=True)
        values = lax.all_gather(values, "ctx", axis=1, tiled=True)
        query_order = slot_range * ctx_count + my_index
        allowed = row_order[None, :] <= query_order[:, None]
        scores = (
            jnp.einsum("hgqd,hkd->hgqk", queries, keys, preferred_element_type=F32) * softmax_scale
        )
        scores = jnp.where(allowed, scores, -1e30)
        peak = jnp.max(scores, axis=-1, keepdims=True)
        weights = jnp.where(allowed, jnp.exp(scores - peak), 0.0)
        weighted = jnp.einsum("hgqk,hkd->hgqd", weights, values.astype(F32))
        attended = weighted / jnp.sum(weights, axis=-1, keepdims=True)
        attended = attended.transpose(2, 0, 1, 3).reshape(kept_dev, query_cols).astype(BF)
        every_head = lax.all_gather(attended, "ctx", axis=0, tiled=True)
    partial_cols = jnp.dot(every_head, out_weight, preferred_element_type=F32)
    head_share = grid.slices_to_rows(partial_cols)
    mixed_share = raw_share + head_share
    square_sum = grid.mp_sum(jnp.sum(mixed_share * mixed_share, axis=1).reshape(1, kept_dev))[0]
    second_normed = (
        mixed_share
        * lax.rsqrt(square_sum / feature_total + 1e-05)[:, None]
        * mlp_gain.astype(F32)
    ).astype(BF)
    mid = feature_cols // 2
    every_normed = grid.gather((second_normed[:, :mid], second_normed[:, mid:]))
    every_normed = every_normed.reshape(rows, feature_cols)
    mlp_partial, tick = feed_forward(grid, every_normed, gate_weight, up_weight, down_weight)
    mlp_share = grid.scatter_sum(mlp_partial.reshape(ctx_count, kept_dev, feature_cols))
    update = (router_score[:, None] * (head_share + mlp_share) + tick).astype(BF)
    returning = (
        jnp.zeros((slots_all, feature_cols), BF)
        .at[recv_index]
        .set(update)
        .reshape(ctx_count, capacity, feature_cols)
    )
    returned = lax.all_to_all(returning, "ctx", split_axis=0, concat_axis=0, tiled=True).reshape(
        slots_all, feature_cols
    )
    arriving = jnp.take(returned, send_index, axis=0, mode="fill", fill_value=0)
    return (tokens.astype(F32) + arriving.astype(F32)).astype(BF)


def solution(mesh):
    in_specs = (
        P("ctx", "mp"),
        P(),
        P(),
        P("ctx", "mp"),
        P("ctx", "mp"),
        P("ctx", "mp"),
        P("mp", "ctx"),
        P("mp"),
        P("mp", "ctx"),
        P("mp", "ctx"),
        P("ctx", "mp"),
        P("ctx"),
        P("ctx"),
    )
    out_specs = P("ctx", "mp")
    return jax.shard_map(body, mesh=mesh, in_specs=in_specs, out_specs=out_specs, check_vma=False)
```

time: 586 us -> 502 us (0.86)
  waiting for transfers between devices: 406 us -> 224 us
  starting transfers between devices: 9.2 us -> 162 us
  blocking collectives: 63.6 us -> 0 us
  between operations: 13.9 us -> 2.69 us
  local copies, waits for them, and re-layouts: 16.6 us -> 27.7 us
  other arithmetic: 27.4 us -> 35.6 us
    reduce_scatter x4 -> x0, waiting for transfers between devices: 237 us -> none  [the longest x1 128 us: body(): lax.psum_scatter(jnp.concatenate([gate_block, up_block], axis=1).astype(j...]
    ppermute x0 -> x83, waiting for transfers between devices: none -> 207 us  [the longest x18 87.3 us: feed_forward(): got[s] = lax.ppermute(send, ('ctx', 'mp'), inward)]
    ppermute x0 -> x83, starting transfers between devices: none -> 153 us  [the longest x18 41.6 us: feed_forward(): passed[s] = lax.ppermute(send, ('ctx', 'mp'), outward)]
    all_gather x4 -> x0, waiting for transfers between devices: 150 us -> none  [the longest x1 72.7 us: body(): lax.all_gather(hidden, 'mp', axis=0, tiled=True)]
    all_to_all x2 -> x0, blocking collectives: 36.8 us -> none  [the longest x1 18.8 us: body(): lax.all_to_all(normed, 'ctx', split_axis=1, concat_axis=0, tiled=True)]
    all_gather x2 -> x0, blocking collectives: 17.6 us -> none  [the longest x1 9.25 us: body(): key_piece = lax.all_gather(key_rows, 'ctx', axis=0, tiled=True)]
    psum x1 -> x0, blocking collectives: 9.26 us -> none  [body(): square_sum = lax.psum(jnp.sum(mixed_share * mixed_share, axis=1), 'mp')]
    dynamic_slice x0 -> x8, local copies, waits for them, and re-layouts: none -> 7.18 us  [the longest x6 7.05 us: pick(): return lax.dynamic_index_in_dim(array, index, axis, keepdims=False)]
  transfers between devices with their start and end apart: 10 -> 85, of which waited for: 10 -> 53; matrix products, arithmetic and copies ran while one was open for 0% -> 6% of each run, Pallas kernels for 0% -> 0%
where the time goes in v1:
time: 502 us; the launch traced here: 497 us
  waiting for transfers between devices  224 us (45%)
  starting transfers between devices  162 us (32%)
  matrix products  45.1 us (9%)
  other arithmetic  35.6 us (7%)
  local copies, waits for them, and re-layouts  27.7 us (6%)
    ppermute x18, waiting for transfers between devices, feed_forward(): got[s] = lax.ppermute(send, ('ctx', 'mp'), inward)  87.3 us
    ppermute x25, waiting for transfers between devices, swap(): return lax.ppermute(x, 'ctx', [(i, i ^ b) for i in range(self.C)])  52.9 us
    ppermute x8, waiting for transfers between devices, slices_to_rows(): got = lax.ppermute(block, ('ctx', 'mp'), self.flat(pairs)).astype(F32)  44.3 us
    ppermute x18, starting transfers between devices, feed_forward(): passed[s] = lax.ppermute(send, ('ctx', 'mp'), outward)  41.6 us
    ppermute x8, starting transfers between devices, rows_to_slices(): got = lax.ppermute(payload[r % self.H], ('ctx', 'mp'), self.flat(pairs))  30 us
    ppermute x25, starting transfers between devices, swap(): return lax.ppermute(x, 'ctx', [(i, i ^ b) for i in range(self.C)])  25.3 us
    ppermute x8, starting transfers between devices, slices_to_rows(): got = lax.ppermute(block, ('ctx', 'mp'), self.flat(pairs)).astype(F32)  25 us
    ppermute x18, starting transfers between devices, feed_forward(): got[s] = lax.ppermute(send, ('ctx', 'mp'), inward)  23.3 us
  transfers between devices with their start and end apart: 85, of which 53 were waited for; matrix products, arithmetic and copies ran while one was open for 6% of the time, Pallas kernels for 0%

profile of v1, /device:TPU:0, one launch (start us, length us, event | category | flops | bytes accessed | tf_op | source)
XLA Modules:
  0.0 496.5 jit_solution(12932442127777388120)
XLA Ops:
  10.1 5.2 %all-to-all-start = ((bf16[8,12,2048]{2,1,0:T(8,128)(2,1)}), bf16[8,12,2048]{2,1,0:T(8,128)(2,1)S(1)}, u32[]{:S(2)}, u32[]{:S(2)}) async-start(bf16[8,12,2048]{2,1,0:T(8,128)(2,1)} %broadcast_select_fusion), calls=%async_computation | async-start | bytes 1048576 | tf_op jit(solution)/shard_map/all_to_all | solution.py:338
  17.5 7.5 %all-to-all-done = bf16[8,12,2048]{2,1,0:T(8,128)(2,1)S(1)} async-done(((bf16[8,12,2048]{2,1,0:T(8,128)(2,1)}), bf16[8,12,2048]{2,1,0:T(8,128)(2,1)S(1)}, u32[]{:S(2)}, u32[]{:S(2)}) %all-to-all-start) | async-done | bytes 393248 | tf_op jit(solution)/shard_map/all_to_all | solution.py:338
  44.0 12.2 %collective-permute-start.5 = (bf16[64,1024]{1,0:T(8,128)(2,1)S(1)}, bf16[64,1024]{1,0:T(8,128)(2,1)S(1)}, u32[]{:S(2)}, u32[]{:S(2)}) collective-permute-start(bf16[64,1024]{1,0:T(8,128)(2,1)S(1)} %get-tuple-element.117), channel_id=1, source_target_pairs={{0,1},{1,9},{2,17},{3,25},{4,5},{5,13},{6,21},{7,29},{8,0},{9,8},{... | collective-permute-start | bytes 393224 | tf_op jit(solution)/shard_map/ppermute | solution.py:142
  56.5 8.7 %collective-permute-start.9 = (bf16[64,1024]{1,0:T(8,128)(2,1)S(1)}, bf16[64,1024]{1,0:T(8,128)(2,1)S(1)}, u32[]{:S(2)}, u32[]{:S(2)}) collective-permute-start(bf16[64,1024]{1,0:T(8,128)(2,1)S(1)} %get-tuple-element.117), channel_id=1, source_target_pairs={{0,3},{1,11},{2,19},{3,27},{4,7},{5,15},{6,23},{7,31},{8,2},{9,10}... | collective-permute-start | bytes 393224 | tf_op jit(solution)/shard_map/ppermute | solution.py:142
  65.2 5.7 %collective-permute-start.7 = (bf16[64,1024]{1,0:T(8,128)(2,1)S(1)}, bf16[64,1024]{1,0:T(8,128)(2,1)S(1)}, u32[]{:S(2)}, u32[]{:S(2)}) collective-permute-start(bf16[64,1024]{1,0:T(8,128)(2,1)S(1)} %get-tuple-element.117), channel_id=1, source_target_pairs={{0,2},{1,10},{2,18},{3,26},{4,6},{5,14},{6,22},{7,30},{8,3},{9,11}... | collective-permute-start | bytes 393224 | tf_op jit(solution)/shard_map/ppermute | solution.py:142
  71.0 5.9 %collective-permute-done.7 = bf16[64,1024]{1,0:T(8,128)(2,1)S(1)} collective-permute-done((bf16[64,1024]{1,0:T(8,128)(2,1)S(1)}, bf16[64,1024]{1,0:T(8,128)(2,1)S(1)}, u32[]{:S(2)}, u32[]{:S(2)}) %collective-permute-start.7) | collective-permute-done | bytes 131104 | tf_op jit(solution)/shard_map/ppermute | solution.py:142
  95.7 6.9 %collective-permute-start.15 = (bf16[4,256,128]{2,1,0:T(8,128)(2,1)S(1)}, bf16[4,256,128]{2,1,0:T(8,128)(2,1)S(1)}, u32[]{:S(2)}, u32[]{:S(2)}) collective-permute-start(bf16[4,256,128]{2,1,0:T(8,128)(2,1)S(1)} %pad_maximum_fusion.24), channel_id=1, source_target_pairs={{0,8},{4,12},{8,0},{12,4},{16,24},{20,28},{24,16},{28,20},{1,9},{5... | collective-permute-start | bytes 786440 | tf_op jit(solution)/shard_map/ppermute | solution.py:53
  102.7 6.4 %collective-permute-done.15 = bf16[4,256,128]{2,1,0:T(8,128)(2,1)S(1)} collective-permute-done((bf16[4,256,128]{2,1,0:T(8,128)(2,1)S(1)}, bf16[4,256,128]{2,1,0:T(8,128)(2,1)S(1)}, u32[]{:S(2)}, u32[]{:S(2)}) %collective-permute-start.15) | collective-permute-done | bytes 262176 | tf_op jit(solution)/shard_map/ppermute | solution.py:53
  151.0 5.6 %collective-permute-done.29 = bf16[64,1024]{1,0:T(8,128)(2,1)S(1)} collective-permute-done((bf16[64,1024]{1,0:T(8,128)(2,1)S(1)}, bf16[64,1024]{1,0:T(8,128)(2,1)S(1)}, u32[]{:S(2)}, u32[]{:S(2)}) %collective-permute-start.29) | collective-permute-done | bytes 131104 | tf_op jit(solution)/shard_map/ppermute | solution.py:159
  156.6 4.4 collective-permute-start.33
  161.1 14.5 %collective-permute-done.28 = bf16[64,1024]{1,0:T(8,128)(2,1)S(1)} collective-permute-done((bf16[64,1024]{1,0:T(8,128)(2,1)S(1)}, bf16[64,1024]{1,0:T(8,128)(2,1)S(1)}, u32[]{:S(2)}, u32[]{:S(2)}) %collective-permute-start.28) | collective-permute-done | bytes 131104 | tf_op jit(solution)/shard_map/ppermute | solution.py:159
  175.5 17.8 %collective-permute-start.32 = (bf16[64,1024]{1,0:T(8,128)(2,1)S(1)}, bf16[64,1024]{1,0:T(8,128)(2,1)S(1)}, u32[]{:S(2)}, u32[]{:S(2)}) collective-permute-start(bf16[64,1024]{1,0:T(8,128)(2,1)S(1)} %get-tuple-element.41), channel_id=1, source_target_pairs={{6,0},{14,1},{22,2},{30,3},{2,4},{10,5},{18,6},{26,7},{7,8},{15,9}... | collective-permute-start | bytes 393224 | tf_op jit(solution)/shard_map/ppermute | solution.py:159
  196.9 20.7 %collective-permute-done.31 = bf16[64,1024]{1,0:T(8,128)(2,1)S(1)} collective-permute-done((bf16[64,1024]{1,0:T(8,128)(2,1)S(1)}, bf16[64,1024]{1,0:T(8,128)(2,1)S(1)}, u32[]{:S(2)}, u32[]{:S(2)}) %collective-permute-start.31) | collective-permute-done | bytes 131104 | tf_op jit(solution)/shard_map/ppermute | solution.py:159
  278.9 7.6 %collective-permute-done.50 = bf16[512,512]{0,1:T(8,128)(2,1)S(1)} collective-permute-done((bf16[512,512]{0,1:T(8,128)(2,1)S(1)}, bf16[512,512]{0,1:T(8,128)(2,1)S(1)}, u32[]{:S(2)}, u32[]{:S(2)}) %collective-permute-start.50) | collective-permute-done | bytes 524320 | tf_op jit(solution)/shard_map/ppermute | solution.py:255
  311.0 4.8 collective-permute-start.55
  319.6 6.7 %collective-permute-done.53 = bf16[512,512]{0,1:T(8,128)(2,1)S(1)} collective-permute-done((bf16[512,512]{0,1:T(8,128)(2,1)S(1)}, bf16[512,512]{0,1:T(8,128)(2,1)S(1)}, u32[]{:S(2)}, u32[]{:S(2)}) %collective-permute-start.53) | collective-permute-done | bytes 524320 | tf_op jit(solution)/shard_map/ppermute | solution.py:255
  329.6 5.5 %collective-permute-done.45 = bf16[512,512]{0,1:T(8,128)(2,1)S(1)} collective-permute-done((bf16[512,512]{0,1:T(8,128)(2,1)S(1)}, bf16[512,512]{0,1:T(8,128)(2,1)S(1)}, u32[]{:S(2)}, u32[]{:S(2)}) %collective-permute-start.45) | collective-permute-done | bytes 524320 | tf_op jit(solution)/shard_map/ppermute | solution.py:255
  338.4 5.1 %collective-permute-done.54 = bf16[512,512]{0,1:T(8,128)(2,1)S(1)} collective-permute-done((bf16[512,512]{0,1:T(8,128)(2,1)S(1)}, bf16[512,512]{0,1:T(8,128)(2,1)S(1)}, u32[]{:S(2)}, u32[]{:S(2)}) %collective-permute-start.54) | collective-permute-done | bytes 524320 | tf_op jit(solution)/shard_map/ppermute | solution.py:255
  346.9 5.1 %collective-permute-done.46 = bf16[512,512]{0,1:T(8,128)(2,1)S(1)} collective-permute-done((bf16[512,512]{0,1:T(8,128)(2,1)S(1)}, bf16[512,512]{0,1:T(8,128)(2,1)S(1)}, u32[]{:S(2)}, u32[]{:S(2)}) %collective-permute-start.46) | collective-permute-done | bytes 524320 | tf_op jit(solution)/shard_map/ppermute | solution.py:255
  355.3 5.1 %collective-permute-done.60 = bf16[512,512]{0,1:T(8,128)(2,1)S(1)} collective-permute-done((bf16[512,512]{0,1:T(8,128)(2,1)S(1)}, bf16[512,512]{0,1:T(8,128)(2,1)S(1)}, u32[]{:S(2)}, u32[]{:S(2)}) %collective-permute-start.60) | collective-permute-done | bytes 524320 | tf_op jit(solution)/shard_map/ppermute | solution.py:255
  363.7 5.1 %collective-permute-done.58 = bf16[512,512]{0,1:T(8,128)(2,1)S(1)} collective-permute-done((bf16[512,512]{0,1:T(8,128)(2,1)S(1)}, bf16[512,512]{0,1:T(8,128)(2,1)S(1)}, u32[]{:S(2)}, u32[]{:S(2)}) %collective-permute-start.58) | collective-permute-done | bytes 524320 | tf_op jit(solution)/shard_map/ppermute | solution.py:255
  372.1 5.1 %collective-permute-done.64 = bf16[512,512]{0,1:T(8,128)(2,1)S(1)} collective-permute-done((bf16[512,512]{0,1:T(8,128)(2,1)S(1)}, bf16[512,512]{0,1:T(8,128)(2,1)S(1)}, u32[]{:S(2)}, u32[]{:S(2)}) %collective-permute-start.64) | collective-permute-done | bytes 524320 | tf_op jit(solution)/shard_map/ppermute | solution.py:255
  380.6 5.1 %collective-permute-done.62 = bf16[512,512]{0,1:T(8,128)(2,1)S(1)} collective-permute-done((bf16[512,512]{0,1:T(8,128)(2,1)S(1)}, bf16[512,512]{0,1:T(8,128)(2,1)S(1)}, u32[]{:S(2)}, u32[]{:S(2)}) %collective-permute-start.62) | collective-permute-done | bytes 524320 | tf_op jit(solution)/shard_map/ppermute | solution.py:255
  389.0 5.2 %collective-permute-done.68 = bf16[512,512]{0,1:T(8,128)(2,1)S(1)} collective-permute-done((bf16[512,512]{0,1:T(8,128)(2,1)S(1)}, bf16[512,512]{0,1:T(8,128)(2,1)S(1)}, u32[]{:S(2)}, u32[]{:S(2)}) %collective-permute-start.68) | collective-permute-done | bytes 524320 | tf_op jit(solution)/shard_map/ppermute | solution.py:255
  397.4 4.4 collective-permute-done.66
  403.6 4.8 collective-permute-start.67
  412.0 9.4 %collective-permute-done.70 = bf16[512,512]{0,1:T(8,128)(2,1)S(1)} collective-permute-done((bf16[512,512]{0,1:T(8,128)(2,1)S(1)}, bf16[512,512]{0,1:T(8,128)(2,1)S(1)}, u32[]{:S(2)}, u32[]{:S(2)}) %collective-permute-start.70) | collective-permute-done | bytes 524320 | tf_op jit(solution)/shard_map/ppermute | solution.py:255
  427.4 4.4 collective-permute-start.74
  435.7 4.7 collective-permute-start.76
  460.8 5.0 %collective-permute-done.79 = bf16[2,64,1024]{2,1,0:T(8,128)(2,1)S(1)} collective-permute-done((bf16[2,64,1024]{2,1,0:T(8,128)(2,1)S(1)}, bf16[2,64,1024]{2,1,0:T(8,128)(2,1)S(1)}, u32[]{:S(2)}, u32[]{:S(2)}) %collective-permute-start.79) | collective-permute-done | bytes 262176 | tf_op jit(solution)/shard_map/ppermute | solution.py:53
  478.7 9.6 %all-to-all-done.1 = bf16[8,12,2048]{2,1,0:T(8,128)(2,1)S(1)} async-done(((bf16[8,12,2048]{2,1,0:T(8,128)(2,1)}), bf16[8,12,2048]{2,1,0:T(8,128)(2,1)S(1)}, u32[]{:S(2)}, u32[]{:S(2)}) %all-to-all-start.1) | async-done | bytes 393248 | tf_op jit(solution)/shard_map/all_to_all | solution.py:443
  491.7 4.4 add_convert_fusion
  (442 shorter events, 265.2 us)
Async XLA Ops:
  10.1 14.9 %all-to-all-start = ((bf16[8,12,2048]{2,1,0:T(8,128)(2,1)}), bf16[8,12,2048]{2,1,0:T(8,128)(2,1)S(1)}, u32[]{:S(2)}, u32[]{:S(2)}) async-start(bf16[8,12,2048]{2,1,0:T(8,128)(2,1)} %broadcast_select_fusion), calls=%async_computation | async-start | bytes 1048576 | tf_op jit(solution)/shard_map/all_to_all | solution.py:338
  40.3 36.7 %collective-permute-start.10 = (bf16[64,1024]{1,0:T(8,128)(2,1)S(1)}, bf16[64,1024]{1,0:T(8,128)(2,1)S(1)}, u32[]{:S(2)}, u32[]{:S(2)}) collective-permute-start(bf16[64,1024]{1,0:T(8,128)(2,1)S(1)} %get-tuple-element.116), channel_id=1, source_target_pairs={{0,7},{1,15},{2,23},{3,31},{4,3},{5,11},{6,19},{7,27},{8,6},{9,14}... | collective-permute-start | bytes 393224 | tf_op jit(solution)/shard_map/ppermute | solution.py:142
  40.4 36.5 %collective-permute-start.8 = (bf16[64,1024]{1,0:T(8,128)(2,1)S(1)}, bf16[64,1024]{1,0:T(8,128)(2,1)S(1)}, u32[]{:S(2)}, u32[]{:S(2)}) collective-permute-start(bf16[64,1024]{1,0:T(8,128)(2,1)S(1)} %get-tuple-element.116), channel_id=1, source_target_pairs={{0,6},{1,14},{2,22},{3,30},{4,2},{5,10},{6,18},{7,26},{8,7},{9,15}... | collective-permute-start | bytes 393224 | tf_op jit(solution)/shard_map/ppermute | solution.py:142
  41.6 29.3 %collective-permute-start.6 = (bf16[64,1024]{1,0:T(8,128)(2,1)S(1)}, bf16[64,1024]{1,0:T(8,128)(2,1)S(1)}, u32[]{:S(2)}, u32[]{:S(2)}) collective-permute-start(bf16[64,1024]{1,0:T(8,128)(2,1)S(1)} %get-tuple-element.116), channel_id=1, source_target_pairs={{0,5},{1,13},{2,21},{3,29},{4,1},{5,9},{6,17},{7,25},{8,4},{9,12},... | collective-permute-start | bytes 393224 | tf_op jit(solution)/shard_map/ppermute | solution.py:142
  44.0 21.1 %collective-permute-start.5 = (bf16[64,1024]{1,0:T(8,128)(2,1)S(1)}, bf16[64,1024]{1,0:T(8,128)(2,1)S(1)}, u32[]{:S(2)}, u32[]{:S(2)}) collective-permute-start(bf16[64,1024]{1,0:T(8,128)(2,1)S(1)} %get-tuple-element.117), channel_id=1, source_target_pairs={{0,1},{1,9},{2,17},{3,25},{4,5},{5,13},{6,21},{7,29},{8,0},{9,8},{... | collective-permute-start | bytes 393224 | tf_op jit(solution)/shard_map/ppermute | solution.py:142
  56.5 20.5 %collective-permute-start.9 = (bf16[64,1024]{1,0:T(8,128)(2,1)S(1)}, bf16[64,1024]{1,0:T(8,128)(2,1)S(1)}, u32[]{:S(2)}, u32[]{:S(2)}) collective-permute-start(bf16[64,1024]{1,0:T(8,128)(2,1)S(1)} %get-tuple-element.117), channel_id=1, source_target_pairs={{0,3},{1,11},{2,19},{3,27},{4,7},{5,15},{6,23},{7,31},{8,2},{9,10}... | collective-permute-start | bytes 393224 | tf_op jit(solution)/shard_map/ppermute | solution.py:142
  70.9 31.8 %collective-permute-start.19 = (f32[4,2,64]{2,0,1:T(4,128)S(1)}, f32[4,2,64]{2,0,1:T(4,128)S(1)}, u32[]{:S(2)}, u32[]{:S(2)}) collective-permute-start(f32[4,2,64]{2,0,1:T(4,128)S(1)} %copy.42), channel_id=1, source_target_pairs={{0,4},{4,0},{8,12},{12,8},{16,20},{20,16},{24,28},{28,24},{1,5},{5... | collective-permute-start | bytes 6152 | tf_op jit(solution)/shard_map/ppermute | solution.py:53
  149.6 26.0 %collective-permute-start.28 = (bf16[64,1024]{1,0:T(8,128)(2,1)S(1)}, bf16[64,1024]{1,0:T(8,128)(2,1)S(1)}, u32[]{:S(2)}, u32[]{:S(2)}) collective-permute-start(bf16[64,1024]{1,0:T(8,128)(2,1)S(1)} %get-tuple-element.44), channel_id=1, source_target_pairs={{2,0},{10,1},{18,2},{26,3},{6,4},{14,5},{22,6},{30,7},{3,8},{11,9}... | collective-permute-start | bytes 393224 | tf_op jit(solution)/shard_map/ppermute | solution.py:159
  149.8 47.0 %collective-permute-start.27 = (bf16[64,1024]{1,0:T(8,128)(2,1)S(1)}, bf16[64,1024]{1,0:T(8,128)(2,1)S(1)}, u32[]{:S(2)}, u32[]{:S(2)}) collective-permute-start(bf16[64,1024]{1,0:T(8,128)(2,1)S(1)} %get-tuple-element.45), channel_id=1, source_target_pairs={{1,0},{9,1},{17,2},{25,3},{5,4},{13,5},{21,6},{29,7},{0,8},{8,9},{... | collective-permute-start | bytes 393224 | tf_op jit(solution)/shard_map/ppermute | solution.py:159
  150.2 46.6 %collective-permute-start.26 = (bf16[64,1024]{1,0:T(8,128)(2,1)S(1)}, bf16[64,1024]{1,0:T(8,128)(2,1)S(1)}, u32[]{:S(2)}, u32[]{:S(2)}) collective-permute-start(bf16[64,1024]{1,0:T(8,128)(2,1)S(1)} %get-tuple-element.46), channel_id=1, source_target_pairs={{0,0},{8,1},{16,2},{24,3},{4,4},{12,5},{20,6},{28,7},{1,8},{9,9},{... | collective-permute-start | bytes 393224 | tf_op jit(solution)/shard_map/ppermute | solution.py:159
  150.9 46.0 %collective-permute-start.30 = (bf16[64,1024]{1,0:T(8,128)(2,1)S(1)}, bf16[64,1024]{1,0:T(8,128)(2,1)S(1)}, u32[]{:S(2)}, u32[]{:S(2)}) collective-permute-start(bf16[64,1024]{1,0:T(8,128)(2,1)S(1)} %get-tuple-element.39), channel_id=1, source_target_pairs={{4,0},{12,1},{20,2},{28,3},{0,4},{8,5},{16,6},{24,7},{5,8},{13,9},... | collective-permute-start | bytes 393224 | tf_op jit(solution)/shard_map/ppermute | solution.py:159
  156.6 40.3 %collective-permute-start.33 = (bf16[64,1024]{1,0:T(8,128)(2,1)S(1)}, bf16[64,1024]{1,0:T(8,128)(2,1)S(1)}, u32[]{:S(2)}, u32[]{:S(2)}) collective-permute-start(bf16[64,1024]{1,0:T(8,128)(2,1)S(1)} %get-tuple-element.40), channel_id=1, source_target_pairs={{7,0},{15,1},{23,2},{31,3},{3,4},{11,5},{19,6},{27,7},{6,8},{14,9}... | collective-permute-start | bytes 393224 | tf_op jit(solution)/shard_map/ppermute | solution.py:159
  175.5 21.4 %collective-permute-start.32 = (bf16[64,1024]{1,0:T(8,128)(2,1)S(1)}, bf16[64,1024]{1,0:T(8,128)(2,1)S(1)}, u32[]{:S(2)}, u32[]{:S(2)}) collective-permute-start(bf16[64,1024]{1,0:T(8,128)(2,1)S(1)} %get-tuple-element.41), channel_id=1, source_target_pairs={{6,0},{14,1},{22,2},{30,3},{2,4},{10,5},{18,6},{26,7},{7,8},{15,9}... | collective-permute-start | bytes 393224 | tf_op jit(solution)/shard_map/ppermute | solution.py:159
  196.8 20.9 %collective-permute-start.31 = (bf16[64,1024]{1,0:T(8,128)(2,1)S(1)}, bf16[64,1024]{1,0:T(8,128)(2,1)S(1)}, u32[]{:S(2)}, u32[]{:S(2)}) collective-permute-start(bf16[64,1024]{1,0:T(8,128)(2,1)S(1)} %get-tuple-element.42), channel_id=1, source_target_pairs={{5,0},{13,1},{21,2},{29,3},{1,4},{9,5},{17,6},{25,7},{4,8},{12,9},... | collective-permute-start | bytes 393224 | tf_op jit(solution)/shard_map/ppermute | solution.py:159
  276.8 15.3 %collective-permute-start.42 = (bf16[512,512]{0,1:T(8,128)(2,1)S(1)}, bf16[512,512]{0,1:T(8,128)(2,1)S(1)}, u32[]{:S(2)}, u32[]{:S(2)}) collective-permute-start(bf16[512,512]{0,1:T(8,128)(2,1)S(1)} %select_select_fusion.1), channel_id=1, source_target_pairs={{3,2},{2,1},{1,0},{4,5},{5,6},{6,7},{11,10},{10,9},{9,8},{12,13},{... | collective-permute-start | bytes 1572872 | tf_op jit(solution)/shard_map/ppermute | solution.py:255
  309.5 16.7 %collective-permute-start.53 = (bf16[512,512]{0,1:T(8,128)(2,1)S(1)}, bf16[512,512]{0,1:T(8,128)(2,1)S(1)}, u32[]{:S(2)}, u32[]{:S(2)}) collective-permute-start(bf16[512,512]{0,1:T(8,128)(2,1)S(1)} %get-tuple-element.87), channel_id=1, source_target_pairs={{3,2},{2,1},{1,0},{4,5},{5,6},{6,7},{11,10},{10,9},{9,8},{12,13},{... | collective-permute-start | bytes 1572872 | tf_op jit(solution)/shard_map/ppermute | solution.py:255
  311.0 15.6 %collective-permute-start.55 = (bf16[512,256]{0,1:T(8,128)(2,1)S(1)}, bf16[512,256]{0,1:T(8,128)(2,1)S(1)}, u32[]{:S(2)}, u32[]{:S(2)}) collective-permute-start(bf16[512,256]{0,1:T(8,128)(2,1)S(1)} %fusion.74), channel_id=1, source_target_pairs={{2,3},{1,2},{0,1},{5,4},{6,5},{7,6},{10,11},{9,10},{8,9},{13,12},{... | collective-permute-start | bytes 786440 | tf_op jit(solution)/shard_map/ppermute | solution.py:264
  316.3 19.1 %collective-permute-start.47 = (bf16[512,256]{0,1:T(8,128)(2,1)S(1)}, bf16[512,256]{0,1:T(8,128)(2,1)S(1)}, u32[]{:S(2)}, u32[]{:S(2)}) collective-permute-start(bf16[512,256]{0,1:T(8,128)(2,1)S(1)} %fusion.77), channel_id=1, source_target_pairs={{2,3},{1,2},{0,1},{5,4},{6,5},{7,6},{10,11},{9,10},{8,9},{13,12},{... | collective-permute-start | bytes 786440 | tf_op jit(solution)/shard_map/ppermute | solution.py:264
  318.3 16.8 %collective-permute-start.45 = (bf16[512,512]{0,1:T(8,128)(2,1)S(1)}, bf16[512,512]{0,1:T(8,128)(2,1)S(1)}, u32[]{:S(2)}, u32[]{:S(2)}) collective-permute-start(bf16[512,512]{0,1:T(8,128)(2,1)S(1)} %get-tuple-element.81), channel_id=1, source_target_pairs={{3,2},{2,1},{1,0},{4,5},{5,6},{6,7},{11,10},{10,9},{9,8},{12,13},{... | collective-permute-start | bytes 1572872 | tf_op jit(solution)/shard_map/ppermute | solution.py:255
  326.8 17.1 %collective-permute-start.56 = (bf16[512,256]{0,1:T(8,128)(2,1)S(1)}, bf16[512,256]{0,1:T(8,128)(2,1)S(1)}, u32[]{:S(2)}, u32[]{:S(2)}) collective-permute-start(bf16[512,256]{0,1:T(8,128)(2,1)S(1)} %get-tuple-element.31), channel_id=1, source_target_pairs={{2,3},{1,2},{0,1},{5,4},{6,5},{7,6},{10,11},{9,10},{8,9},{13,12},{... | collective-permute-start | bytes 786440 | tf_op jit(solution)/shard_map/ppermute | solution.py:264
  328.3 15.3 %collective-permute-start.54 = (bf16[512,512]{0,1:T(8,128)(2,1)S(1)}, bf16[512,512]{0,1:T(8,128)(2,1)S(1)}, u32[]{:S(2)}, u32[]{:S(2)}) collective-permute-start(bf16[512,512]{0,1:T(8,128)(2,1)S(1)} %get-tuple-element.85), channel_id=1, source_target_pairs={{3,2},{2,1},{1,0},{4,5},{5,6},{6,7},{11,10},{10,9},{9,8},{12,13},{... | collective-permute-start | bytes 1572872 | tf_op jit(solution)/shard_map/ppermute | solution.py:255
  335.7 16.6 %collective-permute-start.48 = (bf16[512,256]{0,1:T(8,128)(2,1)S(1)}, bf16[512,256]{0,1:T(8,128)(2,1)S(1)}, u32[]{:S(2)}, u32[]{:S(2)}) collective-permute-start(bf16[512,256]{0,1:T(8,128)(2,1)S(1)} %get-tuple-element.25), channel_id=1, source_target_pairs={{2,3},{1,2},{0,1},{5,4},{6,5},{7,6},{10,11},{9,10},{8,9},{13,12},{... | collective-permute-start | bytes 786440 | tf_op jit(solution)/shard_map/ppermute | solution.py:264
  344.1 16.6 %collective-permute-start.57 = (bf16[512,256]{0,1:T(8,128)(2,1)S(1)}, bf16[512,256]{0,1:T(8,128)(2,1)S(1)}, u32[]{:S(2)}, u32[]{:S(2)}) collective-permute-start(bf16[512,256]{0,1:T(8,128)(2,1)S(1)} %get-tuple-element.29), channel_id=1, source_target_pairs={{2,3},{1,2},{0,1},{5,4},{6,5},{7,6},{10,11},{9,10},{8,9},{13,12},{... | collective-permute-start | bytes 786440 | tf_op jit(solution)/shard_map/ppermute | solution.py:264
  352.5 16.6 %collective-permute-start.49 = (bf16[512,256]{0,1:T(8,128)(2,1)S(1)}, bf16[512,256]{0,1:T(8,128)(2,1)S(1)}, u32[]{:S(2)}, u32[]{:S(2)}) collective-permute-start(bf16[512,256]{0,1:T(8,128)(2,1)S(1)} %get-tuple-element.23), channel_id=1, source_target_pairs={{2,3},{1,2},{0,1},{5,4},{6,5},{7,6},{10,11},{9,10},{8,9},{13,12},{... | collective-permute-start | bytes 786440 | tf_op jit(solution)/shard_map/ppermute | solution.py:264
  360.9 16.6 %collective-permute-start.61 = (bf16[512,256]{0,1:T(8,128)(2,1)S(1)}, bf16[512,256]{0,1:T(8,128)(2,1)S(1)}, u32[]{:S(2)}, u32[]{:S(2)}) collective-permute-start(bf16[512,256]{0,1:T(8,128)(2,1)S(1)} %get-tuple-element.27), channel_id=1, source_target_pairs={{2,3},{1,2},{0,1},{5,4},{6,5},{7,6},{10,11},{9,10},{8,9},{13,12},{... | collective-permute-start | bytes 786440 | tf_op jit(solution)/shard_map/ppermute | solution.py:264
  369.4 16.7 %collective-permute-start.59 = (bf16[512,256]{0,1:T(8,128)(2,1)S(1)}, bf16[512,256]{0,1:T(8,128)(2,1)S(1)}, u32[]{:S(2)}, u32[]{:S(2)}) collective-permute-start(bf16[512,256]{0,1:T(8,128)(2,1)S(1)} %get-tuple-element.21), channel_id=1, source_target_pairs={{2,3},{1,2},{0,1},{5,4},{6,5},{7,6},{10,11},{9,10},{8,9},{13,12},{... | collective-permute-start | bytes 786440 | tf_op jit(solution)/shard_map/ppermute | solution.py:264
  377.8 16.7 %collective-permute-start.65 = (bf16[512,256]{0,1:T(8,128)(2,1)S(1)}, bf16[512,256]{0,1:T(8,128)(2,1)S(1)}, u32[]{:S(2)}, u32[]{:S(2)}) collective-permute-start(bf16[512,256]{0,1:T(8,128)(2,1)S(1)} %get-tuple-element.19), channel_id=1, source_target_pairs={{2,3},{1,2},{0,1},{5,4},{6,5},{7,6},{10,11},{9,10},{8,9},{13,12},{... | collective-permute-start | bytes 786440 | tf_op jit(solution)/shard_map/ppermute | solution.py:264
  379.3 14.9 %collective-permute-start.68 = (bf16[512,512]{0,1:T(8,128)(2,1)S(1)}, bf16[512,512]{0,1:T(8,128)(2,1)S(1)}, u32[]{:S(2)}, u32[]{:S(2)}) collective-permute-start(bf16[512,512]{0,1:T(8,128)(2,1)S(1)} %get-tuple-element.73), channel_id=1, source_target_pairs={{3,2},{2,1},{1,0},{4,5},{5,6},{6,7},{11,10},{10,9},{9,8},{12,13},{... | collective-permute-start | bytes 1572872 | tf_op jit(solution)/shard_map/ppermute | solution.py:255
  386.2 17.2 %collective-permute-start.63 = (bf16[512,256]{0,1:T(8,128)(2,1)S(1)}, bf16[512,256]{0,1:T(8,128)(2,1)S(1)}, u32[]{:S(2)}, u32[]{:S(2)}) collective-permute-start(bf16[512,256]{0,1:T(8,128)(2,1)S(1)} %get-tuple-element.15), channel_id=1, source_target_pairs={{2,3},{1,2},{0,1},{5,4},{6,5},{7,6},{10,11},{9,10},{8,9},{13,12},{... | collective-permute-start | bytes 786440 | tf_op jit(solution)/shard_map/ppermute | solution.py:264
  394.7 15.7 %collective-permute-start.69 = (bf16[512,256]{0,1:T(8,128)(2,1)S(1)}, bf16[512,256]{0,1:T(8,128)(2,1)S(1)}, u32[]{:S(2)}, u32[]{:S(2)}) collective-permute-start(bf16[512,256]{0,1:T(8,128)(2,1)S(1)} %get-tuple-element.17), channel_id=1, source_target_pairs={{2,3},{1,2},{0,1},{5,4},{6,5},{7,6},{10,11},{9,10},{8,9},{13,12},{... | collective-permute-start | bytes 786440 | tf_op jit(solution)/shard_map/ppermute | solution.py:264
  402.1 19.3 %collective-permute-start.70 = (bf16[512,512]{0,1:T(8,128)(2,1)S(1)}, bf16[512,512]{0,1:T(8,128)(2,1)S(1)}, u32[]{:S(2)}, u32[]{:S(2)}) collective-permute-start(bf16[512,512]{0,1:T(8,128)(2,1)S(1)} %get-tuple-element.65), channel_id=1, source_target_pairs={{3,2},{2,1},{1,0},{4,5},{5,6},{6,7},{11,10},{10,9},{9,8},{12,13},{... | collective-permute-start | bytes 1572872 | tf_op jit(solution)/shard_map/ppermute | solution.py:255
  403.6 17.9 %collective-permute-start.67 = (bf16[512,256]{0,1:T(8,128)(2,1)S(1)}, bf16[512,256]{0,1:T(8,128)(2,1)S(1)}, u32[]{:S(2)}, u32[]{:S(2)}) collective-permute-start(bf16[512,256]{0,1:T(8,128)(2,1)S(1)} %get-tuple-element.13), channel_id=1, source_target_pairs={{2,3},{1,2},{0,1},{5,4},{6,5},{7,6},{10,11},{9,10},{8,9},{13,12},{... | collective-permute-start | bytes 786440 | tf_op jit(solution)/shard_map/ppermute | solution.py:264
  (81 other events, 923.7 us)

commit v2 on v1

v2 whole, which is shorter than its diff:
```python
import jax
import jax.numpy as jnp
from jax import lax
from jax.sharding import PartitionSpec as P


HEAD_DIM = 128
BF = jnp.bfloat16
F32 = jnp.float32
WIDTH = 256
EARLY = 10


def rotate(values, positions):
    half_dim = values.shape[-1] // 2
    exponent = jnp.arange(half_dim, dtype=F32) * (2.0 / values.shape[-1])
    frequency = 500000.0 ** (-exponent)
    angles = positions.astype(F32)[:, None] * frequency[None, :]
    cosine = jnp.cos(angles)
    sine_part = jnp.sin(angles)
    first_half = values[..., :half_dim]
    second_half = values[..., half_dim:]
    return jnp.concatenate(
        [
            first_half * cosine - second_half * sine_part,
            second_half * cosine + first_half * sine_part,
        ],
        axis=-1,
    )


def flip_blocks(x, b):
    view = x.reshape(x.shape[0] // (2 * b), 2, b, *x.shape[1:])
    return view[:, ::-1].reshape(x.shape)


class Grid:
    def __init__(self):
        self.C = lax.axis_size("ctx")
        self.M = lax.axis_size("mp")
        self.c = lax.axis_index("ctx")
        self.m = lax.axis_index("mp")
        self.H = self.C // self.M
        self.far_bits = []
        bit = 2
        while bit < self.C:
            self.far_bits.append(bit)
            bit *= 2
        self.even = list(range(0, self.C, 2))
        self.order = self.even + [i + 1 for i in self.even]

    def bit(self, b):
        return (self.c // b) % 2

    def swap(self, x, b):
        return lax.ppermute(x, "ctx", [(i, i ^ b) for i in range(self.C)])

    def flat(self, pairs):
        return [(a * self.M + b, d * self.M + e) for (a, b), (d, e) in pairs]

    def rotate_mp(self, block_for):
        return [
            lax.ppermute(block_for(s), "mp", [(i, (i + s) % self.M) for i in range(self.M)])
            for s in range(1, self.M)
        ]

    def mp_sum(self, x):
        total = x
        for other in self.rotate_mp(lambda s: x):
            total = total + other
        return total

    def far_gather(self, x, bits):
        have = {0: x}
        for b in bits:
            keys = list(have)
            got = self.swap(jnp.stack([have[k] for k in keys]), b)
            for j, k in enumerate(keys):
                have[k ^ b] = got[j]
        return have

    def gather(self, parts):
        a = self.far_gather(parts[0], self.far_bits)
        b = self.far_gather(parts[1], self.far_bits[::-1])
        near = jnp.concatenate(
            [jnp.concatenate([a[i], b[i]], axis=1) for i in self.even], axis=0
        )
        return jnp.concatenate([near, self.swap(near, 1)], axis=0)

    def small_gather(self, x):
        near = self.far_gather(x, self.far_bits)
        near = jnp.stack([near[i] for i in self.even])
        other = self.swap(near, 1)
        return jnp.stack([near, other], axis=1).reshape(self.C, *x.shape)

    def xor_order(self, x, value):
        b = 1
        while b < self.C:
            x = jnp.where((value // b) % 2 == 1, flip_blocks(x, b), x)
            b *= 2
        return x

    def far_halve(self, blocks, bits):
        for b in bits:
            keep = [k for k in blocks if not k & b]
            got = self.swap(jnp.stack([blocks[k ^ b] for k in keep]).astype(BF), b)
            blocks = {k: blocks[k] + got[j].astype(F32) for j, k in enumerate(keep)}
        return blocks[0]

    def scatter_sum(self, near, far):
        half = near.shape[1] // 2
        n = near.shape[0] // len(self.even)
        near = near + self.swap(far.astype(BF), 1).astype(F32)
        parts = []
        for cols, bits in (
            (slice(0, half), self.far_bits[::-1]),
            (slice(half, None), self.far_bits),
        ):
            blocks = {i: near[j * n : (j + 1) * n, cols] for j, i in enumerate(self.even)}
            parts.append(self.far_halve(blocks, bits))
        return jnp.concatenate(parts, axis=1)

    def rows_to_slices(self, local_rows):
        n = local_rows.shape[0]
        f = local_rows.shape[1] // self.H
        payload = [
            lax.dynamic_slice(local_rows, (0, ((self.c % self.H) ^ i) * f), (n, f))
            for i in range(self.H)
        ]
        blocks = []
        for r in range(self.C):
            pairs = [
                ((a, b), (self.H * b + (a ^ r) % self.H, (a ^ r) // self.H))
                for a in range(self.C)
                for b in range(self.M)
            ]
            blocks.append(lax.ppermute(payload[r % self.H], ("ctx", "mp"), self.flat(pairs)))
        arrived = blocks[1]
        b = 1
        while b < self.H:
            swapped = self.bit(b) == 1
            blocks = [jnp.where(swapped, blocks[r ^ b], blocks[r]) for r in range(self.C)]
            b *= 2
        return blocks, arrived

    def slices_to_rows(self, partial):
        n = partial.shape[0] // self.C
        f = partial.shape[1]
        first = self.H * self.m
        full = jnp.zeros((self.C, n, f), BF)
        for r in range(self.C):
            got = lax.dynamic_slice(partial, (((self.c ^ r) ^ first) * n, 0), (n, f))
            if r:
                got = self.swap(got, r)
            full = lax.dynamic_update_slice(full, got[None], (self.c ^ r, 0, 0))

        def share(s):
            return lax.dynamic_slice(full, ((self.m + s) % self.M * self.H, 0, 0), (self.H, n, f))

        total = share(0).astype(F32)
        for got in self.rotate_mp(share):
            total = total + got.astype(F32)
        return [total[h] for h in range(self.H)]


def columns(weight, index):
    return lax.dynamic_slice(
        weight, (0, index * HEAD_DIM), (weight.shape[0], HEAD_DIM)
    )


def head_weights(grid, query_weight, key_weight, value_weight):
    group = grid.c // (grid.C // 2)
    odd = grid.bit(1) == 1
    mine = jnp.where(odd, value_weight, key_weight)
    other = jnp.where(odd, key_weight, value_weight)

    def side(near, kv):
        parts = []
        for g in range(2):
            parts += [columns(query_weight, grid.c ^ (i + near)) for i in grid.even[2 * g : 2 * g + 2]]
            parts.append(columns(kv, group ^ g))
        return jnp.concatenate(parts, axis=1)

    return side(1, other), side(0, mine)


def head_reduce(grid, send, keep):
    d = HEAD_DIM
    near = keep + grid.swap(send, 1).astype(F32)
    half = near.shape[0] // 2
    group_bit = grid.C // 2
    side_bit = grid.far_bits[0]
    first, second = near[:half], near[half:]
    got = grid.swap(first[:, 3 * d :].astype(BF), group_bit).astype(F32)
    a = first[:, : 3 * d] + got
    out = jnp.concatenate([second[:, d : 3 * d], second[:, 4 * d :]], axis=1).astype(BF)
    got = grid.swap(out, side_bit).astype(F32)
    b0 = second[:, :d] + got[:, :d]
    bg0 = second[:, 2 * d : 3 * d] + got[:, d : 2 * d]
    b4 = second[:, 3 * d : 4 * d] + got[:, 2 * d : 3 * d]
    bg1 = second[:, 5 * d :] + got[:, 3 * d :]
    got = grid.swap(a[:, d:].astype(BF), side_bit).astype(F32)
    query_a = a[:, :d] + got[:, :d]
    own_a = a[:, 2 * d :] + got[:, d:]
    got = grid.swap(jnp.concatenate([b4, bg1], axis=1).astype(BF), group_bit).astype(F32)
    query_b = b0 + got[:, :d]
    own_b = bg0 + got[:, d:]
    return jnp.concatenate([query_a, query_b], axis=0), jnp.concatenate([own_a, own_b], axis=0)


def feed_forward(grid, normed, scale, gate_weight, up_weight, down_weight):
    C, M = grid.C, grid.M
    rows = normed.shape[0]
    hidden_cols = gate_weight.shape[1]
    width = WIDTH if hidden_cols % WIDTH == 0 else HEAD_DIM
    count = hidden_cols // width
    streams = 2
    place = jnp.where(grid.c % 2 == 1, grid.m, M - 1 - grid.m)

    def at(a, p):
        return (a, p if a % 2 == 1 else M - 1 - p)

    inward = grid.flat([(at(a, p), at(a, p + 1)) for a in range(C) for p in range(M - 1)])
    outward = grid.flat([(at(a, p + 1), at(a, p)) for a in range(C) for p in range(M - 1)])

    def choose(options):
        return lax.select_n(place, *options)

    partial = {}

    def part(k):
        if k not in partial:
            lo, hi = k * width, (k + 1) * width
            g = jnp.dot(normed, gate_weight[:, lo:hi], preferred_element_type=F32)
            u = jnp.dot(normed, up_weight[:, lo:hi], preferred_element_type=F32)
            partial[k] = jnp.concatenate([g.astype(BF), u.astype(BF)], axis=1)
        return partial[k]

    lists = [list(range(s, count, streams)) for s in range(streams)]
    got = [None] * streams
    passed = [None] * streams
    hist = [[] for _ in range(streams)]
    hids = [[] for _ in range(streams)]
    waiting = []
    taken = 0
    total = None
    zero = jnp.zeros((rows, 2 * width), BF)
    tick = normed[:8, :128].astype(F32) * 0.0
    last = max(len(ks) for ks in lists) + 2 * (M - 1) - 1
    for t in range(last + 1):
        for s in range(streams):
            ks = lists[s]
            n = len(ks)
            came = got[s]
            if t < n + M - 2:
                options = [part(ks[t - p]) if 0 <= t - p < n else zero for p in range(M - 1)]
                own = choose(options + [zero])
                send = own if came is None else (own.astype(F32) + came.astype(F32)).astype(BF)
                got[s] = lax.ppermute(send, ("ctx", "mp"), inward)
            i = t - (M - 1)
            if 0 <= i < n + M - 2:
                if i < n:
                    full = came.astype(F32) + part(ks[i]).astype(F32)
                    g, u = full[:, :width] * scale, full[:, width:] * scale
                    hids[s].append((jax.nn.silu(g) * u).astype(BF))
                fresh = hids[s][i] if i < n else jnp.zeros((rows, width), BF)
                send = fresh if passed[s] is None else jnp.where(place == M - 1, fresh, passed[s])
                passed[s] = lax.ppermute(send, ("ctx", "mp"), outward)
                hist[s].append(passed[s])
            j = i - (M - 2) - 1
            if 0 <= j < n:
                options = [hist[s][j + M - 2 - p] for p in range(M - 1)] + [hids[s][j]]
                here = place
                if taken:
                    *options, here = lax.optimization_barrier((*options, place))
                waiting.append((ks[j], lax.select_n(here, *options)))
            tick = tick * 0.5
            tick = lax.optimization_barrier(tick)
            final = t == last and s == streams - 1
            if (not taken and len(waiting) >= EARLY) or (final and waiting):
                waiting.sort(key=lambda kv: kv[0])
                k0, k1 = waiting[0][0], waiting[-1][0] + 1
                assert k1 - k0 == len(waiting)
                block = lax.optimization_barrier(jnp.concatenate([b for _, b in waiting], axis=1))
                taken += len(waiting)
                waiting.clear()
                weight = down_weight[k0 * width : k1 * width]
                if final:
                    half = rows // 2
                    far = jnp.dot(block[half:], weight, preferred_element_type=F32)
                    near = jnp.dot(block[:half], weight, preferred_element_type=F32)
                    if total is not None:
                        far = far + total[half:]
                        near = near + total[:half]
                    total = near, far
                else:
                    total = jnp.dot(block, weight, preferred_element_type=F32)
                    total = lax.optimization_barrier(total)
    return *total, jnp.sum(tick)


def body(
    tokens,
    norm_gain,
    router_weight,
    query_weight,
    key_weight,
    value_weight,
    out_weight,
    mlp_gain,
    gate_weight,
    up_weight,
    down_weight,
    destination,
    kept_pos,
):
    grid = Grid()
    ctx_count, mp_count = grid.C, grid.M
    my_index = grid.c
    tok_dev = tokens.shape[0]
    kept_dev = kept_pos.shape[0]
    rows = kept_dev * ctx_count
    feature_cols = tokens.shape[1]
    feature_total = feature_cols * mp_count
    slice_cols = feature_total // ctx_count
    capacity = (3 * kept_dev // 2 + ctx_count - 1) // ctx_count
    slots_all = ctx_count * capacity
    head_dim = HEAD_DIM
    query_cols = query_weight.shape[1]
    key_cols = key_weight.shape[1]
    kv_local = key_cols // head_dim
    q_local = query_cols // head_dim
    group_size = q_local // kv_local
    peer_ids = jnp.arange(ctx_count, dtype=jnp.int32)
    is_kept = destination >= 0
    owner_ids = destination // kept_dev
    slot_ids = destination % kept_dev
    kept_order = slot_ids * ctx_count + owner_ids
    first_order = jnp.min(jnp.where(is_kept, kept_order, ctx_count * kept_dev))
    first_slots = (first_order - peer_ids + ctx_count - 1) // ctx_count
    owner_match = owner_ids[:, None] == peer_ids[None, :]
    send_index = (
        owner_ids * capacity
        + slot_ids
        - jnp.sum(jnp.where(owner_match, first_slots[None, :], 0), axis=1)
    )
    send_index = jnp.where(is_kept, send_index, slots_all)
    slot_ids_all = jnp.arange(slots_all, dtype=jnp.int32)
    takes = (slot_ids_all[:, None] == send_index[None, :]).astype(BF)
    outgoing = (
        jnp.dot(takes, tokens, preferred_element_type=F32)
        .astype(BF)
        .reshape(ctx_count, capacity, feature_cols)
    )
    incoming = lax.all_to_all(outgoing, "ctx", split_axis=0, concat_axis=0, tiled=True).reshape(
        slots_all, feature_cols
    )
    slot_range = jnp.arange(kept_dev, dtype=jnp.int32)
    source_ids = kept_pos // tok_dev
    source_match = source_ids[:, None] == peer_ids[None, :]
    first_from = jnp.min(jnp.where(source_match, slot_range[:, None], kept_dev), axis=0)
    recv_index = (
        source_ids * capacity
        + slot_range
        - jnp.sum(jnp.where(source_match, first_from[None, :], 0), axis=1)
    )
    local_rows = incoming[recv_index]
    fits = q_local == ctx_count and kv_local == 2 and len(grid.far_bits) == 2
    blocks, arrived = grid.rows_to_slices(local_rows)
    my_rows, _ = lax.optimization_barrier((local_rows, arrived))
    raw_share = my_rows.astype(F32)
    my_router = lax.dynamic_slice(router_weight, (grid.m * feature_cols,), (feature_cols,))
    sums = grid.mp_sum(
        jnp.stack(
            [
                jnp.sum(raw_share * raw_share, axis=1),
                jnp.sum(raw_share * my_router.astype(F32)[None, :], axis=1),
            ]
        )
    )
    router_score = jax.nn.sigmoid(sums[1])
    inverse = lax.rsqrt(sums[0] / feature_total + 1e-05)
    shared = grid.small_gather(jnp.stack([inverse, kept_pos.astype(F32)]))
    shared = grid.xor_order(shared, my_index ^ (grid.H * grid.m))
    inverse_all = shared[:, 0].reshape(rows)
    pos_all = shared[:, 1].reshape(rows)
    my_gain = lax.dynamic_slice(norm_gain, (my_index * slice_cols,), (slice_cols,))
    my_gain = my_gain.astype(F32)[None, :]
    scaled = jnp.concatenate([(b.astype(F32) * my_gain).astype(BF) for b in blocks], axis=0)
    softmax_scale = head_dim ** (-0.5)
    if fits:
        send_weight, keep_weight = head_weights(grid, query_weight, key_weight, value_weight)
        out_rows = jnp.concatenate(
            [
                lax.dynamic_slice(
                    out_weight, ((my_index ^ i) * head_dim, 0), (head_dim, out_weight.shape[1])
                )
                for i in grid.order
            ],
            axis=0,
        )
        send = jnp.dot(scaled, send_weight, preferred_element_type=F32).astype(BF)
        keep = jnp.dot(scaled, keep_weight, preferred_element_type=F32)
        query, own = head_reduce(grid, send, keep)
        query = rotate(query * inverse_all[:, None], pos_all).astype(BF)
        own = own * inverse_all[:, None]
        even = grid.bit(1) == 0
        own = jnp.where(even, rotate(own, pos_all), own).astype(BF)
        other = grid.swap(own, 1)
        keys = jnp.where(even, own, other)
        values = jnp.where(even, other, own)
        allowed = pos_all[None, :] <= pos_all[:, None]
        scores = (
            lax.dot_general(query, keys, (((1,), (1,)), ((), ())), preferred_element_type=F32)
            * softmax_scale
        )
        scores = jnp.where(allowed, scores, -1e30)
        peak = jnp.max(scores, axis=-1, keepdims=True)
        weights = jnp.where(allowed, jnp.exp(scores - peak), 0.0)
        weighted = jnp.dot(weights, values.astype(F32))
        attended = (weighted / jnp.sum(weights, axis=-1, keepdims=True)).astype(BF)
        half = rows // 2
        first = grid.far_gather(attended[:half], grid.far_bits)
        second = grid.far_gather(attended[half:], grid.far_bits[::-1])
        near = jnp.concatenate(
            [jnp.concatenate([first[i], second[i]], axis=0) for i in grid.even], axis=1
        )
        span = len(grid.even) * head_dim
        partial_cols = jnp.dot(near, out_rows[:span], preferred_element_type=F32) + jnp.dot(
            grid.swap(near, 1), out_rows[span:], preferred_element_type=F32
        )
    else:
        stacked = jnp.concatenate([query_weight, key_weight, value_weight], axis=1)
        projected = jnp.dot(scaled, stacked, preferred_element_type=F32)
        mine = lax.psum_scatter(projected, "ctx", scatter_dimension=0, tiled=True)
        my_inverse = lax.dynamic_slice(inverse_all, (my_index * kept_dev,), (kept_dev,))
        my_pos = lax.dynamic_slice(pos_all, (my_index * kept_dev,), (kept_dev,))
        mine = mine * my_inverse[:, None]
        by_head = mine.reshape(kept_dev, q_local + 2 * kv_local, head_dim).transpose(1, 0, 2)
        queries = rotate(by_head[:q_local], my_pos).astype(BF)
        queries = queries.reshape(kv_local, group_size, kept_dev, head_dim)
        keys = rotate(by_head[q_local : q_local + kv_local], my_pos).astype(BF)
        values = by_head[q_local + kv_local :].astype(BF)
        keys = lax.all_gather(keys, "ctx", axis=1, tiled=True)
        values = lax.all_gather(values, "ctx", axis=1, tiled=True)
        allowed = pos_all[None, :] <= my_pos[:, None]
        scores = (
            jnp.einsum("hgqd,hkd->hgqk", queries, keys, preferred_element_type=F32) * softmax_scale
        )
        scores = jnp.where(allowed, scores, -1e30)
        peak = jnp.max(scores, axis=-1, keepdims=True)
        weights = jnp.where(allowed, jnp.exp(scores - peak), 0.0)
        weighted = jnp.einsum("hgqk,hkd->hgqd", weights, values.astype(F32))
        attended = weighted / jnp.sum(weights, axis=-1, keepdims=True)
        attended = attended.transpose(2, 0, 1, 3).reshape(kept_dev, query_cols).astype(BF)
        every_head = lax.all_gather(attended, "ctx", axis=0, tiled=True)
        partial_cols = jnp.dot(every_head, out_weight, preferred_element_type=F32)
    head_share = jnp.concatenate(grid.slices_to_rows(partial_cols.astype(BF)), axis=1)
    mixed_share = raw_share + head_share
    square_sum = grid.mp_sum(jnp.sum(mixed_share * mixed_share, axis=1))
    second_inverse = grid.small_gather(lax.rsqrt(square_sum / feature_total + 1e-05))
    second_inverse = second_inverse[jnp.array(grid.order)].reshape(rows, 1)
    second_scaled = (mixed_share * mlp_gain.astype(F32)).astype(BF)
    mid = feature_cols // 2
    every_scaled = grid.gather((second_scaled[:, :mid], second_scaled[:, mid:]))
    near, far, tick = feed_forward(
        grid, every_scaled, second_inverse, gate_weight, up_weight, down_weight
    )
    mlp_share = grid.scatter_sum(near, far)
    update = (router_score[:, None] * (head_share + mlp_share) + tick).astype(BF)
    places = (slot_ids_all[:, None] == recv_index[None, :]).astype(BF)
    returning = (
        jnp.dot(places, update, preferred_element_type=F32)
        .astype(BF)
        .reshape(ctx_count, capacity, feature_cols)
    )
    returned = lax.all_to_all(returning, "ctx", split_axis=0, concat_axis=0, tiled=True).reshape(
        slots_all, feature_cols
    )
    lands = (send_index[:, None] == slot_ids_all[None, :]).astype(BF)
    arriving = jnp.dot(lands, returned, preferred_element_type=F32)
    return (tokens.astype(F32) + arriving).astype(BF)


def solution(mesh):
    in_specs = (
        P("ctx", "mp"),
        P(),
        P(),
        P("ctx", "mp"),
        P("ctx", "mp"),
        P("ctx", "mp"),
        P("mp", "ctx"),
        P("mp"),
        P("mp", "ctx"),
        P("mp", "ctx"),
        P("ctx", "mp"),
        P("ctx"),
        P("ctx"),
    )
    out_specs = P("ctx", "mp")
    return jax.shard_map(body, mesh=mesh, in_specs=in_specs, out_specs=out_specs, check_vma=False)
```

time: 502 us -> 446 us (0.89)
  waiting for transfers between devices: 224 us -> 162 us
  matrix products: 45.1 us -> 63.9 us
  local copies, waits for them, and re-layouts: 27.7 us -> 12.9 us
  blocking collectives: 0 us -> 12.1 us
  other arithmetic: 35.6 us -> 25.6 us
    ppermute x22 -> x17, waiting for transfers between devices: 60.3 us -> 26.1 us  [the longest x9 26.1 us: rotate_mp(): lax.ppermute(block_for(s), 'mp', [(i, (i + s) % self.M) for i in range(se...]
    ppermute x22 -> x17, starting transfers between devices: 62.8 us -> 37.4 us  [the longest x8 20.7 us: rows_to_slices(): lax.ppermute(payload[r % self.H], ('ctx', 'mp'), self.flat(pairs))]
    ppermute x18, starting transfers between devices: 41.6 us -> 61.3 us  [feed_forward(): passed[s] = lax.ppermute(send, ('ctx', 'mp'), outward)]
    ppermute x18, waiting for transfers between devices: 87.3 us -> 67.7 us  [feed_forward(): got[s] = lax.ppermute(send, ('ctx', 'mp'), inward)]
    dot_general x6 -> x10, matrix products: 13.9 us -> 27.3 us  [the longest x1 7.14 us: feed_forward(): total = jnp.dot(block, weight, preferred_element_type=F32)]
    all_to_all x0 -> x1, blocking collectives: none -> 12.1 us  [body(): lax.all_to_all(returning, 'ctx', split_axis=0, concat_axis=0, tiled=True)]
    ppermute x25 -> x34, starting transfers between devices: 25.3 us -> 35.1 us  [swap(): return lax.ppermute(x, 'ctx', [(i, i ^ b) for i in range(self.C)])]
    all_to_all x1 -> x0, waiting for transfers between devices: 9.62 us -> none  [body(): lax.all_to_all(returning, 'ctx', split_axis=0, concat_axis=0, tiled=True)]
  transfers between devices with their start and end apart: 85 -> 88, of which waited for: 53 -> 48; matrix products, arithmetic and copies ran while one was open for 6% -> 9% of each run, Pallas kernels for 0% -> 0%
where the time goes in v2:
time: 446 us; the launch traced here: 442 us
  starting transfers between devices  162 us (36%)
  waiting for transfers between devices  162 us (36%)
  matrix products  63.9 us (14%)
  other arithmetic  25.6 us (6%)
  local copies, waits for them, and re-layouts  12.9 us (3%)
  blocking collectives  12.1 us (3%)
    ppermute x18, waiting for transfers between devices, feed_forward(): got[s] = lax.ppermute(send, ('ctx', 'mp'), inward)  67.7 us
    ppermute x18, starting transfers between devices, feed_forward(): passed[s] = lax.ppermute(send, ('ctx', 'mp'), outward)  61.3 us
    ppermute x34, waiting for transfers between devices, swap(): return lax.ppermute(x, 'ctx', [(i, i ^ b) for i in range(self.C)])  55.2 us
    ppermute x34, starting transfers between devices, swap(): return lax.ppermute(x, 'ctx', [(i, i ^ b) for i in range(self.C)])  35.1 us
    ppermute x9, waiting for transfers between devices, rotate_mp(): lax.ppermute(block_for(s), 'mp', [(i, (i + s) % self.M) for i in range(se...  26.1 us
    ppermute x18, starting transfers between devices, feed_forward(): got[s] = lax.ppermute(send, ('ctx', 'mp'), inward)  23.4 us
    ppermute x8, starting transfers between devices, rows_to_slices(): lax.ppermute(payload[r % self.H], ('ctx', 'mp'), self.flat(pairs))  20.7 us
    dot_general x14, matrix products, part(): g = jnp.dot(normed, gate_weight[:, lo:hi], preferred_element_type=F32)  19.1 us
  transfers between devices with their start and end apart: 88, of which 48 were waited for; matrix products, arithmetic and copies ran while one was open for 9% of the time, Pallas kernels for 0%

profile of v2, /device:TPU:0, one launch (start us, length us, event | category | flops | bytes accessed | tf_op | source)
XLA Modules:
  0.0 441.5 jit_solution(7334835690105004663)
XLA Ops:
  5.9 5.2 %all-to-all-start = ((bf16[8,12,2048]{2,1,0:T(8,128)(2,1)}), bf16[8,12,2048]{2,1,0:T(8,128)(2,1)S(1)}, u32[]{:S(2)}, u32[]{:S(2)}) async-start(bf16[8,12,2048]{2,1,0:T(8,128)(2,1)} %reshape.138), calls=%async_computation | async-start | bytes 1048576 | tf_op jit(solution)/shard_map/all_to_all | solution.py:356
  23.3 5.2 %collective-permute-start.8 = (bf16[64,1024]{1,0:T(8,128)(2,1)S(1)}, bf16[64,1024]{1,0:T(8,128)(2,1)S(1)}, u32[]{:S(2)}, u32[]{:S(2)}) collective-permute-start(bf16[64,1024]{1,0:T(8,128)(2,1)S(1)} %get-tuple-element.172), channel_id=1, source_target_pairs={{0,5},{1,13},{2,21},{3,29},{4,1},{5,9},{6,17},{7,25},{8,4},{9,12},... | collective-permute-start | bytes 393224 | tf_op jit(solution)/shard_map/ppermute | solution.py:137
  28.5 5.7 %collective-permute-start.10 = (bf16[64,1024]{1,0:T(8,128)(2,1)S(1)}, bf16[64,1024]{1,0:T(8,128)(2,1)S(1)}, u32[]{:S(2)}, u32[]{:S(2)}) collective-permute-start(bf16[64,1024]{1,0:T(8,128)(2,1)S(1)} %get-tuple-element.172), channel_id=1, source_target_pairs={{0,6},{1,14},{2,22},{3,30},{4,2},{5,10},{6,18},{7,26},{8,7},{9,15}... | collective-permute-start | bytes 393224 | tf_op jit(solution)/shard_map/ppermute | solution.py:137
  34.5 4.7 %collective-permute-start.12 = (bf16[64,1024]{1,0:T(8,128)(2,1)S(1)}, bf16[64,1024]{1,0:T(8,128)(2,1)S(1)}, u32[]{:S(2)}, u32[]{:S(2)}) collective-permute-start(bf16[64,1024]{1,0:T(8,128)(2,1)S(1)} %get-tuple-element.172), channel_id=1, source_target_pairs={{0,7},{1,15},{2,23},{3,31},{4,3},{5,11},{6,19},{7,27},{8,6},{9,14}... | collective-permute-start | bytes 393224 | tf_op jit(solution)/shard_map/ppermute | solution.py:137
  39.5 4.1 collective-permute-start.13
  45.1 6.9 %collective-permute-start.2 = (f32[2,64]{1,0:T(2,128)S(1)}, f32[2,64]{1,0:T(2,128)S(1)}, u32[]{:S(2)}, u32[]{:S(2)}) collective-permute-start(f32[2,64]{1,0:T(2,128)S(1)} %pad_maximum_fusion.29), channel_id=1, source_target_pairs={{0,2},{1,3},{2,0},{3,1},{4,6},{5,7},{6,4},{7,5},{8,10},{9,11},{10,... | collective-permute-start | bytes 1544 | tf_op jit(solution)/shard_map/ppermute | solution.py:63
  57.5 6.6 %collective-permute-start.4 = (f32[1,2,64]{2,1,0:T(2,128)S(1)}, f32[1,2,64]{2,1,0:T(2,128)S(1)}, u32[]{:S(2)}, u32[]{:S(2)}) collective-permute-start(f32[1,2,64]{2,1,0:T(2,128)S(1)} %maximum_bitcast_fusion), channel_id=1, source_target_pairs={{0,8},{4,12},{8,0},{12,4},{16,24},{20,28},{24,16},{28,20},{1,9},{5... | collective-permute-start | bytes 1544 | tf_op jit(solution)/shard_map/ppermute | solution.py:56
  78.0 5.0 %collective-permute-done.15 = bf16[256,384]{1,0:T(8,128)(2,1)S(1)} collective-permute-done((bf16[256,384]{1,0:T(8,128)(2,1)S(1)}, bf16[256,384]{1,0:T(8,128)(2,1)S(1)}, u32[]{:S(2)}, u32[]{:S(2)}) %collective-permute-start.15) | collective-permute-done | bytes 196640 | tf_op jit(solution)/shard_map/ppermute | solution.py:56
  116.3 7.4 %collective-permute-done.29 = bf16[64,1024]{1,0:T(8,128)(2,1)S(1)} collective-permute-done((bf16[64,1024]{1,0:T(8,128)(2,1)S(1)}, bf16[64,1024]{1,0:T(8,128)(2,1)S(1)}, u32[]{:S(2)}, u32[]{:S(2)}) %collective-permute-start.29) | collective-permute-done | bytes 131104 | tf_op jit(solution)/shard_map/ppermute | solution.py:56
  125.9 7.0 %collective-permute-done.34 = bf16[2,64,1024]{2,1,0:T(8,128)(2,1)S(1)} collective-permute-done((bf16[2,64,1024]{2,1,0:T(8,128)(2,1)S(1)}, bf16[2,64,1024]{2,1,0:T(8,128)(2,1)S(1)}, u32[]{:S(2)}, u32[]{:S(2)}) %collective-permute-start.34) | collective-permute-done | bytes 262176 | tf_op jit(solution)/shard_map/ppermute | solution.py:63
  132.9 15.4 %collective-permute-done.33 = bf16[2,64,1024]{2,1,0:T(8,128)(2,1)S(1)} collective-permute-done((bf16[2,64,1024]{2,1,0:T(8,128)(2,1)S(1)}, bf16[2,64,1024]{2,1,0:T(8,128)(2,1)S(1)}, u32[]{:S(2)}, u32[]{:S(2)}) %collective-permute-start.33) | collective-permute-done | bytes 262176 | tf_op jit(solution)/shard_map/ppermute | solution.py:63
  212.9 12.4 %collective-permute-done.40 = bf16[512,512]{0,1:T(8,128)(2,1)S(1)} collective-permute-done((bf16[512,512]{0,1:T(8,128)(2,1)S(1)}, bf16[512,512]{0,1:T(8,128)(2,1)S(1)}, u32[]{:S(2)}, u32[]{:S(2)}) %collective-permute-start.40) | collective-permute-done | bytes 524320 | tf_op jit(solution)/shard_map/ppermute | solution.py:260
  229.2 7.5 %collective-permute-done.41 = bf16[512,512]{0,1:T(8,128)(2,1)S(1)} collective-permute-done((bf16[512,512]{0,1:T(8,128)(2,1)S(1)}, bf16[512,512]{0,1:T(8,128)(2,1)S(1)}, u32[]{:S(2)}, u32[]{:S(2)}) %collective-permute-start.41) | collective-permute-done | bytes 524320 | tf_op jit(solution)/shard_map/ppermute | solution.py:260
  238.2 4.0 collective-permute-done.64
  249.7 3.9 collective-permute-done.65
  265.4 4.6 %collective-permute-start.56 = (bf16[512,256]{0,1:T(8,128)(2,1)S(1)}, bf16[512,256]{0,1:T(8,128)(2,1)S(1)}, u32[]{:S(2)}, u32[]{:S(2)}) collective-permute-start(bf16[512,256]{0,1:T(8,128)(2,1)S(1)} %get-tuple-element.71), channel_id=1, source_target_pairs={{2,3},{1,2},{0,1},{5,4},{6,5},{7,6},{10,11},{9,10},{8,9},{13,12},{... | collective-permute-start | bytes 786440 | tf_op jit(solution)/shard_map/ppermute | solution.py:269
  275.2 3.9 collective-permute-done.44
  281.0 4.6 %collective-permute-start.57 = (bf16[512,256]{0,1:T(8,128)(2,1)S(1)}, bf16[512,256]{0,1:T(8,128)(2,1)S(1)}, u32[]{:S(2)}, u32[]{:S(2)}) collective-permute-start(bf16[512,256]{0,1:T(8,128)(2,1)S(1)} %get-tuple-element.69), channel_id=1, source_target_pairs={{2,3},{1,2},{0,1},{5,4},{6,5},{7,6},{10,11},{9,10},{8,9},{13,12},{... | collective-permute-start | bytes 786440 | tf_op jit(solution)/shard_map/ppermute | solution.py:269
  287.3 6.1 %collective-permute-done.45 = bf16[512,512]{0,1:T(8,128)(2,1)S(1)} collective-permute-done((bf16[512,512]{0,1:T(8,128)(2,1)S(1)}, bf16[512,512]{0,1:T(8,128)(2,1)S(1)}, u32[]{:S(2)}, u32[]{:S(2)}) %collective-permute-start.45) | collective-permute-done | bytes 524320 | tf_op jit(solution)/shard_map/ppermute | solution.py:260
  302.8 4.6 %collective-permute-start.74 = (bf16[512,256]{0,1:T(8,128)(2,1)S(1)}, bf16[512,256]{0,1:T(8,128)(2,1)S(1)}, u32[]{:S(2)}, u32[]{:S(2)}) collective-permute-start(bf16[512,256]{0,1:T(8,128)(2,1)S(1)} %get-tuple-element.65), channel_id=1, source_target_pairs={{2,3},{1,2},{0,1},{5,4},{6,5},{7,6},{10,11},{9,10},{8,9},{13,12},{... | collective-permute-start | bytes 786440 | tf_op jit(solution)/shard_map/ppermute | solution.py:269
  313.3 4.4 collective-permute-start.75
  319.6 6.4 %collective-permute-done.46 = bf16[512,512]{0,1:T(8,128)(2,1)S(1)} collective-permute-done((bf16[512,512]{0,1:T(8,128)(2,1)S(1)}, bf16[512,512]{0,1:T(8,128)(2,1)S(1)}, u32[]{:S(2)}, u32[]{:S(2)}) %collective-permute-start.46) | collective-permute-done | bytes 524320 | tf_op jit(solution)/shard_map/ppermute | solution.py:260
  328.0 4.8 %collective-permute-start.59 = (bf16[512,256]{0,1:T(8,128)(2,1)S(1)}, bf16[512,256]{0,1:T(8,128)(2,1)S(1)}, u32[]{:S(2)}, u32[]{:S(2)}) collective-permute-start(bf16[512,256]{0,1:T(8,128)(2,1)S(1)} %get-tuple-element.59), channel_id=1, source_target_pairs={{2,3},{1,2},{0,1},{5,4},{6,5},{7,6},{10,11},{9,10},{8,9},{13,12},{... | collective-permute-start | bytes 786440 | tf_op jit(solution)/shard_map/ppermute | solution.py:269
  335.4 7.4 %collective-permute-done.47 = bf16[512,512]{0,1:T(8,128)(2,1)S(1)} collective-permute-done((bf16[512,512]{0,1:T(8,128)(2,1)S(1)}, bf16[512,512]{0,1:T(8,128)(2,1)S(1)}, u32[]{:S(2)}, u32[]{:S(2)}) %collective-permute-start.47) | collective-permute-done | bytes 524320 | tf_op jit(solution)/shard_map/ppermute | solution.py:260
  345.4 4.8 %collective-permute-start.77 = (bf16[512,256]{0,1:T(8,128)(2,1)S(1)}, bf16[512,256]{0,1:T(8,128)(2,1)S(1)}, u32[]{:S(2)}, u32[]{:S(2)}) collective-permute-start(bf16[512,256]{0,1:T(8,128)(2,1)S(1)} %get-tuple-element.53), channel_id=1, source_target_pairs={{2,3},{1,2},{0,1},{5,4},{6,5},{7,6},{10,11},{9,10},{8,9},{13,12},{... | collective-permute-start | bytes 786440 | tf_op jit(solution)/shard_map/ppermute | solution.py:269
  351.6 4.6 %collective-permute-start.60 = (bf16[512,256]{0,1:T(8,128)(2,1)S(1)}, bf16[512,256]{0,1:T(8,128)(2,1)S(1)}, u32[]{:S(2)}, u32[]{:S(2)}) collective-permute-start(bf16[512,256]{0,1:T(8,128)(2,1)S(1)} %get-tuple-element.55), channel_id=1, source_target_pairs={{2,3},{1,2},{0,1},{5,4},{6,5},{7,6},{10,11},{9,10},{8,9},{13,12},{... | collective-permute-start | bytes 786440 | tf_op jit(solution)/shard_map/ppermute | solution.py:269
  360.3 4.5 %collective-permute-start.61 = (bf16[512,256]{0,1:T(8,128)(2,1)S(1)}, bf16[512,256]{0,1:T(8,128)(2,1)S(1)}, u32[]{:S(2)}, u32[]{:S(2)}) collective-permute-start(bf16[512,256]{0,1:T(8,128)(2,1)S(1)} %get-tuple-element.51), channel_id=1, source_target_pairs={{2,3},{1,2},{0,1},{5,4},{6,5},{7,6},{10,11},{9,10},{8,9},{13,12},{... | collective-permute-start | bytes 786440 | tf_op jit(solution)/shard_map/ppermute | solution.py:269
  371.7 4.4 collective-permute-start.79
  378.4 7.1 %fusion = f32[512,2048]{1,0:T(8,128)} fusion(bf16[512,2560]{0,1:T(8,128)(2,1)S(1)} %get-tuple-element.156, bf16[3584,2048]{1,0:T(8,128)(2,1)S(1)} %bitcast.155), kind=kOutput, calls=%fused_computation.2 | convolution fusion | flops 5368709120 | bytes 17301504 | tf_op jit(solution)/shard_map/dot_general | solution.py:298
  409.1 6.4 %collective-permute-done.83 = bf16[2,64,1024]{2,1,0:T(8,128)(2,1)S(1)} collective-permute-done((bf16[2,64,1024]{2,1,0:T(8,128)(2,1)S(1)}, bf16[2,64,1024]{2,1,0:T(8,128)(2,1)S(1)}, u32[]{:S(2)}, u32[]{:S(2)}) %collective-permute-start.83) | collective-permute-done | bytes 262176 | tf_op jit(solution)/shard_map/ppermute | solution.py:56
  416.4 4.2 collective-permute-done.84
  427.0 12.1 %all_to_all.10 = bf16[8,12,2048]{2,1,0:T(8,128)(2,1)S(1)} all-to-all(bf16[8,12,2048]{2,1,0:T(8,128)(2,1)S(1)} %reshape.145), channel_id=1, replica_groups=mesh['ctx'=8,'mp'=4] {'ctx'}, dimensions={0} | all-to-all | bytes 786432 | tf_op jit(solution)/shard_map/all_to_all | solution.py:478
  (420 shorter events, 243.1 us)
Async XLA Ops:
  5.9 14.9 %all-to-all-start = ((bf16[8,12,2048]{2,1,0:T(8,128)(2,1)}), bf16[8,12,2048]{2,1,0:T(8,128)(2,1)S(1)}, u32[]{:S(2)}, u32[]{:S(2)}) async-start(bf16[8,12,2048]{2,1,0:T(8,128)(2,1)} %reshape.138), calls=%async_computation | async-start | bytes 1048576 | tf_op jit(solution)/shard_map/all_to_all | solution.py:356
  23.3 16.2 %collective-permute-start.8 = (bf16[64,1024]{1,0:T(8,128)(2,1)S(1)}, bf16[64,1024]{1,0:T(8,128)(2,1)S(1)}, u32[]{:S(2)}, u32[]{:S(2)}) collective-permute-start(bf16[64,1024]{1,0:T(8,128)(2,1)S(1)} %get-tuple-element.172), channel_id=1, source_target_pairs={{0,5},{1,13},{2,21},{3,29},{4,1},{5,9},{6,17},{7,25},{8,4},{9,12},... | collective-permute-start | bytes 393224 | tf_op jit(solution)/shard_map/ppermute | solution.py:137
  28.5 15.1 %collective-permute-start.9 = (bf16[64,1024]{1,0:T(8,128)(2,1)S(1)}, bf16[64,1024]{1,0:T(8,128)(2,1)S(1)}, u32[]{:S(2)}, u32[]{:S(2)}) collective-permute-start(bf16[64,1024]{1,0:T(8,128)(2,1)S(1)} %get-tuple-element.171), channel_id=1, source_target_pairs={{0,1},{1,9},{2,17},{3,25},{4,5},{5,13},{6,21},{7,29},{8,0},{9,8},{... | collective-permute-start | bytes 393224 | tf_op jit(solution)/shard_map/ppermute | solution.py:137
  28.5 16.6 %collective-permute-start.10 = (bf16[64,1024]{1,0:T(8,128)(2,1)S(1)}, bf16[64,1024]{1,0:T(8,128)(2,1)S(1)}, u32[]{:S(2)}, u32[]{:S(2)}) collective-permute-start(bf16[64,1024]{1,0:T(8,128)(2,1)S(1)} %get-tuple-element.172), channel_id=1, source_target_pairs={{0,6},{1,14},{2,22},{3,30},{4,2},{5,10},{6,18},{7,26},{8,7},{9,15}... | collective-permute-start | bytes 393224 | tf_op jit(solution)/shard_map/ppermute | solution.py:137
  34.2 17.8 %collective-permute-start.11 = (bf16[64,1024]{1,0:T(8,128)(2,1)S(1)}, bf16[64,1024]{1,0:T(8,128)(2,1)S(1)}, u32[]{:S(2)}, u32[]{:S(2)}) collective-permute-start(bf16[64,1024]{1,0:T(8,128)(2,1)S(1)} %get-tuple-element.171), channel_id=1, source_target_pairs={{0,2},{1,10},{2,18},{3,26},{4,6},{5,14},{6,22},{7,30},{8,3},{9,11}... | collective-permute-start | bytes 393224 | tf_op jit(solution)/shard_map/ppermute | solution.py:137
  34.5 19.2 %collective-permute-start.12 = (bf16[64,1024]{1,0:T(8,128)(2,1)S(1)}, bf16[64,1024]{1,0:T(8,128)(2,1)S(1)}, u32[]{:S(2)}, u32[]{:S(2)}) collective-permute-start(bf16[64,1024]{1,0:T(8,128)(2,1)S(1)} %get-tuple-element.172), channel_id=1, source_target_pairs={{0,7},{1,15},{2,23},{3,31},{4,3},{5,11},{6,19},{7,27},{8,6},{9,14}... | collective-permute-start | bytes 393224 | tf_op jit(solution)/shard_map/ppermute | solution.py:137
  39.5 14.2 %collective-permute-start.13 = (bf16[64,1024]{1,0:T(8,128)(2,1)S(1)}, bf16[64,1024]{1,0:T(8,128)(2,1)S(1)}, u32[]{:S(2)}, u32[]{:S(2)}) collective-permute-start(bf16[64,1024]{1,0:T(8,128)(2,1)S(1)} %get-tuple-element.171), channel_id=1, source_target_pairs={{0,3},{1,11},{2,19},{3,27},{4,7},{5,15},{6,23},{7,31},{8,2},{9,10}... | collective-permute-start | bytes 393224 | tf_op jit(solution)/shard_map/ppermute | solution.py:137
  125.0 23.4 %collective-permute-start.33 = (bf16[2,64,1024]{2,1,0:T(8,128)(2,1)S(1)}, bf16[2,64,1024]{2,1,0:T(8,128)(2,1)S(1)}, u32[]{:S(2)}, u32[]{:S(2)}) collective-permute-start(bf16[2,64,1024]{2,1,0:T(8,128)(2,1)S(1)} %get-tuple-element.109), channel_id=1, source_target_pairs={{0,2},{1,3},{2,0},{3,1},{4,6},{5,7},{6,4},{7,5},{8,10},{9,11},{10,... | collective-permute-start | bytes 786440 | tf_op jit(solution)/shard_map/ppermute | solution.py:63
  125.0 23.4 %collective-permute-start.32 = (bf16[2,64,1024]{2,1,0:T(8,128)(2,1)S(1)}, bf16[2,64,1024]{2,1,0:T(8,128)(2,1)S(1)}, u32[]{:S(2)}, u32[]{:S(2)}) collective-permute-start(bf16[2,64,1024]{2,1,0:T(8,128)(2,1)S(1)} %get-tuple-element.107), channel_id=1, source_target_pairs={{0,1},{1,2},{2,3},{3,0},{4,5},{5,6},{6,7},{7,4},{8,9},{9,10},{10,1... | collective-permute-start | bytes 786440 | tf_op jit(solution)/shard_map/ppermute | solution.py:63
  208.6 18.2 %collective-permute-start.63 = (bf16[512,512]{0,1:T(8,128)(2,1)S(1)}, bf16[512,512]{0,1:T(8,128)(2,1)S(1)}, u32[]{:S(2)}, u32[]{:S(2)}) collective-permute-start(bf16[512,512]{0,1:T(8,128)(2,1)S(1)} %select_select_fusion), channel_id=1, source_target_pairs={{3,2},{2,1},{1,0},{4,5},{5,6},{6,7},{11,10},{10,9},{9,8},{12,13},{... | collective-permute-start | bytes 1572872 | tf_op jit(solution)/shard_map/ppermute | solution.py:260
  210.1 15.3 %collective-permute-start.40 = (bf16[512,512]{0,1:T(8,128)(2,1)S(1)}, bf16[512,512]{0,1:T(8,128)(2,1)S(1)}, u32[]{:S(2)}, u32[]{:S(2)}) collective-permute-start(bf16[512,512]{0,1:T(8,128)(2,1)S(1)} %select_select_fusion.1), channel_id=1, source_target_pairs={{3,2},{2,1},{1,0},{4,5},{5,6},{6,7},{11,10},{10,9},{9,8},{12,13},{... | collective-permute-start | bytes 1572872 | tf_op jit(solution)/shard_map/ppermute | solution.py:260
  227.1 15.1 %collective-permute-start.64 = (bf16[512,512]{0,1:T(8,128)(2,1)S(1)}, bf16[512,512]{0,1:T(8,128)(2,1)S(1)}, u32[]{:S(2)}, u32[]{:S(2)}) collective-permute-start(bf16[512,512]{0,1:T(8,128)(2,1)S(1)} %add_convert_fusion.3), channel_id=1, source_target_pairs={{3,2},{2,1},{1,0},{4,5},{5,6},{6,7},{11,10},{10,9},{9,8},{12,13},{... | collective-permute-start | bytes 1572872 | tf_op jit(solution)/shard_map/ppermute | solution.py:260
  248.4 15.1 %collective-permute-start.43 = (bf16[512,512]{0,1:T(8,128)(2,1)S(1)}, bf16[512,512]{0,1:T(8,128)(2,1)S(1)}, u32[]{:S(2)}, u32[]{:S(2)}) collective-permute-start(bf16[512,512]{0,1:T(8,128)(2,1)S(1)} %get-tuple-element.145), channel_id=1, source_target_pairs={{3,2},{2,1},{1,0},{4,5},{5,6},{6,7},{11,10},{10,9},{9,8},{12,13},{... | collective-permute-start | bytes 1572872 | tf_op jit(solution)/shard_map/ppermute | solution.py:260
  256.3 37.5 %collective-permute-start.72 = (bf16[512,256]{0,1:T(8,128)(2,1)S(1)}, bf16[512,256]{0,1:T(8,128)(2,1)S(1)}, u32[]{:S(2)}, u32[]{:S(2)}) collective-permute-start(bf16[512,256]{0,1:T(8,128)(2,1)S(1)} %get-tuple-element.183), channel_id=1, source_target_pairs={{2,3},{1,2},{0,1},{5,4},{6,5},{7,6},{10,11},{9,10},{8,9},{13,12},{... | collective-permute-start | bytes 786440 | tf_op jit(solution)/shard_map/ppermute | solution.py:269
  258.8 14.7 %collective-permute-start.66 = (bf16[512,512]{0,1:T(8,128)(2,1)S(1)}, bf16[512,512]{0,1:T(8,128)(2,1)S(1)}, u32[]{:S(2)}, u32[]{:S(2)}) collective-permute-start(bf16[512,512]{0,1:T(8,128)(2,1)S(1)} %get-tuple-element.141), channel_id=1, source_target_pairs={{3,2},{2,1},{1,0},{4,5},{5,6},{6,7},{11,10},{10,9},{9,8},{12,13},{... | collective-permute-start | bytes 1572872 | tf_op jit(solution)/shard_map/ppermute | solution.py:260
  263.9 15.3 %collective-permute-start.44 = (bf16[512,512]{0,1:T(8,128)(2,1)S(1)}, bf16[512,512]{0,1:T(8,128)(2,1)S(1)}, u32[]{:S(2)}, u32[]{:S(2)}) collective-permute-start(bf16[512,512]{0,1:T(8,128)(2,1)S(1)} %get-tuple-element.143), channel_id=1, source_target_pairs={{3,2},{2,1},{1,0},{4,5},{5,6},{6,7},{11,10},{10,9},{9,8},{12,13},{... | collective-permute-start | bytes 1572872 | tf_op jit(solution)/shard_map/ppermute | solution.py:260
  265.4 15.4 %collective-permute-start.56 = (bf16[512,256]{0,1:T(8,128)(2,1)S(1)}, bf16[512,256]{0,1:T(8,128)(2,1)S(1)}, u32[]{:S(2)}, u32[]{:S(2)}) collective-permute-start(bf16[512,256]{0,1:T(8,128)(2,1)S(1)} %get-tuple-element.71), channel_id=1, source_target_pairs={{2,3},{1,2},{0,1},{5,4},{6,5},{7,6},{10,11},{9,10},{8,9},{13,12},{... | collective-permute-start | bytes 786440 | tf_op jit(solution)/shard_map/ppermute | solution.py:269
  279.5 13.9 %collective-permute-start.45 = (bf16[512,512]{0,1:T(8,128)(2,1)S(1)}, bf16[512,512]{0,1:T(8,128)(2,1)S(1)}, u32[]{:S(2)}, u32[]{:S(2)}) collective-permute-start(bf16[512,512]{0,1:T(8,128)(2,1)S(1)} %get-tuple-element.137), channel_id=1, source_target_pairs={{3,2},{2,1},{1,0},{4,5},{5,6},{6,7},{11,10},{10,9},{9,8},{12,13},{... | collective-permute-start | bytes 1572872 | tf_op jit(solution)/shard_map/ppermute | solution.py:260
  281.0 12.7 %collective-permute-start.57 = (bf16[512,256]{0,1:T(8,128)(2,1)S(1)}, bf16[512,256]{0,1:T(8,128)(2,1)S(1)}, u32[]{:S(2)}, u32[]{:S(2)}) collective-permute-start(bf16[512,256]{0,1:T(8,128)(2,1)S(1)} %get-tuple-element.69), channel_id=1, source_target_pairs={{2,3},{1,2},{0,1},{5,4},{6,5},{7,6},{10,11},{9,10},{8,9},{13,12},{... | collective-permute-start | bytes 786440 | tf_op jit(solution)/shard_map/ppermute | solution.py:269
  286.0 14.9 %collective-permute-start.68 = (bf16[512,512]{0,1:T(8,128)(2,1)S(1)}, bf16[512,512]{0,1:T(8,128)(2,1)S(1)}, u32[]{:S(2)}, u32[]{:S(2)}) collective-permute-start(bf16[512,512]{0,1:T(8,128)(2,1)S(1)} %get-tuple-element.135), channel_id=1, source_target_pairs={{3,2},{2,1},{1,0},{4,5},{5,6},{6,7},{11,10},{10,9},{9,8},{12,13},{... | collective-permute-start | bytes 1572872 | tf_op jit(solution)/shard_map/ppermute | solution.py:260
  301.3 16.7 %collective-permute-start.69 = (bf16[512,512]{0,1:T(8,128)(2,1)S(1)}, bf16[512,512]{0,1:T(8,128)(2,1)S(1)}, u32[]{:S(2)}, u32[]{:S(2)}) collective-permute-start(bf16[512,512]{0,1:T(8,128)(2,1)S(1)} %get-tuple-element.131), channel_id=1, source_target_pairs={{3,2},{2,1},{1,0},{4,5},{5,6},{6,7},{11,10},{10,9},{9,8},{12,13},{... | collective-permute-start | bytes 1572872 | tf_op jit(solution)/shard_map/ppermute | solution.py:260
  307.4 20.2 %collective-permute-start.58 = (bf16[512,256]{0,1:T(8,128)(2,1)S(1)}, bf16[512,256]{0,1:T(8,128)(2,1)S(1)}, u32[]{:S(2)}, u32[]{:S(2)}) collective-permute-start(bf16[512,256]{0,1:T(8,128)(2,1)S(1)} %get-tuple-element.63), channel_id=1, source_target_pairs={{2,3},{1,2},{0,1},{5,4},{6,5},{7,6},{10,11},{9,10},{8,9},{13,12},{... | collective-permute-start | bytes 786440 | tf_op jit(solution)/shard_map/ppermute | solution.py:269
  309.3 16.7 %collective-permute-start.46 = (bf16[512,512]{0,1:T(8,128)(2,1)S(1)}, bf16[512,512]{0,1:T(8,128)(2,1)S(1)}, u32[]{:S(2)}, u32[]{:S(2)}) collective-permute-start(bf16[512,512]{0,1:T(8,128)(2,1)S(1)} %get-tuple-element.133), channel_id=1, source_target_pairs={{3,2},{2,1},{1,0},{4,5},{5,6},{6,7},{11,10},{10,9},{9,8},{12,13},{... | collective-permute-start | bytes 1572872 | tf_op jit(solution)/shard_map/ppermute | solution.py:260
  313.3 19.5 %collective-permute-start.75 = (bf16[512,256]{0,1:T(8,128)(2,1)S(1)}, bf16[512,256]{0,1:T(8,128)(2,1)S(1)}, u32[]{:S(2)}, u32[]{:S(2)}) collective-permute-start(bf16[512,256]{0,1:T(8,128)(2,1)S(1)} %get-tuple-element.61), channel_id=1, source_target_pairs={{2,3},{1,2},{0,1},{5,4},{6,5},{7,6},{10,11},{9,10},{8,9},{13,12},{... | collective-permute-start | bytes 786440 | tf_op jit(solution)/shard_map/ppermute | solution.py:269
  318.3 26.5 %collective-permute-start.70 = (bf16[512,512]{0,1:T(8,128)(2,1)S(1)}, bf16[512,512]{0,1:T(8,128)(2,1)S(1)}, u32[]{:S(2)}, u32[]{:S(2)}) collective-permute-start(bf16[512,512]{0,1:T(8,128)(2,1)S(1)} %get-tuple-element.127), channel_id=1, source_target_pairs={{3,2},{2,1},{1,0},{4,5},{5,6},{6,7},{11,10},{10,9},{9,8},{12,13},{... | collective-permute-start | bytes 1572872 | tf_op jit(solution)/shard_map/ppermute | solution.py:260
  326.3 16.5 %collective-permute-start.47 = (bf16[512,512]{0,1:T(8,128)(2,1)S(1)}, bf16[512,512]{0,1:T(8,128)(2,1)S(1)}, u32[]{:S(2)}, u32[]{:S(2)}) collective-permute-start(bf16[512,512]{0,1:T(8,128)(2,1)S(1)} %get-tuple-element.129), channel_id=1, source_target_pairs={{3,2},{2,1},{1,0},{4,5},{5,6},{6,7},{11,10},{10,9},{9,8},{12,13},{... | collective-permute-start | bytes 1572872 | tf_op jit(solution)/shard_map/ppermute | solution.py:260
  328.0 16.4 %collective-permute-start.59 = (bf16[512,256]{0,1:T(8,128)(2,1)S(1)}, bf16[512,256]{0,1:T(8,128)(2,1)S(1)}, u32[]{:S(2)}, u32[]{:S(2)}) collective-permute-start(bf16[512,256]{0,1:T(8,128)(2,1)S(1)} %get-tuple-element.59), channel_id=1, source_target_pairs={{2,3},{1,2},{0,1},{5,4},{6,5},{7,6},{10,11},{9,10},{8,9},{13,12},{... | collective-permute-start | bytes 786440 | tf_op jit(solution)/shard_map/ppermute | solution.py:269
  343.1 14.8 %collective-permute-start.48 = (bf16[512,512]{0,1:T(8,128)(2,1)S(1)}, bf16[512,512]{0,1:T(8,128)(2,1)S(1)}, u32[]{:S(2)}, u32[]{:S(2)}) collective-permute-start(bf16[512,512]{0,1:T(8,128)(2,1)S(1)} %get-tuple-element.125), channel_id=1, source_target_pairs={{3,2},{2,1},{1,0},{4,5},{5,6},{6,7},{11,10},{10,9},{9,8},{12,13},{... | collective-permute-start | bytes 1572872 | tf_op jit(solution)/shard_map/ppermute | solution.py:260
  345.4 19.6 %collective-permute-start.77 = (bf16[512,256]{0,1:T(8,128)(2,1)S(1)}, bf16[512,256]{0,1:T(8,128)(2,1)S(1)}, u32[]{:S(2)}, u32[]{:S(2)}) collective-permute-start(bf16[512,256]{0,1:T(8,128)(2,1)S(1)} %get-tuple-element.53), channel_id=1, source_target_pairs={{2,3},{1,2},{0,1},{5,4},{6,5},{7,6},{10,11},{9,10},{8,9},{13,12},{... | collective-permute-start | bytes 786440 | tf_op jit(solution)/shard_map/ppermute | solution.py:269
  350.3 14.6 %collective-permute-start.71 = (bf16[512,512]{0,1:T(8,128)(2,1)S(1)}, bf16[512,512]{0,1:T(8,128)(2,1)S(1)}, u32[]{:S(2)}, u32[]{:S(2)}) collective-permute-start(bf16[512,512]{0,1:T(8,128)(2,1)S(1)} %get-tuple-element.123), channel_id=1, source_target_pairs={{3,2},{2,1},{1,0},{4,5},{5,6},{6,7},{11,10},{10,9},{9,8},{12,13},{... | collective-permute-start | bytes 1572872 | tf_op jit(solution)/shard_map/ppermute | solution.py:260
  371.7 13.8 %collective-permute-start.79 = (bf16[512,256]{0,1:T(8,128)(2,1)S(1)}, bf16[512,256]{0,1:T(8,128)(2,1)S(1)}, u32[]{:S(2)}, u32[]{:S(2)}) collective-permute-start(bf16[512,256]{0,1:T(8,128)(2,1)S(1)} %get-tuple-element.155), channel_id=1, source_target_pairs={{2,3},{1,2},{0,1},{5,4},{6,5},{7,6},{10,11},{9,10},{8,9},{13,12},{... | collective-permute-start | bytes 786440 | tf_op jit(solution)/shard_map/ppermute | solution.py:269
  376.1 12.7 %collective-permute-start.62 = (bf16[512,256]{0,1:T(8,128)(2,1)S(1)}, bf16[512,256]{0,1:T(8,128)(2,1)S(1)}, u32[]{:S(2)}, u32[]{:S(2)}) collective-permute-start(bf16[512,256]{0,1:T(8,128)(2,1)S(1)} %get-tuple-element.153), channel_id=1, source_target_pairs={{2,3},{1,2},{0,1},{5,4},{6,5},{7,6},{10,11},{9,10},{8,9},{13,12},{... | collective-permute-start | bytes 786440 | tf_op jit(solution)/shard_map/ppermute | solution.py:269
  (77 other events, 705.1 us)

commit v3 on v2

--- a/solution.py
+++ b/solution.py
@@ -8,7 +8,7 @@
 BF = jnp.bfloat16
 F32 = jnp.float32
 WIDTH = 256
-EARLY = 10
+GROUP = 4
 
 
 def rotate(values, positions):
@@ -135,13 +135,12 @@
                 for b in range(self.M)
             ]
             blocks.append(lax.ppermute(payload[r % self.H], ("ctx", "mp"), self.flat(pairs)))
-        arrived = blocks[1]
         b = 1
         while b < self.H:
             swapped = self.bit(b) == 1
             blocks = [jnp.where(swapped, blocks[r ^ b], blocks[r]) for r in range(self.C)]
             b *= 2
-        return blocks, arrived
+        return blocks
 
     def slices_to_rows(self, partial):
         n = partial.shape[0] // self.C
@@ -185,31 +184,36 @@
     return side(1, other), side(0, mine)
 
 
-def head_reduce(grid, send, keep):
+def head_reduce(grid, send, keep, squares):
     d = HEAD_DIM
-    near = keep + grid.swap(send, 1).astype(F32)
+    other = grid.swap(send, 1)
+    squares = squares + grid.swap(squares, 1)
+    near = keep + other.astype(F32)
     half = near.shape[0] // 2
     group_bit = grid.C // 2
     side_bit = grid.far_bits[0]
     first, second = near[:half], near[half:]
-    got = grid.swap(first[:, 3 * d :].astype(BF), group_bit).astype(F32)
-    a = first[:, : 3 * d] + got
+    sq_a, sq_b = squares[:half], squares[half:]
+    got_a = grid.swap(first[:, 3 * d :].astype(BF), group_bit).astype(F32)
     out = jnp.concatenate([second[:, d : 3 * d], second[:, 4 * d :]], axis=1).astype(BF)
-    got = grid.swap(out, side_bit).astype(F32)
-    b0 = second[:, :d] + got[:, :d]
-    bg0 = second[:, 2 * d : 3 * d] + got[:, d : 2 * d]
-    b4 = second[:, 3 * d : 4 * d] + got[:, 2 * d : 3 * d]
-    bg1 = second[:, 5 * d :] + got[:, 3 * d :]
-    got = grid.swap(a[:, d:].astype(BF), side_bit).astype(F32)
-    query_a = a[:, :d] + got[:, :d]
-    own_a = a[:, 2 * d :] + got[:, d:]
-    got = grid.swap(jnp.concatenate([b4, bg1], axis=1).astype(BF), group_bit).astype(F32)
-    query_b = b0 + got[:, :d]
-    own_b = bg0 + got[:, d:]
-    return jnp.concatenate([query_a, query_b], axis=0), jnp.concatenate([own_a, own_b], axis=0)
-
-
-def feed_forward(grid, normed, scale, gate_weight, up_weight, down_weight):
+    got_b = grid.swap(out, side_bit).astype(F32)
+    sq_a = sq_a + grid.swap(sq_a, group_bit)
+    sq_b = sq_b + grid.swap(sq_b, side_bit)
+    a = first[:, : 3 * d] + got_a
+    b0 = second[:, :d] + got_b[:, :d]
+    bg0 = second[:, 2 * d : 3 * d] + got_b[:, d : 2 * d]
+    b4 = second[:, 3 * d : 4 * d] + got_b[:, 2 * d : 3 * d]
+    bg1 = second[:, 5 * d :] + got_b[:, 3 * d :]
+    got_a = grid.swap(a[:, d:].astype(BF), side_bit).astype(F32)
+    got_b = grid.swap(jnp.concatenate([b4, bg1], axis=1).astype(BF), group_bit).astype(F32)
+    sq_a = sq_a + grid.swap(sq_a, side_bit)
+    sq_b = sq_b + grid.swap(sq_b, group_bit)
+    query = jnp.concatenate([a[:, :d] + got_a[:, :d], b0 + got_b[:, :d]], axis=0)
+    own = jnp.concatenate([a[:, 2 * d :] + got_a[:, d:], bg0 + got_b[:, d:]], axis=0)
+    return query, own, jnp.concatenate([sq_a, sq_b])
+
+
+def feed_forward(grid, normed, gate_weight, up_weight, down_weight):
     C, M = grid.C, grid.M
     rows = normed.shape[0]
     hidden_cols = gate_weight.shape[1]
@@ -243,7 +247,6 @@
     hist = [[] for _ in range(streams)]
     hids = [[] for _ in range(streams)]
     waiting = []
-    taken = 0
     total = None
     zero = jnp.zeros((rows, 2 * width), BF)
     tick = normed[:8, :128].astype(F32) * 0.0
@@ -262,7 +265,7 @@
             if 0 <= i < n + M - 2:
                 if i < n:
                     full = came.astype(F32) + part(ks[i]).astype(F32)
-                    g, u = full[:, :width] * scale, full[:, width:] * scale
+                    g, u = full[:, :width], full[:, width:]
                     hids[s].append((jax.nn.silu(g) * u).astype(BF))
                 fresh = hids[s][i] if i < n else jnp.zeros((rows, width), BF)
                 send = fresh if passed[s] is None else jnp.where(place == M - 1, fresh, passed[s])
@@ -270,20 +273,17 @@
                 hist[s].append(passed[s])
             j = i - (M - 2) - 1
             if 0 <= j < n:
-                options = [hist[s][j + M - 2 - p] for p in range(M - 1)] + [hids[s][j]]
-                here = place
-                if taken:
-                    *options, here = lax.optimization_barrier((*options, place))
-                waiting.append((ks[j], lax.select_n(here, *options)))
+                waiting.append(
+                    (ks[j], choose([hist[s][j + M - 2 - p] for p in range(M - 1)] + [hids[s][j]]))
+                )
             tick = tick * 0.5
             tick = lax.optimization_barrier(tick)
             final = t == last and s == streams - 1
-            if (not taken and len(waiting) >= EARLY) or (final and waiting):
+            if len(waiting) >= GROUP or (final and waiting):
                 waiting.sort(key=lambda kv: kv[0])
                 k0, k1 = waiting[0][0], waiting[-1][0] + 1
                 assert k1 - k0 == len(waiting)
                 block = lax.optimization_barrier(jnp.concatenate([b for _, b in waiting], axis=1))
-                taken += len(waiting)
                 waiting.clear()
                 weight = down_weight[k0 * width : k1 * width]
                 if final:
@@ -293,11 +293,10 @@
                     if total is not None:
                         far = far + total[half:]
                         near = near + total[:half]
-                    total = near, far
                 else:
-                    total = jnp.dot(block, weight, preferred_element_type=F32)
-                    total = lax.optimization_barrier(total)
-    return *total, jnp.sum(tick)
+                    piece = jnp.dot(block, weight, preferred_element_type=F32)
+                    total = lax.optimization_barrier(piece if total is None else total + piece)
+    return near, far, tick[0, 0]
 
 
 def body(
@@ -367,24 +366,13 @@
     )
     local_rows = incoming[recv_index]
     fits = q_local == ctx_count and kv_local == 2 and len(grid.far_bits) == 2
-    blocks, arrived = grid.rows_to_slices(local_rows)
-    my_rows, _ = lax.optimization_barrier((local_rows, arrived))
-    raw_share = my_rows.astype(F32)
+    positions = grid.small_gather(kept_pos.astype(F32))
+    local_rows, positions = lax.optimization_barrier((local_rows, positions))
+    pos_all = grid.xor_order(positions, my_index ^ (grid.H * grid.m)).reshape(rows)
+    blocks = grid.rows_to_slices(local_rows)
+    raw_share = local_rows.astype(F32)
     my_router = lax.dynamic_slice(router_weight, (grid.m * feature_cols,), (feature_cols,))
-    sums = grid.mp_sum(
-        jnp.stack(
-            [
-                jnp.sum(raw_share * raw_share, axis=1),
-                jnp.sum(raw_share * my_router.astype(F32)[None, :], axis=1),
-            ]
-        )
-    )
-    router_score = jax.nn.sigmoid(sums[1])
-    inverse = lax.rsqrt(sums[0] / feature_total + 1e-05)
-    shared = grid.small_gather(jnp.stack([inverse, kept_pos.astype(F32)]))
-    shared = grid.xor_order(shared, my_index ^ (grid.H * grid.m))
-    inverse_all = shared[:, 0].reshape(rows)
-    pos_all = shared[:, 1].reshape(rows)
+    square_part = jnp.concatenate([jnp.sum(b.astype(F32) ** 2, axis=1) for b in blocks])
     my_gain = lax.dynamic_slice(norm_gain, (my_index * slice_cols,), (slice_cols,))
     my_gain = my_gain.astype(F32)[None, :]
     scaled = jnp.concatenate([(b.astype(F32) * my_gain).astype(BF) for b in blocks], axis=0)
@@ -402,7 +390,8 @@
         )
         send = jnp.dot(scaled, send_weight, preferred_element_type=F32).astype(BF)
         keep = jnp.dot(scaled, keep_weight, preferred_element_type=F32)
-        query, own = head_reduce(grid, send, keep)
+        query, own, square_sum = head_reduce(grid, send, keep, square_part)
+        inverse_all = lax.rsqrt(square_sum / feature_total + 1e-05)
         query = rotate(query * inverse_all[:, None], pos_all).astype(BF)
         own = own * inverse_all[:, None]
         even = grid.bit(1) == 0
@@ -434,7 +423,8 @@
         stacked = jnp.concatenate([query_weight, key_weight, value_weight], axis=1)
         projected = jnp.dot(scaled, stacked, preferred_element_type=F32)
         mine = lax.psum_scatter(projected, "ctx", scatter_dimension=0, tiled=True)
-        my_inverse = lax.dynamic_slice(inverse_all, (my_index * kept_dev,), (kept_dev,))
+        square_sum = lax.psum_scatter(square_part, "ctx", scatter_dimension=0, tiled=True)
+        my_inverse = lax.rsqrt(square_sum / feature_total + 1e-05)
         my_pos = lax.dynamic_slice(pos_all, (my_index * kept_dev,), (kept_dev,))
         mine = mine * my_inverse[:, None]
         by_head = mine.reshape(kept_dev, q_local + 2 * kv_local, head_dim).transpose(1, 0, 2)
@@ -458,14 +448,21 @@
         partial_cols = jnp.dot(every_head, out_weight, preferred_element_type=F32)
     head_share = jnp.concatenate(grid.slices_to_rows(partial_cols.astype(BF)), axis=1)
     mixed_share = raw_share + head_share
-    square_sum = grid.mp_sum(jnp.sum(mixed_share * mixed_share, axis=1))
-    second_inverse = grid.small_gather(lax.rsqrt(square_sum / feature_total + 1e-05))
-    second_inverse = second_inverse[jnp.array(grid.order)].reshape(rows, 1)
-    second_scaled = (mixed_share * mlp_gain.astype(F32)).astype(BF)
+    sums = grid.mp_sum(
+        jnp.stack(
+            [
+                jnp.sum(mixed_share * mixed_share, axis=1),
+                jnp.sum(raw_share * my_router.astype(F32)[None, :], axis=1),
+            ]
+        )
+    )
+    router_score = jax.nn.sigmoid(sums[1])
+    second_inverse = lax.rsqrt(sums[0] / feature_total + 1e-05)[:, None]
+    second_scaled = (mixed_share * second_inverse * mlp_gain.astype(F32)).astype(BF)
     mid = feature_cols // 2
     every_scaled = grid.gather((second_scaled[:, :mid], second_scaled[:, mid:]))
     near, far, tick = feed_forward(
-        grid, every_scaled, second_inverse, gate_weight, up_weight, down_weight
+        grid, every_scaled, gate_weight, up_weight, down_weight
     )
     mlp_share = grid.scatter_sum(near, far)
     update = (router_score[:, None] * (head_share + mlp_share) + tick).astype(BF)

time: 446 us -> 437 us (0.980)
  starting transfers between devices: 162 us -> 182 us
  waiting for transfers between devices: 162 us -> 150 us
  matrix products: 63.9 us -> 53.7 us
    ppermute x18, waiting for transfers between devices: 67.7 us -> 55.3 us  [feed_forward(): got[s] = lax.ppermute(send, ('ctx', 'mp'), inward)]
    ppermute x34 -> x36, starting transfers between devices: 35.1 us -> 45.8 us  [swap(): return lax.ppermute(x, 'ctx', [(i, i ^ b) for i in range(self.C)])]
    ppermute x18, starting transfers between devices: 61.3 us -> 71.9 us  [feed_forward(): passed[s] = lax.ppermute(send, ('ctx', 'mp'), outward)]
    ppermute x34 -> x36, waiting for transfers between devices: 55.2 us -> 63.8 us  [swap(): return lax.ppermute(x, 'ctx', [(i, i ^ b) for i in range(self.C)])]
    ppermute x9 -> x6, waiting for transfers between devices: 26.1 us -> 17.6 us  [rotate_mp(): lax.ppermute(block_for(s), 'mp', [(i, (i + s) % self.M) for i in range(se...]
    ppermute x8, waiting for transfers between devices: 0.02 us -> 7.33 us  [rows_to_slices(): lax.ppermute(payload[r % self.H], ('ctx', 'mp'), self.flat(pairs))]
    ppermute x18, waiting for transfers between devices: 11.8 us -> 6.06 us  [feed_forward(): passed[s] = lax.ppermute(send, ('ctx', 'mp'), outward)]
    ppermute x9 -> x6, starting transfers between devices: 16.6 us -> 16.5 us  [rotate_mp(): lax.ppermute(block_for(s), 'mp', [(i, (i + s) % self.M) for i in range(se...]
  transfers between devices with their start and end apart: 88 -> 87, of which waited for: 48 -> 56; matrix products, arithmetic and copies ran while one was open for 9% -> 7% of each run, Pallas kernels for 0% -> 0%
where the time goes in v3:
time: 437 us; the launch traced here: 432 us
  starting transfers between devices  182 us (42%)
  waiting for transfers between devices  150 us (34%)
  matrix products  53.7 us (12%)
  other arithmetic  21.5 us (5%)
  blocking collectives  12.1 us (3%)
  local copies, waits for them, and re-layouts  10.6 us (2%)
    ppermute x18, starting transfers between devices, feed_forward(): passed[s] = lax.ppermute(send, ('ctx', 'mp'), outward)  71.9 us
    ppermute x36, waiting for transfers between devices, swap(): return lax.ppermute(x, 'ctx', [(i, i ^ b) for i in range(self.C)])  63.8 us
    ppermute x18, waiting for transfers between devices, feed_forward(): got[s] = lax.ppermute(send, ('ctx', 'mp'), inward)  55.3 us
    ppermute x36, starting transfers between devices, swap(): return lax.ppermute(x, 'ctx', [(i, i ^ b) for i in range(self.C)])  45.8 us
    ppermute x18, starting transfers between devices, feed_forward(): got[s] = lax.ppermute(send, ('ctx', 'mp'), inward)  23.4 us
    ppermute x8, starting transfers between devices, rows_to_slices(): lax.ppermute(payload[r % self.H], ('ctx', 'mp'), self.flat(pairs))  20.7 us
    ppermute x6, waiting for transfers between devices, rotate_mp(): lax.ppermute(block_for(s), 'mp', [(i, (i + s) % self.M) for i in range(se...  17.6 us
    dot_general x14, matrix products, part(): g = jnp.dot(normed, gate_weight[:, lo:hi], preferred_element_type=F32)  17.5 us
  transfers between devices with their start and end apart: 87, of which 56 were waited for; matrix products, arithmetic and copies ran while one was open for 7% of the time, Pallas kernels for 0%

profile of v3, /device:TPU:0, one launch (start us, length us, event | category | flops | bytes accessed | tf_op | source)
XLA Modules:
  0.0 432.3 jit_solution(4409079728258598755)
XLA Ops:
  9.5 3.5 all-to-all-start
  34.7 5.6 %collective-permute-done.10 = bf16[64,1024]{1,0:T(8,128)(2,1)S(1)} collective-permute-done((bf16[64,1024]{1,0:T(8,128)(2,1)S(1)}, bf16[64,1024]{1,0:T(8,128)(2,1)S(1)}, u32[]{:S(2)}, u32[]{:S(2)}) %collective-permute-start.10) | collective-permute-done | bytes 131104 | tf_op jit(solution)/shard_map/ppermute | solution.py:137
  40.3 12.4 %collective-permute-start.6 = (bf16[64,1024]{1,0:T(8,128)(2,1)S(1)}, bf16[64,1024]{1,0:T(8,128)(2,1)S(1)}, u32[]{:S(2)}, u32[]{:S(2)}) collective-permute-start(bf16[64,1024]{1,0:T(8,128)(2,1)S(1)} %get-tuple-element.143), channel_id=1, source_target_pairs={{0,1},{1,9},{2,17},{3,25},{4,5},{5,13},{6,21},{7,29},{8,0},{9,8},{... | collective-permute-start | bytes 393224 | tf_op jit(solution)/shard_map/ppermute | solution.py:137
  58.1 15.9 %collective-permute-start.17 = (f32[256]{0:T(256)S(1)}, f32[256]{0:T(256)S(1)}, u32[]{:S(2)}, u32[]{:S(2)}) collective-permute-start(f32[256]{0:T(256)S(1)} %get-tuple-element.155), channel_id=1, source_target_pairs={{0,16},{4,20},{8,24},{12,28},{16,0},{20,4},{24,8},{28,12},{1,17},{... | collective-permute-start | bytes 3080 | tf_op jit(solution)/shard_map/ppermute | solution.py:56
  86.2 3.5 collective-permute-done.12
  125.1 7.4 %collective-permute-done.31 = bf16[64,1024]{1,0:T(8,128)(2,1)S(1)} collective-permute-done((bf16[64,1024]{1,0:T(8,128)(2,1)S(1)}, bf16[64,1024]{1,0:T(8,128)(2,1)S(1)}, u32[]{:S(2)}, u32[]{:S(2)}) %collective-permute-start.31) | collective-permute-done | bytes 131104 | tf_op jit(solution)/shard_map/ppermute | solution.py:56
  132.7 4.4 %collective-permute-start.34 = (bf16[2,64,1024]{2,1,0:T(8,128)(2,1)S(1)}, bf16[2,64,1024]{2,1,0:T(8,128)(2,1)S(1)}, u32[]{:S(2)}, u32[]{:S(2)}) collective-permute-start(bf16[2,64,1024]{2,1,0:T(8,128)(2,1)S(1)} %get-tuple-element.77), channel_id=1, source_target_pairs={{0,1},{1,2},{2,3},{3,0},{4,5},{5,6},{6,7},{7,4},{8,9},{9,10},{10,1... | collective-permute-start | bytes 786440 | tf_op jit(solution)/shard_map/ppermute | solution.py:63
  143.8 10.6 %collective-permute-done.35 = bf16[2,64,1024]{2,1,0:T(8,128)(2,1)S(1)} collective-permute-done((bf16[2,64,1024]{2,1,0:T(8,128)(2,1)S(1)}, bf16[2,64,1024]{2,1,0:T(8,128)(2,1)S(1)}, u32[]{:S(2)}, u32[]{:S(2)}) %collective-permute-start.35) | collective-permute-done | bytes 262176 | tf_op jit(solution)/shard_map/ppermute | solution.py:63
  154.9 6.1 %collective-permute-start.37 = (f32[2,64]{1,0:T(2,128)S(1)}, f32[2,64]{1,0:T(2,128)S(1)}, u32[]{:S(2)}, u32[]{:S(2)}) collective-permute-start(f32[2,64]{1,0:T(2,128)S(1)} %pad_maximum_fusion.30), channel_id=1, source_target_pairs={{0,1},{1,2},{2,3},{3,0},{4,5},{5,6},{6,7},{7,4},{8,9},{9,10},{10,1... | collective-permute-start | bytes 1544 | tf_op jit(solution)/shard_map/ppermute | solution.py:63
  219.4 6.8 %collective-permute-done.45 = bf16[512,512]{0,1:T(8,128)(2,1)S(1)} collective-permute-done((bf16[512,512]{0,1:T(8,128)(2,1)S(1)}, bf16[512,512]{0,1:T(8,128)(2,1)S(1)}, u32[]{:S(2)}, u32[]{:S(2)}) %collective-permute-start.45) | collective-permute-done | bytes 524320 | tf_op jit(solution)/shard_map/ppermute | solution.py:263
  227.8 4.1 collective-permute-done.63
  239.2 4.0 collective-permute-done.64
  250.8 4.6 %collective-permute-start.54 = (bf16[512,256]{0,1:T(8,128)(2,1)S(1)}, bf16[512,256]{0,1:T(8,128)(2,1)S(1)}, u32[]{:S(2)}, u32[]{:S(2)}) collective-permute-start(bf16[512,256]{0,1:T(8,128)(2,1)S(1)} %fusion.83), channel_id=1, source_target_pairs={{2,3},{1,2},{0,1},{5,4},{6,5},{7,6},{10,11},{9,10},{8,9},{13,12},{... | collective-permute-start | bytes 786440 | tf_op jit(solution)/shard_map/ppermute | solution.py:272
  257.2 4.6 %collective-permute-start.72 = (bf16[512,256]{0,1:T(8,128)(2,1)S(1)}, bf16[512,256]{0,1:T(8,128)(2,1)S(1)}, u32[]{:S(2)}, u32[]{:S(2)}) collective-permute-start(bf16[512,256]{0,1:T(8,128)(2,1)S(1)} %fusion.76), channel_id=1, source_target_pairs={{2,3},{1,2},{0,1},{5,4},{6,5},{7,6},{10,11},{9,10},{8,9},{13,12},{... | collective-permute-start | bytes 786440 | tf_op jit(solution)/shard_map/ppermute | solution.py:272
  261.8 3.9 collective-permute-done.48
  267.8 4.6 %collective-permute-start.55 = (bf16[512,256]{0,1:T(8,128)(2,1)S(1)}, bf16[512,256]{0,1:T(8,128)(2,1)S(1)}, u32[]{:S(2)}, u32[]{:S(2)}) collective-permute-start(bf16[512,256]{0,1:T(8,128)(2,1)S(1)} %get-tuple-element.35), channel_id=1, source_target_pairs={{2,3},{1,2},{0,1},{5,4},{6,5},{7,6},{10,11},{9,10},{8,9},{13,12},{... | collective-permute-start | bytes 786440 | tf_op jit(solution)/shard_map/ppermute | solution.py:272
  276.3 4.6 %collective-permute-start.73 = (bf16[512,256]{0,1:T(8,128)(2,1)S(1)}, bf16[512,256]{0,1:T(8,128)(2,1)S(1)}, u32[]{:S(2)}, u32[]{:S(2)}) collective-permute-start(bf16[512,256]{0,1:T(8,128)(2,1)S(1)} %get-tuple-element.41), channel_id=1, source_target_pairs={{2,3},{1,2},{0,1},{5,4},{6,5},{7,6},{10,11},{9,10},{8,9},{13,12},{... | collective-permute-start | bytes 786440 | tf_op jit(solution)/shard_map/ppermute | solution.py:272
  284.8 4.6 %collective-permute-start.56 = (bf16[512,256]{0,1:T(8,128)(2,1)S(1)}, bf16[512,256]{0,1:T(8,128)(2,1)S(1)}, u32[]{:S(2)}, u32[]{:S(2)}) collective-permute-start(bf16[512,256]{0,1:T(8,128)(2,1)S(1)} %get-tuple-element.33), channel_id=1, source_target_pairs={{2,3},{1,2},{0,1},{5,4},{6,5},{7,6},{10,11},{9,10},{8,9},{13,12},{... | collective-permute-start | bytes 786440 | tf_op jit(solution)/shard_map/ppermute | solution.py:272
  293.2 4.6 %collective-permute-start.74 = (bf16[512,256]{0,1:T(8,128)(2,1)S(1)}, bf16[512,256]{0,1:T(8,128)(2,1)S(1)}, u32[]{:S(2)}, u32[]{:S(2)}) collective-permute-start(bf16[512,256]{0,1:T(8,128)(2,1)S(1)} %get-tuple-element.39), channel_id=1, source_target_pairs={{2,3},{1,2},{0,1},{5,4},{6,5},{7,6},{10,11},{9,10},{8,9},{13,12},{... | collective-permute-start | bytes 786440 | tf_op jit(solution)/shard_map/ppermute | solution.py:272
  301.6 4.6 %collective-permute-start.57 = (bf16[512,256]{0,1:T(8,128)(2,1)S(1)}, bf16[512,256]{0,1:T(8,128)(2,1)S(1)}, u32[]{:S(2)}, u32[]{:S(2)}) collective-permute-start(bf16[512,256]{0,1:T(8,128)(2,1)S(1)} %get-tuple-element.31), channel_id=1, source_target_pairs={{2,3},{1,2},{0,1},{5,4},{6,5},{7,6},{10,11},{9,10},{8,9},{13,12},{... | collective-permute-start | bytes 786440 | tf_op jit(solution)/shard_map/ppermute | solution.py:272
  310.0 4.6 %collective-permute-start.75 = (bf16[512,256]{0,1:T(8,128)(2,1)S(1)}, bf16[512,256]{0,1:T(8,128)(2,1)S(1)}, u32[]{:S(2)}, u32[]{:S(2)}) collective-permute-start(bf16[512,256]{0,1:T(8,128)(2,1)S(1)} %get-tuple-element.37), channel_id=1, source_target_pairs={{2,3},{1,2},{0,1},{5,4},{6,5},{7,6},{10,11},{9,10},{8,9},{13,12},{... | collective-permute-start | bytes 786440 | tf_op jit(solution)/shard_map/ppermute | solution.py:272
  318.4 4.6 %collective-permute-start.58 = (bf16[512,256]{0,1:T(8,128)(2,1)S(1)}, bf16[512,256]{0,1:T(8,128)(2,1)S(1)}, u32[]{:S(2)}, u32[]{:S(2)}) collective-permute-start(bf16[512,256]{0,1:T(8,128)(2,1)S(1)} %get-tuple-element.25), channel_id=1, source_target_pairs={{2,3},{1,2},{0,1},{5,4},{6,5},{7,6},{10,11},{9,10},{8,9},{13,12},{... | collective-permute-start | bytes 786440 | tf_op jit(solution)/shard_map/ppermute | solution.py:272
  326.8 4.6 %collective-permute-start.76 = (bf16[512,256]{0,1:T(8,128)(2,1)S(1)}, bf16[512,256]{0,1:T(8,128)(2,1)S(1)}, u32[]{:S(2)}, u32[]{:S(2)}) collective-permute-start(bf16[512,256]{0,1:T(8,128)(2,1)S(1)} %get-tuple-element.29), channel_id=1, source_target_pairs={{2,3},{1,2},{0,1},{5,4},{6,5},{7,6},{10,11},{9,10},{8,9},{13,12},{... | collective-permute-start | bytes 786440 | tf_op jit(solution)/shard_map/ppermute | solution.py:272
  335.2 4.6 %collective-permute-start.59 = (bf16[512,256]{0,1:T(8,128)(2,1)S(1)}, bf16[512,256]{0,1:T(8,128)(2,1)S(1)}, u32[]{:S(2)}, u32[]{:S(2)}) collective-permute-start(bf16[512,256]{0,1:T(8,128)(2,1)S(1)} %get-tuple-element.23), channel_id=1, source_target_pairs={{2,3},{1,2},{0,1},{5,4},{6,5},{7,6},{10,11},{9,10},{8,9},{13,12},{... | collective-permute-start | bytes 786440 | tf_op jit(solution)/shard_map/ppermute | solution.py:272
  343.7 4.8 %collective-permute-start.77 = (bf16[512,256]{0,1:T(8,128)(2,1)S(1)}, bf16[512,256]{0,1:T(8,128)(2,1)S(1)}, u32[]{:S(2)}, u32[]{:S(2)}) collective-permute-start(bf16[512,256]{0,1:T(8,128)(2,1)S(1)} %get-tuple-element.27), channel_id=1, source_target_pairs={{2,3},{1,2},{0,1},{5,4},{6,5},{7,6},{10,11},{9,10},{8,9},{13,12},{... | collective-permute-start | bytes 786440 | tf_op jit(solution)/shard_map/ppermute | solution.py:272
  353.2 8.7 %collective-permute-done.71 = bf16[512,512]{0,1:T(8,128)(2,1)S(1)} collective-permute-done((bf16[512,512]{0,1:T(8,128)(2,1)S(1)}, bf16[512,512]{0,1:T(8,128)(2,1)S(1)}, u32[]{:S(2)}, u32[]{:S(2)}) %collective-permute-start.71) | collective-permute-done | bytes 524320 | tf_op jit(solution)/shard_map/ppermute | solution.py:263
  368.0 4.4 %collective-permute-start.79 = (bf16[512,256]{0,1:T(8,128)(2,1)S(1)}, bf16[512,256]{0,1:T(8,128)(2,1)S(1)}, u32[]{:S(2)}, u32[]{:S(2)}) collective-permute-start(bf16[512,256]{0,1:T(8,128)(2,1)S(1)} %broadcast_select_fusion.3), channel_id=1, source_target_pairs={{2,3},{1,2},{0,1},{5,4},{6,5},{7,6},{10,11},{9,10},{8,9},{13,12},{... | collective-permute-start | bytes 786440 | tf_op jit(solution)/shard_map/ppermute | solution.py:272
  376.3 4.6 %collective-permute-start.80 = (bf16[512,256]{0,1:T(8,128)(2,1)S(1)}, bf16[512,256]{0,1:T(8,128)(2,1)S(1)}, u32[]{:S(2)}, u32[]{:S(2)}) collective-permute-start(bf16[512,256]{0,1:T(8,128)(2,1)S(1)} %broadcast_select_fusion.2), channel_id=1, source_target_pairs={{2,3},{1,2},{0,1},{5,4},{6,5},{7,6},{10,11},{9,10},{8,9},{13,12},{... | collective-permute-start | bytes 786440 | tf_op jit(solution)/shard_map/ppermute | solution.py:272
  399.6 6.7 %collective-permute-done.82 = bf16[2,64,1024]{2,1,0:T(8,128)(2,1)S(1)} collective-permute-done((bf16[2,64,1024]{2,1,0:T(8,128)(2,1)S(1)}, bf16[2,64,1024]{2,1,0:T(8,128)(2,1)S(1)}, u32[]{:S(2)}, u32[]{:S(2)}) %collective-permute-start.82) | collective-permute-done | bytes 262176 | tf_op jit(solution)/shard_map/ppermute | solution.py:56
  407.1 4.3 collective-permute-done.83
  413.0 3.5 collective-permute-done.85
  417.7 12.1 %all_to_all.10 = bf16[8,12,2048]{2,1,0:T(8,128)(2,1)S(1)} all-to-all(bf16[8,12,2048]{2,1,0:T(8,128)(2,1)S(1)} %reshape.138), channel_id=1, replica_groups=mesh['ctx'=8,'mp'=4] {'ctx'}, dimensions={0} | all-to-all | bytes 786432 | tf_op jit(solution)/shard_map/all_to_all | solution.py:475
  (414 shorter events, 242.2 us)
Async XLA Ops:
  0.7 20.7 %collective-permute-start = (f32[1,64]{1,0:T(1,128)S(1)}, f32[1,64]{1,0:T(1,128)S(1)}, u32[]{:S(2)}, u32[]{:S(2)}) collective-permute-start(f32[1,64]{1,0:T(1,128)S(1)} %get-tuple-element.162), channel_id=1, source_target_pairs={{0,8},{4,12},{8,0},{12,4},{16,24},{20,28},{24,16},{28,20},{1,9},{5... | collective-permute-start | bytes 776 | tf_op jit(solution)/shard_map/ppermute | solution.py:56
  9.5 16.9 %all-to-all-start = ((bf16[8,12,2048]{2,1,0:T(8,128)(2,1)}), bf16[8,12,2048]{2,1,0:T(8,128)(2,1)S(1)}, u32[]{:S(2)}, u32[]{:S(2)}) async-start(bf16[8,12,2048]{2,1,0:T(8,128)(2,1)} %reshape.129), calls=%async_computation | async-start | bytes 1048576 | tf_op jit(solution)/shard_map/all_to_all | solution.py:355
  27.2 25.5 %collective-permute-start.9 = (bf16[64,1024]{1,0:T(8,128)(2,1)S(1)}, bf16[64,1024]{1,0:T(8,128)(2,1)S(1)}, u32[]{:S(2)}, u32[]{:S(2)}) collective-permute-start(bf16[64,1024]{1,0:T(8,128)(2,1)S(1)} %get-tuple-element.144), channel_id=1, source_target_pairs={{0,7},{1,15},{2,23},{3,31},{4,3},{5,11},{6,19},{7,27},{8,6},{9,14}... | collective-permute-start | bytes 393224 | tf_op jit(solution)/shard_map/ppermute | solution.py:137
  30.7 22.2 %collective-permute-start.7 = (bf16[64,1024]{1,0:T(8,128)(2,1)S(1)}, bf16[64,1024]{1,0:T(8,128)(2,1)S(1)}, u32[]{:S(2)}, u32[]{:S(2)}) collective-permute-start(bf16[64,1024]{1,0:T(8,128)(2,1)S(1)} %get-tuple-element.144), channel_id=1, source_target_pairs={{0,6},{1,14},{2,22},{3,30},{4,2},{5,10},{6,18},{7,26},{8,7},{9,15}... | collective-permute-start | bytes 393224 | tf_op jit(solution)/shard_map/ppermute | solution.py:137
  33.6 20.1 %collective-permute-start.8 = (bf16[64,1024]{1,0:T(8,128)(2,1)S(1)}, bf16[64,1024]{1,0:T(8,128)(2,1)S(1)}, u32[]{:S(2)}, u32[]{:S(2)}) collective-permute-start(bf16[64,1024]{1,0:T(8,128)(2,1)S(1)} %get-tuple-element.143), channel_id=1, source_target_pairs={{0,2},{1,10},{2,18},{3,26},{4,6},{5,14},{6,22},{7,30},{8,3},{9,11}... | collective-permute-start | bytes 393224 | tf_op jit(solution)/shard_map/ppermute | solution.py:137
  33.8 20.1 %collective-permute-start.5 = (bf16[64,1024]{1,0:T(8,128)(2,1)S(1)}, bf16[64,1024]{1,0:T(8,128)(2,1)S(1)}, u32[]{:S(2)}, u32[]{:S(2)}) collective-permute-start(bf16[64,1024]{1,0:T(8,128)(2,1)S(1)} %get-tuple-element.144), channel_id=1, source_target_pairs={{0,5},{1,13},{2,21},{3,29},{4,1},{5,9},{6,17},{7,25},{8,4},{9,12},... | collective-permute-start | bytes 393224 | tf_op jit(solution)/shard_map/ppermute | solution.py:137
  57.6 23.6 %collective-permute-start.11 = (bf16[512,768]{1,0:T(8,128)(2,1)S(1)}, bf16[512,768]{1,0:T(8,128)(2,1)S(1)}, u32[]{:S(2)}, u32[]{:S(2)}) collective-permute-start(bf16[512,768]{1,0:T(8,128)(2,1)S(1)} %convolution_convert_fusion.2), channel_id=1, source_target_pairs={{0,4},{4,0},{8,12},{12,8},{16,20},{20,16},{24,28},{28,24},{1,5},{5... | collective-permute-start | bytes 2359304 | tf_op jit(solution)/shard_map/ppermute | solution.py:56
  58.1 17.4 %collective-permute-start.17 = (f32[256]{0:T(256)S(1)}, f32[256]{0:T(256)S(1)}, u32[]{:S(2)}, u32[]{:S(2)}) collective-permute-start(f32[256]{0:T(256)S(1)} %get-tuple-element.155), channel_id=1, source_target_pairs={{0,16},{4,20},{8,24},{12,28},{16,0},{20,4},{24,8},{28,12},{1,17},{... | collective-permute-start | bytes 3080 | tf_op jit(solution)/shard_map/ppermute | solution.py:56
  137.1 17.3 %collective-permute-start.35 = (bf16[2,64,1024]{2,1,0:T(8,128)(2,1)S(1)}, bf16[2,64,1024]{2,1,0:T(8,128)(2,1)S(1)}, u32[]{:S(2)}, u32[]{:S(2)}) collective-permute-start(bf16[2,64,1024]{2,1,0:T(8,128)(2,1)S(1)} %get-tuple-element.79), channel_id=1, source_target_pairs={{0,2},{1,3},{2,0},{3,1},{4,6},{5,7},{6,4},{7,5},{8,10},{9,11},{10,... | collective-permute-start | bytes 786440 | tf_op jit(solution)/shard_map/ppermute | solution.py:63
  137.1 17.3 %collective-permute-start.36 = (bf16[2,64,1024]{2,1,0:T(8,128)(2,1)S(1)}, bf16[2,64,1024]{2,1,0:T(8,128)(2,1)S(1)}, u32[]{:S(2)}, u32[]{:S(2)}) collective-permute-start(bf16[2,64,1024]{2,1,0:T(8,128)(2,1)S(1)} %get-tuple-element.78), channel_id=1, source_target_pairs={{0,3},{1,0},{2,1},{3,2},{4,7},{5,4},{6,5},{7,6},{8,11},{9,8},{10,9... | collective-permute-start | bytes 786440 | tf_op jit(solution)/shard_map/ppermute | solution.py:63
  250.8 16.8 %collective-permute-start.54 = (bf16[512,256]{0,1:T(8,128)(2,1)S(1)}, bf16[512,256]{0,1:T(8,128)(2,1)S(1)}, u32[]{:S(2)}, u32[]{:S(2)}) collective-permute-start(bf16[512,256]{0,1:T(8,128)(2,1)S(1)} %fusion.83), channel_id=1, source_target_pairs={{2,3},{1,2},{0,1},{5,4},{6,5},{7,6},{10,11},{9,10},{8,9},{13,12},{... | collective-permute-start | bytes 786440 | tf_op jit(solution)/shard_map/ppermute | solution.py:272
  255.7 18.7 %collective-permute-start.66 = (bf16[512,512]{0,1:T(8,128)(2,1)S(1)}, bf16[512,512]{0,1:T(8,128)(2,1)S(1)}, u32[]{:S(2)}, u32[]{:S(2)}) collective-permute-start(bf16[512,512]{0,1:T(8,128)(2,1)S(1)} %get-tuple-element.129), channel_id=1, source_target_pairs={{3,2},{2,1},{1,0},{4,5},{5,6},{6,7},{11,10},{10,9},{9,8},{12,13},{... | collective-permute-start | bytes 1572872 | tf_op jit(solution)/shard_map/ppermute | solution.py:263
  257.2 18.9 %collective-permute-start.72 = (bf16[512,256]{0,1:T(8,128)(2,1)S(1)}, bf16[512,256]{0,1:T(8,128)(2,1)S(1)}, u32[]{:S(2)}, u32[]{:S(2)}) collective-permute-start(bf16[512,256]{0,1:T(8,128)(2,1)S(1)} %fusion.76), channel_id=1, source_target_pairs={{2,3},{1,2},{0,1},{5,4},{6,5},{7,6},{10,11},{9,10},{8,9},{13,12},{... | collective-permute-start | bytes 786440 | tf_op jit(solution)/shard_map/ppermute | solution.py:272
  266.1 16.8 %collective-permute-start.49 = (bf16[512,512]{0,1:T(8,128)(2,1)S(1)}, bf16[512,512]{0,1:T(8,128)(2,1)S(1)}, u32[]{:S(2)}, u32[]{:S(2)}) collective-permute-start(bf16[512,512]{0,1:T(8,128)(2,1)S(1)} %get-tuple-element.121), channel_id=1, source_target_pairs={{3,2},{2,1},{1,0},{4,5},{5,6},{6,7},{11,10},{10,9},{9,8},{12,13},{... | collective-permute-start | bytes 1572872 | tf_op jit(solution)/shard_map/ppermute | solution.py:263
  267.8 16.8 %collective-permute-start.55 = (bf16[512,256]{0,1:T(8,128)(2,1)S(1)}, bf16[512,256]{0,1:T(8,128)(2,1)S(1)}, u32[]{:S(2)}, u32[]{:S(2)}) collective-permute-start(bf16[512,256]{0,1:T(8,128)(2,1)S(1)} %get-tuple-element.35), channel_id=1, source_target_pairs={{2,3},{1,2},{0,1},{5,4},{6,5},{7,6},{10,11},{9,10},{8,9},{13,12},{... | collective-permute-start | bytes 786440 | tf_op jit(solution)/shard_map/ppermute | solution.py:272
  274.8 16.5 %collective-permute-start.67 = (bf16[512,512]{0,1:T(8,128)(2,1)S(1)}, bf16[512,512]{0,1:T(8,128)(2,1)S(1)}, u32[]{:S(2)}, u32[]{:S(2)}) collective-permute-start(bf16[512,512]{0,1:T(8,128)(2,1)S(1)} %get-tuple-element.127), channel_id=1, source_target_pairs={{3,2},{2,1},{1,0},{4,5},{5,6},{6,7},{11,10},{10,9},{9,8},{12,13},{... | collective-permute-start | bytes 1572872 | tf_op jit(solution)/shard_map/ppermute | solution.py:263
  276.3 16.6 %collective-permute-start.73 = (bf16[512,256]{0,1:T(8,128)(2,1)S(1)}, bf16[512,256]{0,1:T(8,128)(2,1)S(1)}, u32[]{:S(2)}, u32[]{:S(2)}) collective-permute-start(bf16[512,256]{0,1:T(8,128)(2,1)S(1)} %get-tuple-element.41), channel_id=1, source_target_pairs={{2,3},{1,2},{0,1},{5,4},{6,5},{7,6},{10,11},{9,10},{8,9},{13,12},{... | collective-permute-start | bytes 786440 | tf_op jit(solution)/shard_map/ppermute | solution.py:272
  283.2 16.5 %collective-permute-start.50 = (bf16[512,512]{0,1:T(8,128)(2,1)S(1)}, bf16[512,512]{0,1:T(8,128)(2,1)S(1)}, u32[]{:S(2)}, u32[]{:S(2)}) collective-permute-start(bf16[512,512]{0,1:T(8,128)(2,1)S(1)} %get-tuple-element.119), channel_id=1, source_target_pairs={{3,2},{2,1},{1,0},{4,5},{5,6},{6,7},{11,10},{10,9},{9,8},{12,13},{... | collective-permute-start | bytes 1572872 | tf_op jit(solution)/shard_map/ppermute | solution.py:263
  284.8 16.6 %collective-permute-start.56 = (bf16[512,256]{0,1:T(8,128)(2,1)S(1)}, bf16[512,256]{0,1:T(8,128)(2,1)S(1)}, u32[]{:S(2)}, u32[]{:S(2)}) collective-permute-start(bf16[512,256]{0,1:T(8,128)(2,1)S(1)} %get-tuple-element.33), channel_id=1, source_target_pairs={{2,3},{1,2},{0,1},{5,4},{6,5},{7,6},{10,11},{9,10},{8,9},{13,12},{... | collective-permute-start | bytes 786440 | tf_op jit(solution)/shard_map/ppermute | solution.py:272
  291.7 16.5 %collective-permute-start.68 = (bf16[512,512]{0,1:T(8,128)(2,1)S(1)}, bf16[512,512]{0,1:T(8,128)(2,1)S(1)}, u32[]{:S(2)}, u32[]{:S(2)}) collective-permute-start(bf16[512,512]{0,1:T(8,128)(2,1)S(1)} %get-tuple-element.125), channel_id=1, source_target_pairs={{3,2},{2,1},{1,0},{4,5},{5,6},{6,7},{11,10},{10,9},{9,8},{12,13},{... | collective-permute-start | bytes 1572872 | tf_op jit(solution)/shard_map/ppermute | solution.py:263
  293.2 16.7 %collective-permute-start.74 = (bf16[512,256]{0,1:T(8,128)(2,1)S(1)}, bf16[512,256]{0,1:T(8,128)(2,1)S(1)}, u32[]{:S(2)}, u32[]{:S(2)}) collective-permute-start(bf16[512,256]{0,1:T(8,128)(2,1)S(1)} %get-tuple-element.39), channel_id=1, source_target_pairs={{2,3},{1,2},{0,1},{5,4},{6,5},{7,6},{10,11},{9,10},{8,9},{13,12},{... | collective-permute-start | bytes 786440 | tf_op jit(solution)/shard_map/ppermute | solution.py:272
  300.1 16.5 %collective-permute-start.51 = (bf16[512,512]{0,1:T(8,128)(2,1)S(1)}, bf16[512,512]{0,1:T(8,128)(2,1)S(1)}, u32[]{:S(2)}, u32[]{:S(2)}) collective-permute-start(bf16[512,512]{0,1:T(8,128)(2,1)S(1)} %get-tuple-element.113), channel_id=1, source_target_pairs={{3,2},{2,1},{1,0},{4,5},{5,6},{6,7},{11,10},{10,9},{9,8},{12,13},{... | collective-permute-start | bytes 1572872 | tf_op jit(solution)/shard_map/ppermute | solution.py:263
  301.6 16.6 %collective-permute-start.57 = (bf16[512,256]{0,1:T(8,128)(2,1)S(1)}, bf16[512,256]{0,1:T(8,128)(2,1)S(1)}, u32[]{:S(2)}, u32[]{:S(2)}) collective-permute-start(bf16[512,256]{0,1:T(8,128)(2,1)S(1)} %get-tuple-element.31), channel_id=1, source_target_pairs={{2,3},{1,2},{0,1},{5,4},{6,5},{7,6},{10,11},{9,10},{8,9},{13,12},{... | collective-permute-start | bytes 786440 | tf_op jit(solution)/shard_map/ppermute | solution.py:272
  308.5 16.5 %collective-permute-start.69 = (bf16[512,512]{0,1:T(8,128)(2,1)S(1)}, bf16[512,512]{0,1:T(8,128)(2,1)S(1)}, u32[]{:S(2)}, u32[]{:S(2)}) collective-permute-start(bf16[512,512]{0,1:T(8,128)(2,1)S(1)} %get-tuple-element.117), channel_id=1, source_target_pairs={{3,2},{2,1},{1,0},{4,5},{5,6},{6,7},{11,10},{10,9},{9,8},{12,13},{... | collective-permute-start | bytes 1572872 | tf_op jit(solution)/shard_map/ppermute | solution.py:263
  310.0 16.6 %collective-permute-start.75 = (bf16[512,256]{0,1:T(8,128)(2,1)S(1)}, bf16[512,256]{0,1:T(8,128)(2,1)S(1)}, u32[]{:S(2)}, u32[]{:S(2)}) collective-permute-start(bf16[512,256]{0,1:T(8,128)(2,1)S(1)} %get-tuple-element.37), channel_id=1, source_target_pairs={{2,3},{1,2},{0,1},{5,4},{6,5},{7,6},{10,11},{9,10},{8,9},{13,12},{... | collective-permute-start | bytes 786440 | tf_op jit(solution)/shard_map/ppermute | solution.py:272
  316.9 16.5 %collective-permute-start.52 = (bf16[512,512]{0,1:T(8,128)(2,1)S(1)}, bf16[512,512]{0,1:T(8,128)(2,1)S(1)}, u32[]{:S(2)}, u32[]{:S(2)}) collective-permute-start(bf16[512,512]{0,1:T(8,128)(2,1)S(1)} %get-tuple-element.111), channel_id=1, source_target_pairs={{3,2},{2,1},{1,0},{4,5},{5,6},{6,7},{11,10},{10,9},{9,8},{12,13},{... | collective-permute-start | bytes 1572872 | tf_op jit(solution)/shard_map/ppermute | solution.py:263
  318.4 16.6 %collective-permute-start.58 = (bf16[512,256]{0,1:T(8,128)(2,1)S(1)}, bf16[512,256]{0,1:T(8,128)(2,1)S(1)}, u32[]{:S(2)}, u32[]{:S(2)}) collective-permute-start(bf16[512,256]{0,1:T(8,128)(2,1)S(1)} %get-tuple-element.25), channel_id=1, source_target_pairs={{2,3},{1,2},{0,1},{5,4},{6,5},{7,6},{10,11},{9,10},{8,9},{13,12},{... | collective-permute-start | bytes 786440 | tf_op jit(solution)/shard_map/ppermute | solution.py:272
  325.3 16.5 %collective-permute-start.70 = (bf16[512,512]{0,1:T(8,128)(2,1)S(1)}, bf16[512,512]{0,1:T(8,128)(2,1)S(1)}, u32[]{:S(2)}, u32[]{:S(2)}) collective-permute-start(bf16[512,512]{0,1:T(8,128)(2,1)S(1)} %get-tuple-element.115), channel_id=1, source_target_pairs={{3,2},{2,1},{1,0},{4,5},{5,6},{6,7},{11,10},{10,9},{9,8},{12,13},{... | collective-permute-start | bytes 1572872 | tf_op jit(solution)/shard_map/ppermute | solution.py:263
  326.8 16.6 %collective-permute-start.76 = (bf16[512,256]{0,1:T(8,128)(2,1)S(1)}, bf16[512,256]{0,1:T(8,128)(2,1)S(1)}, u32[]{:S(2)}, u32[]{:S(2)}) collective-permute-start(bf16[512,256]{0,1:T(8,128)(2,1)S(1)} %get-tuple-element.29), channel_id=1, source_target_pairs={{2,3},{1,2},{0,1},{5,4},{6,5},{7,6},{10,11},{9,10},{8,9},{13,12},{... | collective-permute-start | bytes 786440 | tf_op jit(solution)/shard_map/ppermute | solution.py:272
  333.7 17.7 %collective-permute-start.53 = (bf16[512,512]{0,1:T(8,128)(2,1)S(1)}, bf16[512,512]{0,1:T(8,128)(2,1)S(1)}, u32[]{:S(2)}, u32[]{:S(2)}) collective-permute-start(bf16[512,512]{0,1:T(8,128)(2,1)S(1)} %get-tuple-element.107), channel_id=1, source_target_pairs={{3,2},{2,1},{1,0},{4,5},{5,6},{6,7},{11,10},{10,9},{9,8},{12,13},{... | collective-permute-start | bytes 1572872 | tf_op jit(solution)/shard_map/ppermute | solution.py:263
  342.1 19.8 %collective-permute-start.71 = (bf16[512,512]{0,1:T(8,128)(2,1)S(1)}, bf16[512,512]{0,1:T(8,128)(2,1)S(1)}, u32[]{:S(2)}, u32[]{:S(2)}) collective-permute-start(bf16[512,512]{0,1:T(8,128)(2,1)S(1)} %get-tuple-element.109), channel_id=1, source_target_pairs={{3,2},{2,1},{1,0},{4,5},{5,6},{6,7},{11,10},{10,9},{9,8},{12,13},{... | collective-permute-start | bytes 1572872 | tf_op jit(solution)/shard_map/ppermute | solution.py:263
  343.7 18.5 %collective-permute-start.77 = (bf16[512,256]{0,1:T(8,128)(2,1)S(1)}, bf16[512,256]{0,1:T(8,128)(2,1)S(1)}, u32[]{:S(2)}, u32[]{:S(2)}) collective-permute-start(bf16[512,256]{0,1:T(8,128)(2,1)S(1)} %get-tuple-element.27), channel_id=1, source_target_pairs={{2,3},{1,2},{0,1},{5,4},{6,5},{7,6},{10,11},{9,10},{8,9},{13,12},{... | collective-permute-start | bytes 786440 | tf_op jit(solution)/shard_map/ppermute | solution.py:272
  (75 other events, 627.4 us)

commit v4 on v3

--- a/solution.py
+++ b/solution.py
@@ -247,10 +247,12 @@
     hist = [[] for _ in range(streams)]
     hids = [[] for _ in range(streams)]
     waiting = []
+    taken = 0
     total = None
     zero = jnp.zeros((rows, 2 * width), BF)
     tick = normed[:8, :128].astype(F32) * 0.0
-    last = max(len(ks) for ks in lists) + 2 * (M - 1) - 1
+    last = max(len(ks) for ks in lists) + 2 * (M - 1) - 2
+    straight = [[] for _ in range(streams)]
     for t in range(last + 1):
         for s in range(streams):
             ks = lists[s]
@@ -262,27 +264,34 @@
                 send = own if came is None else (own.astype(F32) + came.astype(F32)).astype(BF)
                 got[s] = lax.ppermute(send, ("ctx", "mp"), inward)
             i = t - (M - 1)
-            if 0 <= i < n + M - 2:
-                if i < n:
-                    full = came.astype(F32) + part(ks[i]).astype(F32)
-                    g, u = full[:, :width], full[:, width:]
-                    hids[s].append((jax.nn.silu(g) * u).astype(BF))
-                fresh = hids[s][i] if i < n else jnp.zeros((rows, width), BF)
+            if 0 <= i < n:
+                full = came.astype(F32) + part(ks[i]).astype(F32)
+                g, u = full[:, :width], full[:, width:]
+                hids[s].append((jax.nn.silu(g) * u).astype(BF))
+            if 0 <= i < n - 1 + M - 2:
+                fresh = hids[s][i] if i < n - 1 else jnp.zeros((rows, width), BF)
                 send = fresh if passed[s] is None else jnp.where(place == M - 1, fresh, passed[s])
                 passed[s] = lax.ppermute(send, ("ctx", "mp"), outward)
                 hist[s].append(passed[s])
+            if i == n - 1:
+                for d in reversed(range(1, M)):
+                    pairs = grid.flat([(at(a, M - 1), at(a, M - 1 - d)) for a in range(C)])
+                    straight[s].append(lax.ppermute(hids[s][i], ("ctx", "mp"), pairs))
             j = i - (M - 2) - 1
-            if 0 <= j < n:
+            if 0 <= j < n - 1:
                 waiting.append(
                     (ks[j], choose([hist[s][j + M - 2 - p] for p in range(M - 1)] + [hids[s][j]]))
                 )
+            if i == n + M - 3:
+                waiting.append((ks[n - 1], choose(straight[s] + [hids[s][n - 1]])))
             tick = tick * 0.5
             tick = lax.optimization_barrier(tick)
-            final = t == last and s == streams - 1
-            if len(waiting) >= GROUP or (final and waiting):
-                waiting.sort(key=lambda kv: kv[0])
+            final = taken + len(waiting) == count
+            waiting.sort(key=lambda kv: kv[0])
+            run = bool(waiting) and waiting[-1][0] - waiting[0][0] == len(waiting) - 1
+            if waiting and ((len(waiting) >= GROUP and run) or final):
+                taken += len(waiting)
                 k0, k1 = waiting[0][0], waiting[-1][0] + 1
-                assert k1 - k0 == len(waiting)
                 block = lax.optimization_barrier(jnp.concatenate([b for _, b in waiting], axis=1))
                 waiting.clear()
                 weight = down_weight[k0 * width : k1 * width]
@@ -390,6 +399,7 @@
         )
         send = jnp.dot(scaled, send_weight, preferred_element_type=F32).astype(BF)
         keep = jnp.dot(scaled, keep_weight, preferred_element_type=F32)
+        keep = lax.optimization_barrier(keep)
         query, own, square_sum = head_reduce(grid, send, keep, square_part)
         inverse_all = lax.rsqrt(square_sum / feature_total + 1e-05)
         query = rotate(query * inverse_all[:, None], pos_all).astype(BF)
@@ -461,9 +471,7 @@
     second_scaled = (mixed_share * second_inverse * mlp_gain.astype(F32)).astype(BF)
     mid = feature_cols // 2
     every_scaled = grid.gather((second_scaled[:, :mid], second_scaled[:, mid:]))
-    near, far, tick = feed_forward(
-        grid, every_scaled, gate_weight, up_weight, down_weight
-    )
+    near, far, tick = feed_forward(grid, every_scaled, gate_weight, up_weight, down_weight)
     mlp_share = grid.scatter_sum(near, far)
     update = (router_score[:, None] * (head_share + mlp_share) + tick).astype(BF)
     places = (slot_ids_all[:, None] == recv_index[None, :]).astype(BF)
@@ -497,4 +505,5 @@
         P("ctx"),
     )
     out_specs = P("ctx", "mp")
+
     return jax.shard_map(body, mesh=mesh, in_specs=in_specs, out_specs=out_specs, check_vma=False)

time: 437 us -> 436 us (level)
  starting transfers between devices: 182 us -> 151 us
  waiting for transfers between devices: 150 us -> 180 us
    ppermute x18 -> x16, starting transfers between devices: 71.9 us -> 37.8 us  [feed_forward(): passed[s] = lax.ppermute(send, ('ctx', 'mp'), outward)]
    ppermute x18, waiting for transfers between devices: 55.3 us -> 76.2 us  [feed_forward(): got[s] = lax.ppermute(send, ('ctx', 'mp'), inward)]
    ppermute x0 -> x6, starting transfers between devices: none -> 14.3 us  [feed_forward(): straight[s].append(lax.ppermute(hids[s][i], ('ctx', 'mp'), pairs))]
    ppermute x6, starting transfers between devices: 16.5 us -> 7.58 us  [rotate_mp(): lax.ppermute(block_for(s), 'mp', [(i, (i + s) % self.M) for i in range(se...]
    ppermute x6, waiting for transfers between devices: 17.6 us -> 26.2 us  [rotate_mp(): lax.ppermute(block_for(s), 'mp', [(i, (i + s) % self.M) for i in range(se...]
    ppermute x0 -> x6, waiting for transfers between devices: none -> 5.76 us  [feed_forward(): straight[s].append(lax.ppermute(hids[s][i], ('ctx', 'mp'), pairs))]
  transfers between devices with their start and end apart: 87 -> 91, of which waited for: 56 -> 52; matrix products, arithmetic and copies ran while one was open for 7% -> 9% of each run, Pallas kernels for 0% -> 0%
where the time goes in v4:
time: 436 us; the launch traced here: 432 us
  waiting for transfers between devices  180 us (41%)
  starting transfers between devices  151 us (35%)
  matrix products  53.4 us (12%)
  other arithmetic  22.4 us (5%)
  blocking collectives  12.5 us (3%)
  local copies, waits for them, and re-layouts  9.9 us (2%)
    ppermute x18, waiting for transfers between devices, feed_forward(): got[s] = lax.ppermute(send, ('ctx', 'mp'), inward)  76.2 us
    ppermute x36, waiting for transfers between devices, swap(): return lax.ppermute(x, 'ctx', [(i, i ^ b) for i in range(self.C)])  61.4 us
    ppermute x36, starting transfers between devices, swap(): return lax.ppermute(x, 'ctx', [(i, i ^ b) for i in range(self.C)])  43.2 us
    ppermute x16, starting transfers between devices, feed_forward(): passed[s] = lax.ppermute(send, ('ctx', 'mp'), outward)  37.8 us
    ppermute x6, waiting for transfers between devices, rotate_mp(): lax.ppermute(block_for(s), 'mp', [(i, (i + s) % self.M) for i in range(se...  26.2 us
    ppermute x18, starting transfers between devices, feed_forward(): got[s] = lax.ppermute(send, ('ctx', 'mp'), inward)  23.4 us
    ppermute x8, starting transfers between devices, rows_to_slices(): lax.ppermute(payload[r % self.H], ('ctx', 'mp'), self.flat(pairs))  21.4 us
    dot_general x14, matrix products, part(): g = jnp.dot(normed, gate_weight[:, lo:hi], preferred_element_type=F32)  17.5 us
  transfers between devices with their start and end apart: 91, of which 52 were waited for; matrix products, arithmetic and copies ran while one was open for 9% of the time, Pallas kernels for 0%

profile of v4, /device:TPU:0, one launch (start us, length us, event | category | flops | bytes accessed | tf_op | source)
XLA Modules:
  0.0 431.9 jit_solution(17118705633322641273)
XLA Ops:
  33.9 5.4 %collective-permute-start.9 = (bf16[64,1024]{1,0:T(8,128)(2,1)S(1)}, bf16[64,1024]{1,0:T(8,128)(2,1)S(1)}, u32[]{:S(2)}, u32[]{:S(2)}) collective-permute-start(bf16[64,1024]{1,0:T(8,128)(2,1)S(1)} %get-tuple-element.138), channel_id=1, source_target_pairs={{0,7},{1,15},{2,23},{3,31},{4,3},{5,11},{6,19},{7,27},{8,6},{9,14}... | collective-permute-start | bytes 393224 | tf_op jit(solution)/shard_map/ppermute | solution.py:137
  39.4 4.0 collective-permute-done.9
  43.5 8.7 %collective-permute-start.5 = (bf16[64,1024]{1,0:T(8,128)(2,1)S(1)}, bf16[64,1024]{1,0:T(8,128)(2,1)S(1)}, u32[]{:S(2)}, u32[]{:S(2)}) collective-permute-start(bf16[64,1024]{1,0:T(8,128)(2,1)S(1)} %get-tuple-element.138), channel_id=1, source_target_pairs={{0,5},{1,13},{2,21},{3,29},{4,1},{5,9},{6,17},{7,25},{8,4},{9,12},... | collective-permute-start | bytes 393224 | tf_op jit(solution)/shard_map/ppermute | solution.py:137
  58.4 11.0 %collective-permute-start.17 = (f32[256]{0:T(256)S(1)}, f32[256]{0:T(256)S(1)}, u32[]{:S(2)}, u32[]{:S(2)}) collective-permute-start(f32[256]{0:T(256)S(1)} %get-tuple-element.149), channel_id=1, source_target_pairs={{0,16},{4,20},{8,24},{12,28},{16,0},{20,4},{24,8},{28,12},{1,17},{... | collective-permute-start | bytes 3080 | tf_op jit(solution)/shard_map/ppermute | solution.py:56
  116.3 6.5 %collective-permute-done.28 = bf16[64,1024]{1,0:T(8,128)(2,1)S(1)} collective-permute-done((bf16[64,1024]{1,0:T(8,128)(2,1)S(1)}, bf16[64,1024]{1,0:T(8,128)(2,1)S(1)}, u32[]{:S(2)}, u32[]{:S(2)}) %collective-permute-start.28) | collective-permute-done | bytes 131104 | tf_op jit(solution)/shard_map/ppermute | solution.py:56
  122.9 5.3 %collective-permute-done.29 = bf16[64,1024]{1,0:T(8,128)(2,1)S(1)} collective-permute-done((bf16[64,1024]{1,0:T(8,128)(2,1)S(1)}, bf16[64,1024]{1,0:T(8,128)(2,1)S(1)}, u32[]{:S(2)}, u32[]{:S(2)}) %collective-permute-start.29) | collective-permute-done | bytes 131104 | tf_op jit(solution)/shard_map/ppermute | solution.py:56
  134.0 5.6 %collective-permute-done.34 = bf16[2,64,1024]{2,1,0:T(8,128)(2,1)S(1)} collective-permute-done((bf16[2,64,1024]{2,1,0:T(8,128)(2,1)S(1)}, bf16[2,64,1024]{2,1,0:T(8,128)(2,1)S(1)}, u32[]{:S(2)}, u32[]{:S(2)}) %collective-permute-start.34) | collective-permute-done | bytes 262176 | tf_op jit(solution)/shard_map/ppermute | solution.py:63
  139.6 4.5 %collective-permute-done.36 = bf16[2,64,1024]{2,1,0:T(8,128)(2,1)S(1)} collective-permute-done((bf16[2,64,1024]{2,1,0:T(8,128)(2,1)S(1)}, bf16[2,64,1024]{2,1,0:T(8,128)(2,1)S(1)}, u32[]{:S(2)}, u32[]{:S(2)}) %collective-permute-start.36) | collective-permute-done | bytes 262176 | tf_op jit(solution)/shard_map/ppermute | solution.py:63
  144.1 11.2 %collective-permute-done.35 = bf16[2,64,1024]{2,1,0:T(8,128)(2,1)S(1)} collective-permute-done((bf16[2,64,1024]{2,1,0:T(8,128)(2,1)S(1)}, bf16[2,64,1024]{2,1,0:T(8,128)(2,1)S(1)}, u32[]{:S(2)}, u32[]{:S(2)}) %collective-permute-start.35) | collective-permute-done | bytes 262176 | tf_op jit(solution)/shard_map/ppermute | solution.py:63
  166.1 3.8 collective-permute-done.41
  172.3 4.1 collective-permute-done.42
  214.6 6.8 %collective-permute-done.60 = bf16[512,512]{0,1:T(8,128)(2,1)S(1)} collective-permute-done((bf16[512,512]{0,1:T(8,128)(2,1)S(1)}, bf16[512,512]{0,1:T(8,128)(2,1)S(1)}, u32[]{:S(2)}, u32[]{:S(2)}) %collective-permute-start.60) | collective-permute-done | bytes 524320 | tf_op jit(solution)/shard_map/ppermute | solution.py:265
  222.9 4.1 collective-permute-done.45
  234.3 4.0 collective-permute-done.46
  245.9 4.6 %collective-permute-start.68 = (bf16[512,256]{0,1:T(8,128)(2,1)S(1)}, bf16[512,256]{0,1:T(8,128)(2,1)S(1)}, u32[]{:S(2)}, u32[]{:S(2)}) collective-permute-start(bf16[512,256]{0,1:T(8,128)(2,1)S(1)} %fusion.87), channel_id=1, source_target_pairs={{2,3},{1,2},{0,1},{5,4},{6,5},{7,6},{10,11},{9,10},{8,9},{13,12},{... | collective-permute-start | bytes 786440 | tf_op jit(solution)/shard_map/ppermute | solution.py:274
  254.4 6.7 %collective-permute-done.63 = bf16[512,512]{0,1:T(8,128)(2,1)S(1)} collective-permute-done((bf16[512,512]{0,1:T(8,128)(2,1)S(1)}, bf16[512,512]{0,1:T(8,128)(2,1)S(1)}, u32[]{:S(2)}, u32[]{:S(2)}) %collective-permute-start.63) | collective-permute-done | bytes 524320 | tf_op jit(solution)/shard_map/ppermute | solution.py:265
  264.5 5.5 %collective-permute-done.48 = bf16[512,512]{0,1:T(8,128)(2,1)S(1)} collective-permute-done((bf16[512,512]{0,1:T(8,128)(2,1)S(1)}, bf16[512,512]{0,1:T(8,128)(2,1)S(1)}, u32[]{:S(2)}, u32[]{:S(2)}) %collective-permute-start.48) | collective-permute-done | bytes 524320 | tf_op jit(solution)/shard_map/ppermute | solution.py:265
  273.3 5.1 %collective-permute-done.64 = bf16[512,512]{0,1:T(8,128)(2,1)S(1)} collective-permute-done((bf16[512,512]{0,1:T(8,128)(2,1)S(1)}, bf16[512,512]{0,1:T(8,128)(2,1)S(1)}, u32[]{:S(2)}, u32[]{:S(2)}) %collective-permute-start.64) | collective-permute-done | bytes 524320 | tf_op jit(solution)/shard_map/ppermute | solution.py:265
  282.1 4.8 %collective-permute-done.49 = bf16[512,512]{0,1:T(8,128)(2,1)S(1)} collective-permute-done((bf16[512,512]{0,1:T(8,128)(2,1)S(1)}, bf16[512,512]{0,1:T(8,128)(2,1)S(1)}, u32[]{:S(2)}, u32[]{:S(2)}) %collective-permute-start.49) | collective-permute-done | bytes 524320 | tf_op jit(solution)/shard_map/ppermute | solution.py:265
  290.7 4.5 %collective-permute-done.65 = bf16[512,512]{0,1:T(8,128)(2,1)S(1)} collective-permute-done((bf16[512,512]{0,1:T(8,128)(2,1)S(1)}, bf16[512,512]{0,1:T(8,128)(2,1)S(1)}, u32[]{:S(2)}, u32[]{:S(2)}) %collective-permute-start.65) | collective-permute-done | bytes 524320 | tf_op jit(solution)/shard_map/ppermute | solution.py:265
  299.2 4.5 %collective-permute-done.50 = bf16[512,512]{0,1:T(8,128)(2,1)S(1)} collective-permute-done((bf16[512,512]{0,1:T(8,128)(2,1)S(1)}, bf16[512,512]{0,1:T(8,128)(2,1)S(1)}, u32[]{:S(2)}, u32[]{:S(2)}) %collective-permute-start.50) | collective-permute-done | bytes 524320 | tf_op jit(solution)/shard_map/ppermute | solution.py:265
  307.6 4.6 %collective-permute-done.66 = bf16[512,512]{0,1:T(8,128)(2,1)S(1)} collective-permute-done((bf16[512,512]{0,1:T(8,128)(2,1)S(1)}, bf16[512,512]{0,1:T(8,128)(2,1)S(1)}, u32[]{:S(2)}, u32[]{:S(2)}) %collective-permute-start.66) | collective-permute-done | bytes 524320 | tf_op jit(solution)/shard_map/ppermute | solution.py:265
  316.0 4.6 %collective-permute-done.51 = bf16[512,512]{0,1:T(8,128)(2,1)S(1)} collective-permute-done((bf16[512,512]{0,1:T(8,128)(2,1)S(1)}, bf16[512,512]{0,1:T(8,128)(2,1)S(1)}, u32[]{:S(2)}, u32[]{:S(2)}) %collective-permute-start.51) | collective-permute-done | bytes 524320 | tf_op jit(solution)/shard_map/ppermute | solution.py:265
  324.4 4.3 collective-permute-done.67
  331.9 5.6 %collective-permute-done.52 = bf16[512,512]{0,1:T(8,128)(2,1)S(1)} collective-permute-done((bf16[512,512]{0,1:T(8,128)(2,1)S(1)}, bf16[512,512]{0,1:T(8,128)(2,1)S(1)}, u32[]{:S(2)}, u32[]{:S(2)}) %collective-permute-start.52) | collective-permute-done | bytes 524320 | tf_op jit(solution)/shard_map/ppermute | solution.py:265
  342.5 5.2 %collective-permute-start.74 = (bf16[512,256]{0,1:T(8,128)(2,1)S(1)}, bf16[512,256]{0,1:T(8,128)(2,1)S(1)}, u32[]{:S(2)}, u32[]{:S(2)}) collective-permute-start(bf16[512,256]{0,1:T(8,128)(2,1)S(1)} %broadcast_select_fusion.4), channel_id=1, source_target_pairs={{2,3},{1,2},{0,1},{5,4},{6,5},{7,6},{10,11},{9,10},{8,9},{13,12},{... | collective-permute-start | bytes 786440 | tf_op jit(solution)/shard_map/ppermute | solution.py:274
  347.8 3.9 collective-permute-start.59
  351.7 4.3 collective-permute-done.77
  376.5 4.4 %collective-permute-start.84 = (bf16[512,256]{0,1:T(8,128)(2,1)S(1)}, bf16[512,256]{0,1:T(8,128)(2,1)S(1)}, u32[]{:S(2)}, u32[]{:S(2)}) collective-permute-start(bf16[512,256]{0,1:T(8,128)(2,1)S(1)} %fusion.85), channel_id=1, source_target_pairs={{0,1},{7,6},{8,9},{15,14},{16,17},{23,22},{24,25},{31,30}} | collective-permute-start | bytes 786440 | tf_op jit(solution)/shard_map/ppermute | solution.py:279
  399.6 6.0 %collective-permute-done.86 = bf16[2,64,1024]{2,1,0:T(8,128)(2,1)S(1)} collective-permute-done((bf16[2,64,1024]{2,1,0:T(8,128)(2,1)S(1)}, bf16[2,64,1024]{2,1,0:T(8,128)(2,1)S(1)}, u32[]{:S(2)}, u32[]{:S(2)}) %collective-permute-start.86) | collective-permute-done | bytes 262176 | tf_op jit(solution)/shard_map/ppermute | solution.py:56
  406.7 3.9 collective-permute-done.87
  417.0 12.5 %all_to_all.10 = bf16[8,12,2048]{2,1,0:T(8,128)(2,1)S(1)} all-to-all(bf16[8,12,2048]{2,1,0:T(8,128)(2,1)S(1)} %reshape.138), channel_id=1, replica_groups=mesh['ctx'=8,'mp'=4] {'ctx'}, dimensions={0} | all-to-all | bytes 786432 | tf_op jit(solution)/shard_map/all_to_all | solution.py:483
  (420 shorter events, 249.3 us)
Async XLA Ops:
  0.7 20.7 %collective-permute-start = (f32[1,64]{1,0:T(1,128)S(1)}, f32[1,64]{1,0:T(1,128)S(1)}, u32[]{:S(2)}, u32[]{:S(2)}) collective-permute-start(f32[1,64]{1,0:T(1,128)S(1)} %get-tuple-element.156), channel_id=1, source_target_pairs={{0,8},{4,12},{8,0},{12,4},{16,24},{20,28},{24,16},{28,20},{1,9},{5... | collective-permute-start | bytes 776 | tf_op jit(solution)/shard_map/ppermute | solution.py:56
  9.5 16.9 %all-to-all-start = ((bf16[8,12,2048]{2,1,0:T(8,128)(2,1)}), bf16[8,12,2048]{2,1,0:T(8,128)(2,1)S(1)}, u32[]{:S(2)}, u32[]{:S(2)}) async-start(bf16[8,12,2048]{2,1,0:T(8,128)(2,1)} %reshape.129), calls=%async_computation | async-start | bytes 1048576 | tf_op jit(solution)/shard_map/all_to_all | solution.py:364
  30.9 21.4 %collective-permute-start.8 = (bf16[64,1024]{1,0:T(8,128)(2,1)S(1)}, bf16[64,1024]{1,0:T(8,128)(2,1)S(1)}, u32[]{:S(2)}, u32[]{:S(2)}) collective-permute-start(bf16[64,1024]{1,0:T(8,128)(2,1)S(1)} %get-tuple-element.137), channel_id=1, source_target_pairs={{0,2},{1,10},{2,18},{3,26},{4,6},{5,14},{6,22},{7,30},{8,3},{9,11}... | collective-permute-start | bytes 393224 | tf_op jit(solution)/shard_map/ppermute | solution.py:137
  32.8 20.3 %collective-permute-start.6 = (bf16[64,1024]{1,0:T(8,128)(2,1)S(1)}, bf16[64,1024]{1,0:T(8,128)(2,1)S(1)}, u32[]{:S(2)}, u32[]{:S(2)}) collective-permute-start(bf16[64,1024]{1,0:T(8,128)(2,1)S(1)} %get-tuple-element.137), channel_id=1, source_target_pairs={{0,1},{1,9},{2,17},{3,25},{4,5},{5,13},{6,21},{7,29},{8,0},{9,8},{... | collective-permute-start | bytes 393224 | tf_op jit(solution)/shard_map/ppermute | solution.py:137
  33.2 22.8 %collective-permute-start.4 = (bf16[64,1024]{1,0:T(8,128)(2,1)S(1)}, bf16[64,1024]{1,0:T(8,128)(2,1)S(1)}, u32[]{:S(2)}, u32[]{:S(2)}) collective-permute-start(bf16[64,1024]{1,0:T(8,128)(2,1)S(1)} %get-tuple-element.137), channel_id=1, source_target_pairs={{0,0},{1,8},{2,16},{3,24},{4,4},{5,12},{6,20},{7,28},{8,1},{9,9},{... | collective-permute-start | bytes 393224 | tf_op jit(solution)/shard_map/ppermute | solution.py:137
  57.8 18.8 %collective-permute-start.11 = (bf16[512,768]{1,0:T(8,128)(2,1)S(1)}, bf16[512,768]{1,0:T(8,128)(2,1)S(1)}, u32[]{:S(2)}, u32[]{:S(2)}) collective-permute-start(bf16[512,768]{1,0:T(8,128)(2,1)S(1)} %convolution_convert_fusion.2), channel_id=1, source_target_pairs={{0,4},{4,0},{8,12},{12,8},{16,20},{20,16},{24,28},{28,24},{1,5},{5... | collective-permute-start | bytes 2359304 | tf_op jit(solution)/shard_map/ppermute | solution.py:56
  111.0 17.4 %collective-permute-start.33 = (bf16[64,1024]{1,0:T(8,128)(2,1)S(1)}, bf16[64,1024]{1,0:T(8,128)(2,1)S(1)}, u32[]{:S(2)}, u32[]{:S(2)}) collective-permute-start(bf16[64,1024]{1,0:T(8,128)(2,1)S(1)} %get-tuple-element.76), channel_id=1, source_target_pairs={{0,28},{4,24},{8,20},{12,16},{16,12},{20,8},{24,4},{28,0},{1,29},{... | collective-permute-start | bytes 393224 | tf_op jit(solution)/shard_map/ppermute | solution.py:56
  112.2 16.2 %collective-permute-start.32 = (bf16[64,1024]{1,0:T(8,128)(2,1)S(1)}, bf16[64,1024]{1,0:T(8,128)(2,1)S(1)}, u32[]{:S(2)}, u32[]{:S(2)}) collective-permute-start(bf16[64,1024]{1,0:T(8,128)(2,1)S(1)} %get-tuple-element.77), channel_id=1, source_target_pairs={{0,24},{4,28},{8,16},{12,20},{16,8},{20,12},{24,0},{28,4},{1,25},{... | collective-permute-start | bytes 393224 | tf_op jit(solution)/shard_map/ppermute | solution.py:56
  132.4 22.9 %collective-permute-start.35 = (bf16[2,64,1024]{2,1,0:T(8,128)(2,1)S(1)}, bf16[2,64,1024]{2,1,0:T(8,128)(2,1)S(1)}, u32[]{:S(2)}, u32[]{:S(2)}) collective-permute-start(bf16[2,64,1024]{2,1,0:T(8,128)(2,1)S(1)} %get-tuple-element.75), channel_id=1, source_target_pairs={{0,2},{1,3},{2,0},{3,1},{4,6},{5,7},{6,4},{7,5},{8,10},{9,11},{10,... | collective-permute-start | bytes 786440 | tf_op jit(solution)/shard_map/ppermute | solution.py:63
  211.7 15.3 %collective-permute-start.45 = (bf16[512,512]{0,1:T(8,128)(2,1)S(1)}, bf16[512,512]{0,1:T(8,128)(2,1)S(1)}, u32[]{:S(2)}, u32[]{:S(2)}) collective-permute-start(bf16[512,512]{0,1:T(8,128)(2,1)S(1)} %select_select_fusion.1), channel_id=1, source_target_pairs={{3,2},{2,1},{1,0},{4,5},{5,6},{6,7},{11,10},{10,9},{9,8},{12,13},{... | collective-permute-start | bytes 1572872 | tf_op jit(solution)/shard_map/ppermute | solution.py:265
  244.4 16.7 %collective-permute-start.63 = (bf16[512,512]{0,1:T(8,128)(2,1)S(1)}, bf16[512,512]{0,1:T(8,128)(2,1)S(1)}, u32[]{:S(2)}, u32[]{:S(2)}) collective-permute-start(bf16[512,512]{0,1:T(8,128)(2,1)S(1)} %get-tuple-element.121), channel_id=1, source_target_pairs={{3,2},{2,1},{1,0},{4,5},{5,6},{6,7},{11,10},{10,9},{9,8},{12,13},{... | collective-permute-start | bytes 1572872 | tf_op jit(solution)/shard_map/ppermute | solution.py:265
  245.9 15.6 %collective-permute-start.68 = (bf16[512,256]{0,1:T(8,128)(2,1)S(1)}, bf16[512,256]{0,1:T(8,128)(2,1)S(1)}, u32[]{:S(2)}, u32[]{:S(2)}) collective-permute-start(bf16[512,256]{0,1:T(8,128)(2,1)S(1)} %fusion.87), channel_id=1, source_target_pairs={{2,3},{1,2},{0,1},{5,4},{6,5},{7,6},{10,11},{9,10},{8,9},{13,12},{... | collective-permute-start | bytes 786440 | tf_op jit(solution)/shard_map/ppermute | solution.py:274
  251.0 19.3 %collective-permute-start.53 = (bf16[512,256]{0,1:T(8,128)(2,1)S(1)}, bf16[512,256]{0,1:T(8,128)(2,1)S(1)}, u32[]{:S(2)}, u32[]{:S(2)}) collective-permute-start(bf16[512,256]{0,1:T(8,128)(2,1)S(1)} %fusion.93), channel_id=1, source_target_pairs={{2,3},{1,2},{0,1},{5,4},{6,5},{7,6},{10,11},{9,10},{8,9},{13,12},{... | collective-permute-start | bytes 786440 | tf_op jit(solution)/shard_map/ppermute | solution.py:274
  252.9 17.0 %collective-permute-start.48 = (bf16[512,512]{0,1:T(8,128)(2,1)S(1)}, bf16[512,512]{0,1:T(8,128)(2,1)S(1)}, u32[]{:S(2)}, u32[]{:S(2)}) collective-permute-start(bf16[512,512]{0,1:T(8,128)(2,1)S(1)} %get-tuple-element.115), channel_id=1, source_target_pairs={{3,2},{2,1},{1,0},{4,5},{5,6},{6,7},{11,10},{10,9},{9,8},{12,13},{... | collective-permute-start | bytes 1572872 | tf_op jit(solution)/shard_map/ppermute | solution.py:265
  261.7 17.1 %collective-permute-start.69 = (bf16[512,256]{0,1:T(8,128)(2,1)S(1)}, bf16[512,256]{0,1:T(8,128)(2,1)S(1)}, u32[]{:S(2)}, u32[]{:S(2)}) collective-permute-start(bf16[512,256]{0,1:T(8,128)(2,1)S(1)} %get-tuple-element.37), channel_id=1, source_target_pairs={{2,3},{1,2},{0,1},{5,4},{6,5},{7,6},{10,11},{9,10},{8,9},{13,12},{... | collective-permute-start | bytes 786440 | tf_op jit(solution)/shard_map/ppermute | solution.py:274
  263.2 15.3 %collective-permute-start.64 = (bf16[512,512]{0,1:T(8,128)(2,1)S(1)}, bf16[512,512]{0,1:T(8,128)(2,1)S(1)}, u32[]{:S(2)}, u32[]{:S(2)}) collective-permute-start(bf16[512,512]{0,1:T(8,128)(2,1)S(1)} %get-tuple-element.119), channel_id=1, source_target_pairs={{3,2},{2,1},{1,0},{4,5},{5,6},{6,7},{11,10},{10,9},{9,8},{12,13},{... | collective-permute-start | bytes 1572872 | tf_op jit(solution)/shard_map/ppermute | solution.py:265
  270.6 16.6 %collective-permute-start.54 = (bf16[512,256]{0,1:T(8,128)(2,1)S(1)}, bf16[512,256]{0,1:T(8,128)(2,1)S(1)}, u32[]{:S(2)}, u32[]{:S(2)}) collective-permute-start(bf16[512,256]{0,1:T(8,128)(2,1)S(1)} %get-tuple-element.31), channel_id=1, source_target_pairs={{2,3},{1,2},{0,1},{5,4},{6,5},{7,6},{10,11},{9,10},{8,9},{13,12},{... | collective-permute-start | bytes 786440 | tf_op jit(solution)/shard_map/ppermute | solution.py:274
  272.0 14.8 %collective-permute-start.49 = (bf16[512,512]{0,1:T(8,128)(2,1)S(1)}, bf16[512,512]{0,1:T(8,128)(2,1)S(1)}, u32[]{:S(2)}, u32[]{:S(2)}) collective-permute-start(bf16[512,512]{0,1:T(8,128)(2,1)S(1)} %get-tuple-element.113), channel_id=1, source_target_pairs={{3,2},{2,1},{1,0},{4,5},{5,6},{6,7},{11,10},{10,9},{9,8},{12,13},{... | collective-permute-start | bytes 1572872 | tf_op jit(solution)/shard_map/ppermute | solution.py:265
  279.0 16.7 %collective-permute-start.70 = (bf16[512,256]{0,1:T(8,128)(2,1)S(1)}, bf16[512,256]{0,1:T(8,128)(2,1)S(1)}, u32[]{:S(2)}, u32[]{:S(2)}) collective-permute-start(bf16[512,256]{0,1:T(8,128)(2,1)S(1)} %get-tuple-element.35), channel_id=1, source_target_pairs={{2,3},{1,2},{0,1},{5,4},{6,5},{7,6},{10,11},{9,10},{8,9},{13,12},{... | collective-permute-start | bytes 786440 | tf_op jit(solution)/shard_map/ppermute | solution.py:274
  280.8 14.5 %collective-permute-start.65 = (bf16[512,512]{0,1:T(8,128)(2,1)S(1)}, bf16[512,512]{0,1:T(8,128)(2,1)S(1)}, u32[]{:S(2)}, u32[]{:S(2)}) collective-permute-start(bf16[512,512]{0,1:T(8,128)(2,1)S(1)} %get-tuple-element.117), channel_id=1, source_target_pairs={{3,2},{2,1},{1,0},{4,5},{5,6},{6,7},{11,10},{10,9},{9,8},{12,13},{... | collective-permute-start | bytes 1572872 | tf_op jit(solution)/shard_map/ppermute | solution.py:265
  287.4 16.7 %collective-permute-start.55 = (bf16[512,256]{0,1:T(8,128)(2,1)S(1)}, bf16[512,256]{0,1:T(8,128)(2,1)S(1)}, u32[]{:S(2)}, u32[]{:S(2)}) collective-permute-start(bf16[512,256]{0,1:T(8,128)(2,1)S(1)} %get-tuple-element.29), channel_id=1, source_target_pairs={{2,3},{1,2},{0,1},{5,4},{6,5},{7,6},{10,11},{9,10},{8,9},{13,12},{... | collective-permute-start | bytes 786440 | tf_op jit(solution)/shard_map/ppermute | solution.py:274
  295.8 16.7 %collective-permute-start.71 = (bf16[512,256]{0,1:T(8,128)(2,1)S(1)}, bf16[512,256]{0,1:T(8,128)(2,1)S(1)}, u32[]{:S(2)}, u32[]{:S(2)}) collective-permute-start(bf16[512,256]{0,1:T(8,128)(2,1)S(1)} %get-tuple-element.33), channel_id=1, source_target_pairs={{2,3},{1,2},{0,1},{5,4},{6,5},{7,6},{10,11},{9,10},{8,9},{13,12},{... | collective-permute-start | bytes 786440 | tf_op jit(solution)/shard_map/ppermute | solution.py:274
  304.3 16.6 %collective-permute-start.56 = (bf16[512,256]{0,1:T(8,128)(2,1)S(1)}, bf16[512,256]{0,1:T(8,128)(2,1)S(1)}, u32[]{:S(2)}, u32[]{:S(2)}) collective-permute-start(bf16[512,256]{0,1:T(8,128)(2,1)S(1)} %get-tuple-element.27), channel_id=1, source_target_pairs={{2,3},{1,2},{0,1},{5,4},{6,5},{7,6},{10,11},{9,10},{8,9},{13,12},{... | collective-permute-start | bytes 786440 | tf_op jit(solution)/shard_map/ppermute | solution.py:274
  312.7 16.2 %collective-permute-start.72 = (bf16[512,256]{0,1:T(8,128)(2,1)S(1)}, bf16[512,256]{0,1:T(8,128)(2,1)S(1)}, u32[]{:S(2)}, u32[]{:S(2)}) collective-permute-start(bf16[512,256]{0,1:T(8,128)(2,1)S(1)} %get-tuple-element.25), channel_id=1, source_target_pairs={{2,3},{1,2},{0,1},{5,4},{6,5},{7,6},{10,11},{9,10},{8,9},{13,12},{... | collective-permute-start | bytes 786440 | tf_op jit(solution)/shard_map/ppermute | solution.py:274
  321.1 16.6 %collective-permute-start.57 = (bf16[512,256]{0,1:T(8,128)(2,1)S(1)}, bf16[512,256]{0,1:T(8,128)(2,1)S(1)}, u32[]{:S(2)}, u32[]{:S(2)}) collective-permute-start(bf16[512,256]{0,1:T(8,128)(2,1)S(1)} %get-tuple-element.21), channel_id=1, source_target_pairs={{2,3},{1,2},{0,1},{5,4},{6,5},{7,6},{10,11},{9,10},{8,9},{13,12},{... | collective-permute-start | bytes 786440 | tf_op jit(solution)/shard_map/ppermute | solution.py:274
  339.9 16.1 %collective-permute-start.77 = (bf16[512,512]{0,1:T(8,128)(2,1)S(1)}, bf16[512,512]{0,1:T(8,128)(2,1)S(1)}, u32[]{:S(2)}, u32[]{:S(2)}) collective-permute-start(bf16[512,512]{0,1:T(8,128)(2,1)S(1)} %get-tuple-element.91), channel_id=1, source_target_pairs={{3,2},{2,1},{1,0},{4,5},{5,6},{6,7},{11,10},{10,9},{9,8},{12,13},{... | collective-permute-start | bytes 1572872 | tf_op jit(solution)/shard_map/ppermute | solution.py:265
  341.2 30.1 %collective-permute-start.81 = (bf16[512,512]{0,1:T(8,128)(2,1)S(1)}, bf16[512,512]{0,1:T(8,128)(2,1)S(1)}, u32[]{:S(2)}, u32[]{:S(2)}) collective-permute-start(bf16[512,512]{0,1:T(8,128)(2,1)S(1)} %get-tuple-element.89), channel_id=1, source_target_pairs={{3,2},{2,1},{1,0},{4,5},{5,6},{6,7},{11,10},{10,9},{9,8},{12,13},{... | collective-permute-start | bytes 1572872 | tf_op jit(solution)/shard_map/ppermute | solution.py:265
  342.5 21.2 %collective-permute-start.74 = (bf16[512,256]{0,1:T(8,128)(2,1)S(1)}, bf16[512,256]{0,1:T(8,128)(2,1)S(1)}, u32[]{:S(2)}, u32[]{:S(2)}) collective-permute-start(bf16[512,256]{0,1:T(8,128)(2,1)S(1)} %broadcast_select_fusion.4), channel_id=1, source_target_pairs={{2,3},{1,2},{0,1},{5,4},{6,5},{7,6},{10,11},{9,10},{8,9},{13,12},{... | collective-permute-start | bytes 786440 | tf_op jit(solution)/shard_map/ppermute | solution.py:274
  356.3 26.8 %collective-permute-start.80 = (bf16[512,256]{0,1:T(8,128)(2,1)S(1)}, bf16[512,256]{0,1:T(8,128)(2,1)S(1)}, u32[]{:S(2)}, u32[]{:S(2)}) collective-permute-start(bf16[512,256]{0,1:T(8,128)(2,1)S(1)} %fusion.86), channel_id=1, source_target_pairs={{0,1},{7,6},{8,9},{15,14},{16,17},{23,22},{24,25},{31,30}} | collective-permute-start | bytes 786440 | tf_op jit(solution)/shard_map/ppermute | solution.py:279
  359.1 25.3 %collective-permute-start.79 = (bf16[512,256]{0,1:T(8,128)(2,1)S(1)}, bf16[512,256]{0,1:T(8,128)(2,1)S(1)}, u32[]{:S(2)}, u32[]{:S(2)}) collective-permute-start(bf16[512,256]{0,1:T(8,128)(2,1)S(1)} %fusion.86), channel_id=1, source_target_pairs={{0,2},{7,5},{8,10},{15,13},{16,18},{23,21},{24,26},{31,29}} | collective-permute-start | bytes 786440 | tf_op jit(solution)/shard_map/ppermute | solution.py:279
  360.5 23.9 %collective-permute-start.78 = (bf16[512,256]{0,1:T(8,128)(2,1)S(1)}, bf16[512,256]{0,1:T(8,128)(2,1)S(1)}, u32[]{:S(2)}, u32[]{:S(2)}) collective-permute-start(bf16[512,256]{0,1:T(8,128)(2,1)S(1)} %fusion.86), channel_id=1, source_target_pairs={{0,3},{7,4},{8,11},{15,12},{16,19},{23,20},{24,27},{31,28}} | collective-permute-start | bytes 786440 | tf_op jit(solution)/shard_map/ppermute | solution.py:279
  364.5 16.6 %collective-permute-start.76 = (bf16[512,256]{0,1:T(8,128)(2,1)S(1)}, bf16[512,256]{0,1:T(8,128)(2,1)S(1)}, u32[]{:S(2)}, u32[]{:S(2)}) collective-permute-start(bf16[512,256]{0,1:T(8,128)(2,1)S(1)} %get-tuple-element.129), channel_id=1, source_target_pairs={{2,3},{1,2},{0,1},{5,4},{6,5},{7,6},{10,11},{9,10},{8,9},{13,12},{... | collective-permute-start | bytes 786440 | tf_op jit(solution)/shard_map/ppermute | solution.py:274
  (79 other events, 701.7 us)

commit v5 on v4

--- a/solution.py
+++ b/solution.py
@@ -88,10 +88,12 @@
         return jnp.concatenate([near, self.swap(near, 1)], axis=0)
 
     def small_gather(self, x):
-        near = self.far_gather(x, self.far_bits)
-        near = jnp.stack([near[i] for i in self.even])
-        other = self.swap(near, 1)
-        return jnp.stack([near, other], axis=1).reshape(self.C, *x.shape)
+        out = x[None]
+        b = 1
+        while b < self.C:
+            out = jnp.concatenate([out, self.swap(out, b)])
+            b *= 2
+        return out
 
     def xor_order(self, x, value):
         b = 1
@@ -194,8 +196,8 @@
     side_bit = grid.far_bits[0]
     first, second = near[:half], near[half:]
     sq_a, sq_b = squares[:half], squares[half:]
+    out = jnp.concatenate([second[:, d : 3 * d], second[:, 4 * d :]], axis=1).astype(BF)
     got_a = grid.swap(first[:, 3 * d :].astype(BF), group_bit).astype(F32)
-    out = jnp.concatenate([second[:, d : 3 * d], second[:, 4 * d :]], axis=1).astype(BF)
     got_b = grid.swap(out, side_bit).astype(F32)
     sq_a = sq_a + grid.swap(sq_a, group_bit)
     sq_b = sq_b + grid.swap(sq_b, side_bit)
@@ -299,6 +301,7 @@
                     half = rows // 2
                     far = jnp.dot(block[half:], weight, preferred_element_type=F32)
                     near = jnp.dot(block[:half], weight, preferred_element_type=F32)
+                    near = lax.optimization_barrier(near)
                     if total is not None:
                         far = far + total[half:]
                         near = near + total[:half]
@@ -361,6 +364,7 @@
         .astype(BF)
         .reshape(ctx_count, capacity, feature_cols)
     )
+    positions = grid.small_gather(kept_pos.astype(F32))
     incoming = lax.all_to_all(outgoing, "ctx", split_axis=0, concat_axis=0, tiled=True).reshape(
         slots_all, feature_cols
     )
@@ -375,8 +379,6 @@
     )
     local_rows = incoming[recv_index]
     fits = q_local == ctx_count and kv_local == 2 and len(grid.far_bits) == 2
-    positions = grid.small_gather(kept_pos.astype(F32))
-    local_rows, positions = lax.optimization_barrier((local_rows, positions))
     pos_all = grid.xor_order(positions, my_index ^ (grid.H * grid.m)).reshape(rows)
     blocks = grid.rows_to_slices(local_rows)
     raw_share = local_rows.astype(F32)
@@ -467,10 +469,12 @@
         )
     )
     router_score = jax.nn.sigmoid(sums[1])
-    second_inverse = lax.rsqrt(sums[0] / feature_total + 1e-05)[:, None]
-    second_scaled = (mixed_share * second_inverse * mlp_gain.astype(F32)).astype(BF)
+    second_inverse = grid.small_gather(lax.rsqrt(sums[0] / feature_total + 1e-05))
+    second_inverse = jnp.concatenate([second_inverse[i] for i in grid.order])[:, None]
+    second_scaled = (mixed_share * mlp_gain.astype(F32)).astype(BF)
     mid = feature_cols // 2
     every_scaled = grid.gather((second_scaled[:, :mid], second_scaled[:, mid:]))
+    every_scaled = (every_scaled.astype(F32) * second_inverse).astype(BF)
     near, far, tick = feed_forward(grid, every_scaled, gate_weight, up_weight, down_weight)
     mlp_share = grid.scatter_sum(near, far)
     update = (router_score[:, None] * (head_share + mlp_share) + tick).astype(BF)

time: 436 us -> 432 us (level)
  waiting for transfers between devices: 180 us -> 149 us
  starting transfers between devices: 151 us -> 174 us
    ppermute x16, starting transfers between devices: 37.8 us -> 57 us  [feed_forward(): passed[s] = lax.ppermute(send, ('ctx', 'mp'), outward)]
    ppermute x18, waiting for transfers between devices: 76.2 us -> 61.4 us  [feed_forward(): got[s] = lax.ppermute(send, ('ctx', 'mp'), inward)]
    ppermute x36 -> x39, waiting for transfers between devices: 61.4 us -> 54.8 us  [swap(): return lax.ppermute(x, 'ctx', [(i, i ^ b) for i in range(self.C)])]
    ppermute x8, waiting for transfers between devices: 6.84 us -> 0.84 us  [rows_to_slices(): lax.ppermute(payload[r % self.H], ('ctx', 'mp'), self.flat(pairs))]
    ppermute x36 -> x39, starting transfers between devices: 43.2 us -> 45.4 us  [swap(): return lax.ppermute(x, 'ctx', [(i, i ^ b) for i in range(self.C)])]
  transfers between devices with their start and end apart: 91 -> 94, of which waited for: 52 -> 52; matrix products, arithmetic and copies ran while one was open for 9% -> 10% of each run, Pallas kernels for 0% -> 0%
where the time goes in v5:
time: 432 us; the launch traced here: 427 us
  starting transfers between devices  174 us (40%)
  waiting for transfers between devices  149 us (34%)
  matrix products  52.9 us (12%)
  other arithmetic  25 us (6%)
  blocking collectives  12.3 us (3%)
  local copies, waits for them, and re-layouts  11.4 us (3%)
    ppermute x18, waiting for transfers between devices, feed_forward(): got[s] = lax.ppermute(send, ('ctx', 'mp'), inward)  61.4 us
    ppermute x16, starting transfers between devices, feed_forward(): passed[s] = lax.ppermute(send, ('ctx', 'mp'), outward)  57 us
    ppermute x39, waiting for transfers between devices, swap(): return lax.ppermute(x, 'ctx', [(i, i ^ b) for i in range(self.C)])  54.8 us
    ppermute x39, starting transfers between devices, swap(): return lax.ppermute(x, 'ctx', [(i, i ^ b) for i in range(self.C)])  45.4 us
    ppermute x18, starting transfers between devices, feed_forward(): got[s] = lax.ppermute(send, ('ctx', 'mp'), inward)  23.3 us
    ppermute x6, waiting for transfers between devices, rotate_mp(): lax.ppermute(block_for(s), 'mp', [(i, (i + s) % self.M) for i in range(se...  22.7 us
    ppermute x8, starting transfers between devices, rows_to_slices(): lax.ppermute(payload[r % self.H], ('ctx', 'mp'), self.flat(pairs))  22 us
    dot_general x14, matrix products, part(): g = jnp.dot(normed, gate_weight[:, lo:hi], preferred_element_type=F32)  17.7 us
  transfers between devices with their start and end apart: 94, of which 52 were waited for; matrix products, arithmetic and copies ran while one was open for 10% of the time, Pallas kernels for 0%

profile of v5, /device:TPU:0, one launch (start us, length us, event | category | flops | bytes accessed | tf_op | source)
XLA Modules:
  0.0 427.1 jit_solution(9692568128110907258)
XLA Ops:
  7.0 4.8 %all-to-all-start = ((bf16[8,12,2048]{2,1,0:T(8,128)(2,1)}), bf16[8,12,2048]{2,1,0:T(8,128)(2,1)S(1)}, u32[]{:S(2)}, u32[]{:S(2)}) async-start(bf16[8,12,2048]{2,1,0:T(8,128)(2,1)} %reshape.187), calls=%async_computation | async-start | bytes 1048576 | tf_op jit(solution)/shard_map/all_to_all | solution.py:368
  35.5 5.7 %collective-permute-start.7 = (bf16[64,1024]{1,0:T(8,128)(2,1)S(1)}, bf16[64,1024]{1,0:T(8,128)(2,1)S(1)}, u32[]{:S(2)}, u32[]{:S(2)}) collective-permute-start(bf16[64,1024]{1,0:T(8,128)(2,1)S(1)} %get-tuple-element.138), channel_id=1, source_target_pairs={{0,6},{1,14},{2,22},{3,30},{4,2},{5,10},{6,18},{7,26},{8,7},{9,15}... | collective-permute-start | bytes 393224 | tf_op jit(solution)/shard_map/ppermute | solution.py:139
  41.2 4.9 %collective-permute-start.5 = (bf16[64,1024]{1,0:T(8,128)(2,1)S(1)}, bf16[64,1024]{1,0:T(8,128)(2,1)S(1)}, u32[]{:S(2)}, u32[]{:S(2)}) collective-permute-start(bf16[64,1024]{1,0:T(8,128)(2,1)S(1)} %get-tuple-element.138), channel_id=1, source_target_pairs={{0,5},{1,13},{2,21},{3,29},{4,1},{5,9},{6,17},{7,25},{8,4},{9,12},... | collective-permute-start | bytes 393224 | tf_op jit(solution)/shard_map/ppermute | solution.py:139
  46.3 4.6 %collective-permute-start.3 = (bf16[64,1024]{1,0:T(8,128)(2,1)S(1)}, bf16[64,1024]{1,0:T(8,128)(2,1)S(1)}, u32[]{:S(2)}, u32[]{:S(2)}) collective-permute-start(bf16[64,1024]{1,0:T(8,128)(2,1)S(1)} %get-tuple-element.138), channel_id=1, source_target_pairs={{0,4},{1,12},{2,20},{3,28},{4,0},{5,8},{6,16},{7,24},{8,5},{9,13},... | collective-permute-start | bytes 393224 | tf_op jit(solution)/shard_map/ppermute | solution.py:139
  54.6 11.6 %collective-permute-start.17 = (f32[256]{0:T(256)S(1)}, f32[256]{0:T(256)S(1)}, u32[]{:S(2)}, u32[]{:S(2)}) collective-permute-start(f32[256]{0:T(256)S(1)} %get-tuple-element.153), channel_id=1, source_target_pairs={{0,16},{4,20},{8,24},{12,28},{16,0},{20,4},{24,8},{28,12},{1,17},{... | collective-permute-start | bytes 3080 | tf_op jit(solution)/shard_map/ppermute | solution.py:56
  113.2 6.5 %collective-permute-done.28 = bf16[64,1024]{1,0:T(8,128)(2,1)S(1)} collective-permute-done((bf16[64,1024]{1,0:T(8,128)(2,1)S(1)}, bf16[64,1024]{1,0:T(8,128)(2,1)S(1)}, u32[]{:S(2)}, u32[]{:S(2)}) %collective-permute-start.28) | collective-permute-done | bytes 131104 | tf_op jit(solution)/shard_map/ppermute | solution.py:56
  119.6 5.5 %collective-permute-done.29 = bf16[64,1024]{1,0:T(8,128)(2,1)S(1)} collective-permute-done((bf16[64,1024]{1,0:T(8,128)(2,1)S(1)}, bf16[64,1024]{1,0:T(8,128)(2,1)S(1)}, u32[]{:S(2)}, u32[]{:S(2)}) %collective-permute-start.29) | collective-permute-done | bytes 131104 | tf_op jit(solution)/shard_map/ppermute | solution.py:56
  130.0 6.4 %collective-permute-done.34 = bf16[2,64,1024]{2,1,0:T(8,128)(2,1)S(1)} collective-permute-done((bf16[2,64,1024]{2,1,0:T(8,128)(2,1)S(1)}, bf16[2,64,1024]{2,1,0:T(8,128)(2,1)S(1)}, u32[]{:S(2)}, u32[]{:S(2)}) %collective-permute-start.34) | collective-permute-done | bytes 262176 | tf_op jit(solution)/shard_map/ppermute | solution.py:63
  136.5 4.4 %collective-permute-done.36 = bf16[2,64,1024]{2,1,0:T(8,128)(2,1)S(1)} collective-permute-done((bf16[2,64,1024]{2,1,0:T(8,128)(2,1)S(1)}, bf16[2,64,1024]{2,1,0:T(8,128)(2,1)S(1)}, u32[]{:S(2)}, u32[]{:S(2)}) %collective-permute-start.36) | collective-permute-done | bytes 262176 | tf_op jit(solution)/shard_map/ppermute | solution.py:63
  140.8 10.1 %collective-permute-done.35 = bf16[2,64,1024]{2,1,0:T(8,128)(2,1)S(1)} collective-permute-done((bf16[2,64,1024]{2,1,0:T(8,128)(2,1)S(1)}, bf16[2,64,1024]{2,1,0:T(8,128)(2,1)S(1)}, u32[]{:S(2)}, u32[]{:S(2)}) %collective-permute-start.35) | collective-permute-done | bytes 262176 | tf_op jit(solution)/shard_map/ppermute | solution.py:63
  211.1 7.6 %collective-permute-done.63 = bf16[512,512]{0,1:T(8,128)(2,1)S(1)} collective-permute-done((bf16[512,512]{0,1:T(8,128)(2,1)S(1)}, bf16[512,512]{0,1:T(8,128)(2,1)S(1)}, u32[]{:S(2)}, u32[]{:S(2)}) %collective-permute-start.63) | collective-permute-done | bytes 524320 | tf_op jit(solution)/shard_map/ppermute | solution.py:267
  220.2 4.1 collective-permute-done.48
  225.8 4.1 collective-permute-done.64
  231.6 4.0 collective-permute-done.49
  237.2 4.1 collective-permute-done.65
  243.2 4.6 %collective-permute-start.71 = (bf16[512,256]{0,1:T(8,128)(2,1)S(1)}, bf16[512,256]{0,1:T(8,128)(2,1)S(1)}, u32[]{:S(2)}, u32[]{:S(2)}) collective-permute-start(bf16[512,256]{0,1:T(8,128)(2,1)S(1)} %fusion.81), channel_id=1, source_target_pairs={{2,3},{1,2},{0,1},{5,4},{6,5},{7,6},{10,11},{9,10},{8,9},{13,12},{... | collective-permute-start | bytes 786440 | tf_op jit(solution)/shard_map/ppermute | solution.py:276
  248.3 3.7 collective-permute-start.56
  262.1 4.8 %collective-permute-done.51 = bf16[512,512]{0,1:T(8,128)(2,1)S(1)} collective-permute-done((bf16[512,512]{0,1:T(8,128)(2,1)S(1)}, bf16[512,512]{0,1:T(8,128)(2,1)S(1)}, u32[]{:S(2)}, u32[]{:S(2)}) %collective-permute-start.51) | collective-permute-done | bytes 524320 | tf_op jit(solution)/shard_map/ppermute | solution.py:267
  272.2 3.7 collective-permute-done.67
  276.5 3.9 collective-permute-start.73
  285.2 3.7 collective-permute-start.58
  293.6 3.7 collective-permute-start.74
  302.1 3.7 collective-permute-start.59
  310.6 3.7 collective-permute-start.75
  319.0 3.7 collective-permute-start.60
  327.3 4.0 collective-permute-start.76
  331.3 4.6 %collective-permute-done.55 = bf16[512,512]{0,1:T(8,128)(2,1)S(1)} collective-permute-done((bf16[512,512]{0,1:T(8,128)(2,1)S(1)}, bf16[512,512]{0,1:T(8,128)(2,1)S(1)}, u32[]{:S(2)}, u32[]{:S(2)}) %collective-permute-start.55) | collective-permute-done | bytes 524320 | tf_op jit(solution)/shard_map/ppermute | solution.py:267
  342.4 5.2 %collective-permute-start.77 = (bf16[512,256]{0,1:T(8,128)(2,1)S(1)}, bf16[512,256]{0,1:T(8,128)(2,1)S(1)}, u32[]{:S(2)}, u32[]{:S(2)}) collective-permute-start(bf16[512,256]{0,1:T(8,128)(2,1)S(1)} %broadcast_select_fusion.4), channel_id=1, source_target_pairs={{2,3},{1,2},{0,1},{5,4},{6,5},{7,6},{10,11},{9,10},{8,9},{13,12},{... | collective-permute-start | bytes 786440 | tf_op jit(solution)/shard_map/ppermute | solution.py:276
  347.6 3.9 collective-permute-start.62
  376.0 4.4 %collective-permute-start.87 = (bf16[512,256]{0,1:T(8,128)(2,1)S(1)}, bf16[512,256]{0,1:T(8,128)(2,1)S(1)}, u32[]{:S(2)}, u32[]{:S(2)}) collective-permute-start(bf16[512,256]{0,1:T(8,128)(2,1)S(1)} %fusion.79), channel_id=1, source_target_pairs={{0,1},{7,6},{8,9},{15,14},{16,17},{23,22},{24,25},{31,30}} | collective-permute-start | bytes 786440 | tf_op jit(solution)/shard_map/ppermute | solution.py:281
  397.7 6.2 %collective-permute-done.91 = bf16[2,64,1024]{2,1,0:T(8,128)(2,1)S(1)} collective-permute-done((bf16[2,64,1024]{2,1,0:T(8,128)(2,1)S(1)}, bf16[2,64,1024]{2,1,0:T(8,128)(2,1)S(1)}, u32[]{:S(2)}, u32[]{:S(2)}) %collective-permute-start.91) | collective-permute-done | bytes 262176 | tf_op jit(solution)/shard_map/ppermute | solution.py:56
  412.1 12.3 %all_to_all.10 = bf16[8,12,2048]{2,1,0:T(8,128)(2,1)S(1)} all-to-all(bf16[8,12,2048]{2,1,0:T(8,128)(2,1)S(1)} %reshape.196), channel_id=1, replica_groups=mesh['ctx'=8,'mp'=4] {'ctx'}, dimensions={0} | all-to-all | bytes 786432 | tf_op jit(solution)/shard_map/all_to_all | solution.py:487
  (434 shorter events, 256.1 us)
Async XLA Ops:
  0.7 19.4 %collective-permute-start = (f32[1,64]{1,0:T(1,128)S(1)}, f32[1,64]{1,0:T(1,128)S(1)}, u32[]{:S(2)}, u32[]{:S(2)}) collective-permute-start(f32[1,64]{1,0:T(1,128)S(1)} %get-tuple-element.161), channel_id=1, source_target_pairs={{0,4},{4,0},{8,12},{12,8},{16,20},{20,16},{24,28},{28,24},{1,5},{5... | collective-permute-start | bytes 776 | tf_op jit(solution)/shard_map/ppermute | solution.py:56
  7.0 20.7 %all-to-all-start = ((bf16[8,12,2048]{2,1,0:T(8,128)(2,1)}), bf16[8,12,2048]{2,1,0:T(8,128)(2,1)S(1)}, u32[]{:S(2)}, u32[]{:S(2)}) async-start(bf16[8,12,2048]{2,1,0:T(8,128)(2,1)} %reshape.187), calls=%async_computation | async-start | bytes 1048576 | tf_op jit(solution)/shard_map/all_to_all | solution.py:368
  34.4 16.7 %collective-permute-start.6 = (bf16[64,1024]{1,0:T(8,128)(2,1)S(1)}, bf16[64,1024]{1,0:T(8,128)(2,1)S(1)}, u32[]{:S(2)}, u32[]{:S(2)}) collective-permute-start(bf16[64,1024]{1,0:T(8,128)(2,1)S(1)} %get-tuple-element.137), channel_id=1, source_target_pairs={{0,1},{1,9},{2,17},{3,25},{4,5},{5,13},{6,21},{7,29},{8,0},{9,8},{... | collective-permute-start | bytes 393224 | tf_op jit(solution)/shard_map/ppermute | solution.py:139
  34.9 17.3 %collective-permute-start.4 = (bf16[64,1024]{1,0:T(8,128)(2,1)S(1)}, bf16[64,1024]{1,0:T(8,128)(2,1)S(1)}, u32[]{:S(2)}, u32[]{:S(2)}) collective-permute-start(bf16[64,1024]{1,0:T(8,128)(2,1)S(1)} %get-tuple-element.137), channel_id=1, source_target_pairs={{0,0},{1,8},{2,16},{3,24},{4,4},{5,12},{6,20},{7,28},{8,1},{9,9},{... | collective-permute-start | bytes 393224 | tf_op jit(solution)/shard_map/ppermute | solution.py:139
  35.5 15.4 %collective-permute-start.7 = (bf16[64,1024]{1,0:T(8,128)(2,1)S(1)}, bf16[64,1024]{1,0:T(8,128)(2,1)S(1)}, u32[]{:S(2)}, u32[]{:S(2)}) collective-permute-start(bf16[64,1024]{1,0:T(8,128)(2,1)S(1)} %get-tuple-element.138), channel_id=1, source_target_pairs={{0,6},{1,14},{2,22},{3,30},{4,2},{5,10},{6,18},{7,26},{8,7},{9,15}... | collective-permute-start | bytes 393224 | tf_op jit(solution)/shard_map/ppermute | solution.py:139
  54.5 19.0 %collective-permute-start.11 = (bf16[512,768]{1,0:T(8,128)(2,1)S(1)}, bf16[512,768]{1,0:T(8,128)(2,1)S(1)}, u32[]{:S(2)}, u32[]{:S(2)}) collective-permute-start(bf16[512,768]{1,0:T(8,128)(2,1)S(1)} %convolution_convert_fusion.2), channel_id=1, source_target_pairs={{0,4},{4,0},{8,12},{12,8},{16,20},{20,16},{24,28},{28,24},{1,5},{5... | collective-permute-start | bytes 2359304 | tf_op jit(solution)/shard_map/ppermute | solution.py:56
  107.6 17.7 %collective-permute-start.33 = (bf16[64,1024]{1,0:T(8,128)(2,1)S(1)}, bf16[64,1024]{1,0:T(8,128)(2,1)S(1)}, u32[]{:S(2)}, u32[]{:S(2)}) collective-permute-start(bf16[64,1024]{1,0:T(8,128)(2,1)S(1)} %get-tuple-element.76), channel_id=1, source_target_pairs={{0,28},{4,24},{8,20},{12,16},{16,12},{20,8},{24,4},{28,0},{1,29},{... | collective-permute-start | bytes 393224 | tf_op jit(solution)/shard_map/ppermute | solution.py:56
  108.8 16.5 %collective-permute-start.32 = (bf16[64,1024]{1,0:T(8,128)(2,1)S(1)}, bf16[64,1024]{1,0:T(8,128)(2,1)S(1)}, u32[]{:S(2)}, u32[]{:S(2)}) collective-permute-start(bf16[64,1024]{1,0:T(8,128)(2,1)S(1)} %get-tuple-element.77), channel_id=1, source_target_pairs={{0,24},{4,28},{8,16},{12,20},{16,8},{20,12},{24,0},{28,4},{1,25},{... | collective-permute-start | bytes 393224 | tf_op jit(solution)/shard_map/ppermute | solution.py:56
  110.5 14.8 %collective-permute-start.31 = (bf16[64,1024]{1,0:T(8,128)(2,1)S(1)}, bf16[64,1024]{1,0:T(8,128)(2,1)S(1)}, u32[]{:S(2)}, u32[]{:S(2)}) collective-permute-start(bf16[64,1024]{1,0:T(8,128)(2,1)S(1)} %get-tuple-element.78), channel_id=1, source_target_pairs={{0,20},{4,16},{8,28},{12,24},{16,4},{20,0},{24,12},{28,8},{1,21},{... | collective-permute-start | bytes 393224 | tf_op jit(solution)/shard_map/ppermute | solution.py:56
  126.5 14.3 %collective-permute-start.36 = (bf16[2,64,1024]{2,1,0:T(8,128)(2,1)S(1)}, bf16[2,64,1024]{2,1,0:T(8,128)(2,1)S(1)}, u32[]{:S(2)}, u32[]{:S(2)}) collective-permute-start(bf16[2,64,1024]{2,1,0:T(8,128)(2,1)S(1)} %get-tuple-element.74), channel_id=1, source_target_pairs={{0,3},{1,0},{2,1},{3,2},{4,7},{5,4},{6,5},{7,6},{8,11},{9,8},{10,9... | collective-permute-start | bytes 786440 | tf_op jit(solution)/shard_map/ppermute | solution.py:63
  129.3 21.7 %collective-permute-start.35 = (bf16[2,64,1024]{2,1,0:T(8,128)(2,1)S(1)}, bf16[2,64,1024]{2,1,0:T(8,128)(2,1)S(1)}, u32[]{:S(2)}, u32[]{:S(2)}) collective-permute-start(bf16[2,64,1024]{2,1,0:T(8,128)(2,1)S(1)} %get-tuple-element.75), channel_id=1, source_target_pairs={{0,2},{1,3},{2,0},{3,1},{4,6},{5,7},{6,4},{7,5},{8,10},{9,11},{10,... | collective-permute-start | bytes 786440 | tf_op jit(solution)/shard_map/ppermute | solution.py:63
  209.0 15.3 %collective-permute-start.48 = (bf16[512,512]{0,1:T(8,128)(2,1)S(1)}, bf16[512,512]{0,1:T(8,128)(2,1)S(1)}, u32[]{:S(2)}, u32[]{:S(2)}) collective-permute-start(bf16[512,512]{0,1:T(8,128)(2,1)S(1)} %select_select_fusion.1), channel_id=1, source_target_pairs={{3,2},{2,1},{1,0},{4,5},{5,6},{6,7},{11,10},{10,9},{9,8},{12,13},{... | collective-permute-start | bytes 1572872 | tf_op jit(solution)/shard_map/ppermute | solution.py:267
  241.7 15.1 %collective-permute-start.66 = (bf16[512,512]{0,1:T(8,128)(2,1)S(1)}, bf16[512,512]{0,1:T(8,128)(2,1)S(1)}, u32[]{:S(2)}, u32[]{:S(2)}) collective-permute-start(bf16[512,512]{0,1:T(8,128)(2,1)S(1)} %get-tuple-element.121), channel_id=1, source_target_pairs={{3,2},{2,1},{1,0},{4,5},{5,6},{6,7},{11,10},{10,9},{9,8},{12,13},{... | collective-permute-start | bytes 1572872 | tf_op jit(solution)/shard_map/ppermute | solution.py:267
  248.3 18.9 %collective-permute-start.56 = (bf16[512,256]{0,1:T(8,128)(2,1)S(1)}, bf16[512,256]{0,1:T(8,128)(2,1)S(1)}, u32[]{:S(2)}, u32[]{:S(2)}) collective-permute-start(bf16[512,256]{0,1:T(8,128)(2,1)S(1)} %fusion.87), channel_id=1, source_target_pairs={{2,3},{1,2},{0,1},{5,4},{6,5},{7,6},{10,11},{9,10},{8,9},{13,12},{... | collective-permute-start | bytes 786440 | tf_op jit(solution)/shard_map/ppermute | solution.py:276
  252.0 14.8 %collective-permute-start.51 = (bf16[512,512]{0,1:T(8,128)(2,1)S(1)}, bf16[512,512]{0,1:T(8,128)(2,1)S(1)}, u32[]{:S(2)}, u32[]{:S(2)}) collective-permute-start(bf16[512,512]{0,1:T(8,128)(2,1)S(1)} %get-tuple-element.115), channel_id=1, source_target_pairs={{3,2},{2,1},{1,0},{4,5},{5,6},{6,7},{11,10},{10,9},{9,8},{12,13},{... | collective-permute-start | bytes 1572872 | tf_op jit(solution)/shard_map/ppermute | solution.py:267
  257.4 18.9 %collective-permute-start.72 = (bf16[512,256]{0,1:T(8,128)(2,1)S(1)}, bf16[512,256]{0,1:T(8,128)(2,1)S(1)}, u32[]{:S(2)}, u32[]{:S(2)}) collective-permute-start(bf16[512,256]{0,1:T(8,128)(2,1)S(1)} %get-tuple-element.25), channel_id=1, source_target_pairs={{2,3},{1,2},{0,1},{5,4},{6,5},{7,6},{10,11},{9,10},{8,9},{13,12},{... | collective-permute-start | bytes 786440 | tf_op jit(solution)/shard_map/ppermute | solution.py:276
  260.8 15.1 %collective-permute-start.67 = (bf16[512,512]{0,1:T(8,128)(2,1)S(1)}, bf16[512,512]{0,1:T(8,128)(2,1)S(1)}, u32[]{:S(2)}, u32[]{:S(2)}) collective-permute-start(bf16[512,512]{0,1:T(8,128)(2,1)S(1)} %get-tuple-element.119), channel_id=1, source_target_pairs={{3,2},{2,1},{1,0},{4,5},{5,6},{6,7},{11,10},{10,9},{9,8},{12,13},{... | collective-permute-start | bytes 1572872 | tf_op jit(solution)/shard_map/ppermute | solution.py:267
  267.4 17.6 %collective-permute-start.57 = (bf16[512,256]{0,1:T(8,128)(2,1)S(1)}, bf16[512,256]{0,1:T(8,128)(2,1)S(1)}, u32[]{:S(2)}, u32[]{:S(2)}) collective-permute-start(bf16[512,256]{0,1:T(8,128)(2,1)S(1)} %get-tuple-element.35), channel_id=1, source_target_pairs={{2,3},{1,2},{0,1},{5,4},{6,5},{7,6},{10,11},{9,10},{8,9},{13,12},{... | collective-permute-start | bytes 786440 | tf_op jit(solution)/shard_map/ppermute | solution.py:276
  276.5 17.0 %collective-permute-start.73 = (bf16[512,256]{0,1:T(8,128)(2,1)S(1)}, bf16[512,256]{0,1:T(8,128)(2,1)S(1)}, u32[]{:S(2)}, u32[]{:S(2)}) collective-permute-start(bf16[512,256]{0,1:T(8,128)(2,1)S(1)} %get-tuple-element.23), channel_id=1, source_target_pairs={{2,3},{1,2},{0,1},{5,4},{6,5},{7,6},{10,11},{9,10},{8,9},{13,12},{... | collective-permute-start | bytes 786440 | tf_op jit(solution)/shard_map/ppermute | solution.py:276
  285.2 16.7 %collective-permute-start.58 = (bf16[512,256]{0,1:T(8,128)(2,1)S(1)}, bf16[512,256]{0,1:T(8,128)(2,1)S(1)}, u32[]{:S(2)}, u32[]{:S(2)}) collective-permute-start(bf16[512,256]{0,1:T(8,128)(2,1)S(1)} %get-tuple-element.33), channel_id=1, source_target_pairs={{2,3},{1,2},{0,1},{5,4},{6,5},{7,6},{10,11},{9,10},{8,9},{13,12},{... | collective-permute-start | bytes 786440 | tf_op jit(solution)/shard_map/ppermute | solution.py:276
  293.6 16.7 %collective-permute-start.74 = (bf16[512,256]{0,1:T(8,128)(2,1)S(1)}, bf16[512,256]{0,1:T(8,128)(2,1)S(1)}, u32[]{:S(2)}, u32[]{:S(2)}) collective-permute-start(bf16[512,256]{0,1:T(8,128)(2,1)S(1)} %get-tuple-element.21), channel_id=1, source_target_pairs={{2,3},{1,2},{0,1},{5,4},{6,5},{7,6},{10,11},{9,10},{8,9},{13,12},{... | collective-permute-start | bytes 786440 | tf_op jit(solution)/shard_map/ppermute | solution.py:276
  302.1 16.6 %collective-permute-start.59 = (bf16[512,256]{0,1:T(8,128)(2,1)S(1)}, bf16[512,256]{0,1:T(8,128)(2,1)S(1)}, u32[]{:S(2)}, u32[]{:S(2)}) collective-permute-start(bf16[512,256]{0,1:T(8,128)(2,1)S(1)} %get-tuple-element.31), channel_id=1, source_target_pairs={{2,3},{1,2},{0,1},{5,4},{6,5},{7,6},{10,11},{9,10},{8,9},{13,12},{... | collective-permute-start | bytes 786440 | tf_op jit(solution)/shard_map/ppermute | solution.py:276
  310.6 16.5 %collective-permute-start.75 = (bf16[512,256]{0,1:T(8,128)(2,1)S(1)}, bf16[512,256]{0,1:T(8,128)(2,1)S(1)}, u32[]{:S(2)}, u32[]{:S(2)}) collective-permute-start(bf16[512,256]{0,1:T(8,128)(2,1)S(1)} %get-tuple-element.19), channel_id=1, source_target_pairs={{2,3},{1,2},{0,1},{5,4},{6,5},{7,6},{10,11},{9,10},{8,9},{13,12},{... | collective-permute-start | bytes 786440 | tf_op jit(solution)/shard_map/ppermute | solution.py:276
  319.0 17.2 %collective-permute-start.60 = (bf16[512,256]{0,1:T(8,128)(2,1)S(1)}, bf16[512,256]{0,1:T(8,128)(2,1)S(1)}, u32[]{:S(2)}, u32[]{:S(2)}) collective-permute-start(bf16[512,256]{0,1:T(8,128)(2,1)S(1)} %get-tuple-element.29), channel_id=1, source_target_pairs={{2,3},{1,2},{0,1},{5,4},{6,5},{7,6},{10,11},{9,10},{8,9},{13,12},{... | collective-permute-start | bytes 786440 | tf_op jit(solution)/shard_map/ppermute | solution.py:276
  327.3 15.0 %collective-permute-start.76 = (bf16[512,256]{0,1:T(8,128)(2,1)S(1)}, bf16[512,256]{0,1:T(8,128)(2,1)S(1)}, u32[]{:S(2)}, u32[]{:S(2)}) collective-permute-start(bf16[512,256]{0,1:T(8,128)(2,1)S(1)} %get-tuple-element.17), channel_id=1, source_target_pairs={{2,3},{1,2},{0,1},{5,4},{6,5},{7,6},{10,11},{9,10},{8,9},{13,12},{... | collective-permute-start | bytes 786440 | tf_op jit(solution)/shard_map/ppermute | solution.py:276
  339.7 15.5 %collective-permute-start.80 = (bf16[512,512]{0,1:T(8,128)(2,1)S(1)}, bf16[512,512]{0,1:T(8,128)(2,1)S(1)}, u32[]{:S(2)}, u32[]{:S(2)}) collective-permute-start(bf16[512,512]{0,1:T(8,128)(2,1)S(1)} %get-tuple-element.91), channel_id=1, source_target_pairs={{3,2},{2,1},{1,0},{4,5},{5,6},{6,7},{11,10},{10,9},{9,8},{12,13},{... | collective-permute-start | bytes 1572872 | tf_op jit(solution)/shard_map/ppermute | solution.py:267
  341.0 29.8 %collective-permute-start.84 = (bf16[512,512]{0,1:T(8,128)(2,1)S(1)}, bf16[512,512]{0,1:T(8,128)(2,1)S(1)}, u32[]{:S(2)}, u32[]{:S(2)}) collective-permute-start(bf16[512,512]{0,1:T(8,128)(2,1)S(1)} %get-tuple-element.89), channel_id=1, source_target_pairs={{3,2},{2,1},{1,0},{4,5},{5,6},{6,7},{11,10},{10,9},{9,8},{12,13},{... | collective-permute-start | bytes 1572872 | tf_op jit(solution)/shard_map/ppermute | solution.py:267
  342.4 21.1 %collective-permute-start.77 = (bf16[512,256]{0,1:T(8,128)(2,1)S(1)}, bf16[512,256]{0,1:T(8,128)(2,1)S(1)}, u32[]{:S(2)}, u32[]{:S(2)}) collective-permute-start(bf16[512,256]{0,1:T(8,128)(2,1)S(1)} %broadcast_select_fusion.4), channel_id=1, source_target_pairs={{2,3},{1,2},{0,1},{5,4},{6,5},{7,6},{10,11},{9,10},{8,9},{13,12},{... | collective-permute-start | bytes 786440 | tf_op jit(solution)/shard_map/ppermute | solution.py:276
  355.5 27.1 %collective-permute-start.83 = (bf16[512,256]{0,1:T(8,128)(2,1)S(1)}, bf16[512,256]{0,1:T(8,128)(2,1)S(1)}, u32[]{:S(2)}, u32[]{:S(2)}) collective-permute-start(bf16[512,256]{0,1:T(8,128)(2,1)S(1)} %fusion.80), channel_id=1, source_target_pairs={{0,1},{7,6},{8,9},{15,14},{16,17},{23,22},{24,25},{31,30}} | collective-permute-start | bytes 786440 | tf_op jit(solution)/shard_map/ppermute | solution.py:281
  358.8 25.1 %collective-permute-start.82 = (bf16[512,256]{0,1:T(8,128)(2,1)S(1)}, bf16[512,256]{0,1:T(8,128)(2,1)S(1)}, u32[]{:S(2)}, u32[]{:S(2)}) collective-permute-start(bf16[512,256]{0,1:T(8,128)(2,1)S(1)} %fusion.80), channel_id=1, source_target_pairs={{0,2},{7,5},{8,10},{15,13},{16,18},{23,21},{24,26},{31,29}} | collective-permute-start | bytes 786440 | tf_op jit(solution)/shard_map/ppermute | solution.py:281
  360.1 23.8 %collective-permute-start.81 = (bf16[512,256]{0,1:T(8,128)(2,1)S(1)}, bf16[512,256]{0,1:T(8,128)(2,1)S(1)}, u32[]{:S(2)}, u32[]{:S(2)}) collective-permute-start(bf16[512,256]{0,1:T(8,128)(2,1)S(1)} %fusion.80), channel_id=1, source_target_pairs={{0,3},{7,4},{8,11},{15,12},{16,19},{23,20},{24,27},{31,28}} | collective-permute-start | bytes 786440 | tf_op jit(solution)/shard_map/ppermute | solution.py:281
  364.1 16.5 %collective-permute-start.79 = (bf16[512,256]{0,1:T(8,128)(2,1)S(1)}, bf16[512,256]{0,1:T(8,128)(2,1)S(1)}, u32[]{:S(2)}, u32[]{:S(2)}) collective-permute-start(bf16[512,256]{0,1:T(8,128)(2,1)S(1)} %get-tuple-element.129), channel_id=1, source_target_pairs={{2,3},{1,2},{0,1},{5,4},{6,5},{7,6},{10,11},{9,10},{8,9},{13,12},{... | collective-permute-start | bytes 786440 | tf_op jit(solution)/shard_map/ppermute | solution.py:276
  (82 other events, 716.5 us)

commit v6 on v5

--- a/solution.py
+++ b/solution.py
@@ -233,15 +233,18 @@
     def choose(options):
         return lax.select_n(place, *options)
 
-    partial = {}
+    products = {}
 
     def part(k):
-        if k not in partial:
-            lo, hi = k * width, (k + 1) * width
-            g = jnp.dot(normed, gate_weight[:, lo:hi], preferred_element_type=F32)
-            u = jnp.dot(normed, up_weight[:, lo:hi], preferred_element_type=F32)
-            partial[k] = jnp.concatenate([g.astype(BF), u.astype(BF)], axis=1)
-        return partial[k]
+        first = k - k % streams
+        if first not in products:
+            lo, hi = first * width, min(first + streams, count) * width
+            g = jnp.dot(normed, gate_weight[:, lo:hi], preferred_element_type=F32).astype(BF)
+            u = jnp.dot(normed, up_weight[:, lo:hi], preferred_element_type=F32).astype(BF)
+            products[first] = g, u
+        cols = slice((k - first) * width, (k - first + 1) * width)
+        g, u = products[first]
+        return jnp.concatenate([g[:, cols], u[:, cols]], axis=1)
 
     lists = [list(range(s, count, streams)) for s in range(streams)]
     got = [None] * streams

time: 432 us -> 433 us (level)
    dot_general x28 -> x14, matrix products: 32.5 us -> 33.3 us  [the longest x7 20.5 us: part(): jnp.dot(normed, gate_weight[:, lo:hi], preferred_element_type=F32)]
  transfers between devices with their start and end apart: 94 -> 94, of which waited for: 52 -> 52; matrix products, arithmetic and copies ran while one was open for 10% -> 9% of each run, Pallas kernels for 0% -> 0%
where the time goes in v6:
time: 433 us; the launch traced here: 429 us
  starting transfers between devices  173 us (40%)
  waiting for transfers between devices  150 us (35%)
  matrix products  53.9 us (12%)
  other arithmetic  25 us (6%)
  blocking collectives  12.3 us (3%)
  local copies, waits for them, and re-layouts  11.9 us (3%)
    ppermute x18, waiting for transfers between devices, feed_forward(): got[s] = lax.ppermute(send, ('ctx', 'mp'), inward)  62.1 us
    ppermute x16, starting transfers between devices, feed_forward(): passed[s] = lax.ppermute(send, ('ctx', 'mp'), outward)  56.8 us
    ppermute x39, waiting for transfers between devices, swap(): return lax.ppermute(x, 'ctx', [(i, i ^ b) for i in range(self.C)])  54.7 us
    ppermute x39, starting transfers between devices, swap(): return lax.ppermute(x, 'ctx', [(i, i ^ b) for i in range(self.C)])  45.5 us
    ppermute x18, starting transfers between devices, feed_forward(): got[s] = lax.ppermute(send, ('ctx', 'mp'), inward)  23.4 us
    ppermute x6, waiting for transfers between devices, rotate_mp(): lax.ppermute(block_for(s), 'mp', [(i, (i + s) % self.M) for i in range(se...  22.8 us
    ppermute x8, starting transfers between devices, rows_to_slices(): lax.ppermute(payload[r % self.H], ('ctx', 'mp'), self.flat(pairs))  22 us
    dot_general x7, matrix products, part(): jnp.dot(normed, gate_weight[:, lo:hi], preferred_element_type=F32)  20.5 us
  transfers between devices with their start and end apart: 94, of which 52 were waited for; matrix products, arithmetic and copies ran while one was open for 9% of the time, Pallas kernels for 0%

profile of v6, /device:TPU:0, one launch (start us, length us, event | category | flops | bytes accessed | tf_op | source)
XLA Modules:
  0.0 428.7 jit_solution(5159505046463469166)
XLA Ops:
  7.0 4.8 %all-to-all-start = ((bf16[8,12,2048]{2,1,0:T(8,128)(2,1)}), bf16[8,12,2048]{2,1,0:T(8,128)(2,1)S(1)}, u32[]{:S(2)}, u32[]{:S(2)}) async-start(bf16[8,12,2048]{2,1,0:T(8,128)(2,1)} %reshape.187), calls=%async_computation | async-start | bytes 1048576 | tf_op jit(solution)/shard_map/all_to_all | solution.py:371
  35.6 5.7 %collective-permute-start.7 = (bf16[64,1024]{1,0:T(8,128)(2,1)S(1)}, bf16[64,1024]{1,0:T(8,128)(2,1)S(1)}, u32[]{:S(2)}, u32[]{:S(2)}) collective-permute-start(bf16[64,1024]{1,0:T(8,128)(2,1)S(1)} %get-tuple-element.166), channel_id=1, source_target_pairs={{0,6},{1,14},{2,22},{3,30},{4,2},{5,10},{6,18},{7,26},{8,7},{9,15}... | collective-permute-start | bytes 393224 | tf_op jit(solution)/shard_map/ppermute | solution.py:139
  41.3 4.9 %collective-permute-start.5 = (bf16[64,1024]{1,0:T(8,128)(2,1)S(1)}, bf16[64,1024]{1,0:T(8,128)(2,1)S(1)}, u32[]{:S(2)}, u32[]{:S(2)}) collective-permute-start(bf16[64,1024]{1,0:T(8,128)(2,1)S(1)} %get-tuple-element.166), channel_id=1, source_target_pairs={{0,5},{1,13},{2,21},{3,29},{4,1},{5,9},{6,17},{7,25},{8,4},{9,12},... | collective-permute-start | bytes 393224 | tf_op jit(solution)/shard_map/ppermute | solution.py:139
  46.4 4.6 %collective-permute-start.3 = (bf16[64,1024]{1,0:T(8,128)(2,1)S(1)}, bf16[64,1024]{1,0:T(8,128)(2,1)S(1)}, u32[]{:S(2)}, u32[]{:S(2)}) collective-permute-start(bf16[64,1024]{1,0:T(8,128)(2,1)S(1)} %get-tuple-element.166), channel_id=1, source_target_pairs={{0,4},{1,12},{2,20},{3,28},{4,0},{5,8},{6,16},{7,24},{8,5},{9,13},... | collective-permute-start | bytes 393224 | tf_op jit(solution)/shard_map/ppermute | solution.py:139
  54.7 11.6 %collective-permute-start.17 = (f32[256]{0:T(256)S(1)}, f32[256]{0:T(256)S(1)}, u32[]{:S(2)}, u32[]{:S(2)}) collective-permute-start(f32[256]{0:T(256)S(1)} %get-tuple-element.181), channel_id=1, source_target_pairs={{0,16},{4,20},{8,24},{12,28},{16,0},{20,4},{24,8},{28,12},{1,17},{... | collective-permute-start | bytes 3080 | tf_op jit(solution)/shard_map/ppermute | solution.py:56
  113.2 6.5 %collective-permute-done.28 = bf16[64,1024]{1,0:T(8,128)(2,1)S(1)} collective-permute-done((bf16[64,1024]{1,0:T(8,128)(2,1)S(1)}, bf16[64,1024]{1,0:T(8,128)(2,1)S(1)}, u32[]{:S(2)}, u32[]{:S(2)}) %collective-permute-start.28) | collective-permute-done | bytes 131104 | tf_op jit(solution)/shard_map/ppermute | solution.py:56
  119.7 5.5 %collective-permute-done.29 = bf16[64,1024]{1,0:T(8,128)(2,1)S(1)} collective-permute-done((bf16[64,1024]{1,0:T(8,128)(2,1)S(1)}, bf16[64,1024]{1,0:T(8,128)(2,1)S(1)}, u32[]{:S(2)}, u32[]{:S(2)}) %collective-permute-start.29) | collective-permute-done | bytes 131104 | tf_op jit(solution)/shard_map/ppermute | solution.py:56
  130.0 6.4 %collective-permute-done.34 = bf16[2,64,1024]{2,1,0:T(8,128)(2,1)S(1)} collective-permute-done((bf16[2,64,1024]{2,1,0:T(8,128)(2,1)S(1)}, bf16[2,64,1024]{2,1,0:T(8,128)(2,1)S(1)}, u32[]{:S(2)}, u32[]{:S(2)}) %collective-permute-start.34) | collective-permute-done | bytes 262176 | tf_op jit(solution)/shard_map/ppermute | solution.py:63
  136.5 4.4 %collective-permute-done.36 = bf16[2,64,1024]{2,1,0:T(8,128)(2,1)S(1)} collective-permute-done((bf16[2,64,1024]{2,1,0:T(8,128)(2,1)S(1)}, bf16[2,64,1024]{2,1,0:T(8,128)(2,1)S(1)}, u32[]{:S(2)}, u32[]{:S(2)}) %collective-permute-start.36) | collective-permute-done | bytes 262176 | tf_op jit(solution)/shard_map/ppermute | solution.py:63
  140.9 10.1 %collective-permute-done.35 = bf16[2,64,1024]{2,1,0:T(8,128)(2,1)S(1)} collective-permute-done((bf16[2,64,1024]{2,1,0:T(8,128)(2,1)S(1)}, bf16[2,64,1024]{2,1,0:T(8,128)(2,1)S(1)}, u32[]{:S(2)}, u32[]{:S(2)}) %collective-permute-start.35) | collective-permute-done | bytes 262176 | tf_op jit(solution)/shard_map/ppermute | solution.py:63
  212.2 8.3 %collective-permute-done.63 = bf16[512,512]{0,1:T(8,128)(2,1)S(1)} collective-permute-done((bf16[512,512]{0,1:T(8,128)(2,1)S(1)}, bf16[512,512]{0,1:T(8,128)(2,1)S(1)}, u32[]{:S(2)}, u32[]{:S(2)}) %collective-permute-start.63) | collective-permute-done | bytes 524320 | tf_op jit(solution)/shard_map/ppermute | solution.py:270
  222.0 4.1 collective-permute-done.48
  227.6 4.1 collective-permute-done.64
  233.4 4.0 collective-permute-done.49
  239.0 4.1 collective-permute-done.65
  245.0 4.6 %collective-permute-start.71 = (bf16[512,256]{0,1:T(8,128)(2,1)S(1)}, bf16[512,256]{0,1:T(8,128)(2,1)S(1)}, u32[]{:S(2)}, u32[]{:S(2)}) collective-permute-start(bf16[512,256]{0,1:T(8,128)(2,1)S(1)} %fusion.123), channel_id=1, source_target_pairs={{2,3},{1,2},{0,1},{5,4},{6,5},{7,6},{10,11},{9,10},{8,9},{13,12},{... | collective-permute-start | bytes 786440 | tf_op jit(solution)/shard_map/ppermute | solution.py:279
  254.9 3.7 collective-permute-done.66
  264.0 4.6 %collective-permute-done.51 = bf16[512,512]{0,1:T(8,128)(2,1)S(1)} collective-permute-done((bf16[512,512]{0,1:T(8,128)(2,1)S(1)}, bf16[512,512]{0,1:T(8,128)(2,1)S(1)}, u32[]{:S(2)}, u32[]{:S(2)}) %collective-permute-start.51) | collective-permute-done | bytes 524320 | tf_op jit(solution)/shard_map/ppermute | solution.py:270
  274.0 3.7 collective-permute-done.67
  278.3 3.9 collective-permute-start.73
  287.0 3.7 collective-permute-start.58
  295.4 3.7 collective-permute-start.74
  303.9 3.7 collective-permute-start.59
  312.3 3.7 collective-permute-start.75
  320.8 3.7 collective-permute-start.60
  329.1 4.0 collective-permute-start.76
  333.1 4.6 %collective-permute-done.55 = bf16[512,512]{0,1:T(8,128)(2,1)S(1)} collective-permute-done((bf16[512,512]{0,1:T(8,128)(2,1)S(1)}, bf16[512,512]{0,1:T(8,128)(2,1)S(1)}, u32[]{:S(2)}, u32[]{:S(2)}) %collective-permute-start.55) | collective-permute-done | bytes 524320 | tf_op jit(solution)/shard_map/ppermute | solution.py:270
  344.2 5.2 %collective-permute-start.77 = (bf16[512,256]{0,1:T(8,128)(2,1)S(1)}, bf16[512,256]{0,1:T(8,128)(2,1)S(1)}, u32[]{:S(2)}, u32[]{:S(2)}) collective-permute-start(bf16[512,256]{0,1:T(8,128)(2,1)S(1)} %broadcast_select_fusion.4), channel_id=1, source_target_pairs={{2,3},{1,2},{0,1},{5,4},{6,5},{7,6},{10,11},{9,10},{8,9},{13,12},{... | collective-permute-start | bytes 786440 | tf_op jit(solution)/shard_map/ppermute | solution.py:279
  349.4 3.9 collective-permute-start.62
  377.9 4.4 %collective-permute-start.87 = (bf16[512,256]{0,1:T(8,128)(2,1)S(1)}, bf16[512,256]{0,1:T(8,128)(2,1)S(1)}, u32[]{:S(2)}, u32[]{:S(2)}) collective-permute-start(bf16[512,256]{0,1:T(8,128)(2,1)S(1)} %fusion.121), channel_id=1, source_target_pairs={{0,1},{7,6},{8,9},{15,14},{16,17},{23,22},{24,25},{31,30}} | collective-permute-start | bytes 786440 | tf_op jit(solution)/shard_map/ppermute | solution.py:284
  399.6 6.2 %collective-permute-done.91 = bf16[2,64,1024]{2,1,0:T(8,128)(2,1)S(1)} collective-permute-done((bf16[2,64,1024]{2,1,0:T(8,128)(2,1)S(1)}, bf16[2,64,1024]{2,1,0:T(8,128)(2,1)S(1)}, u32[]{:S(2)}, u32[]{:S(2)}) %collective-permute-start.91) | collective-permute-done | bytes 262176 | tf_op jit(solution)/shard_map/ppermute | solution.py:56
  414.0 12.3 %all_to_all.10 = bf16[8,12,2048]{2,1,0:T(8,128)(2,1)S(1)} all-to-all(bf16[8,12,2048]{2,1,0:T(8,128)(2,1)S(1)} %reshape.196), channel_id=1, replica_groups=mesh['ctx'=8,'mp'=4] {'ctx'}, dimensions={0} | all-to-all | bytes 786432 | tf_op jit(solution)/shard_map/all_to_all | solution.py:490
  (425 shorter events, 257.5 us)
Async XLA Ops:
  0.7 19.4 %collective-permute-start = (f32[1,64]{1,0:T(1,128)S(1)}, f32[1,64]{1,0:T(1,128)S(1)}, u32[]{:S(2)}, u32[]{:S(2)}) collective-permute-start(f32[1,64]{1,0:T(1,128)S(1)} %get-tuple-element.189), channel_id=1, source_target_pairs={{0,4},{4,0},{8,12},{12,8},{16,20},{20,16},{24,28},{28,24},{1,5},{5... | collective-permute-start | bytes 776 | tf_op jit(solution)/shard_map/ppermute | solution.py:56
  7.0 20.8 %all-to-all-start = ((bf16[8,12,2048]{2,1,0:T(8,128)(2,1)}), bf16[8,12,2048]{2,1,0:T(8,128)(2,1)S(1)}, u32[]{:S(2)}, u32[]{:S(2)}) async-start(bf16[8,12,2048]{2,1,0:T(8,128)(2,1)} %reshape.187), calls=%async_computation | async-start | bytes 1048576 | tf_op jit(solution)/shard_map/all_to_all | solution.py:371
  34.5 16.7 %collective-permute-start.6 = (bf16[64,1024]{1,0:T(8,128)(2,1)S(1)}, bf16[64,1024]{1,0:T(8,128)(2,1)S(1)}, u32[]{:S(2)}, u32[]{:S(2)}) collective-permute-start(bf16[64,1024]{1,0:T(8,128)(2,1)S(1)} %get-tuple-element.165), channel_id=1, source_target_pairs={{0,1},{1,9},{2,17},{3,25},{4,5},{5,13},{6,21},{7,29},{8,0},{9,8},{... | collective-permute-start | bytes 393224 | tf_op jit(solution)/shard_map/ppermute | solution.py:139
  34.9 17.2 %collective-permute-start.4 = (bf16[64,1024]{1,0:T(8,128)(2,1)S(1)}, bf16[64,1024]{1,0:T(8,128)(2,1)S(1)}, u32[]{:S(2)}, u32[]{:S(2)}) collective-permute-start(bf16[64,1024]{1,0:T(8,128)(2,1)S(1)} %get-tuple-element.165), channel_id=1, source_target_pairs={{0,0},{1,8},{2,16},{3,24},{4,4},{5,12},{6,20},{7,28},{8,1},{9,9},{... | collective-permute-start | bytes 393224 | tf_op jit(solution)/shard_map/ppermute | solution.py:139
  35.6 15.4 %collective-permute-start.7 = (bf16[64,1024]{1,0:T(8,128)(2,1)S(1)}, bf16[64,1024]{1,0:T(8,128)(2,1)S(1)}, u32[]{:S(2)}, u32[]{:S(2)}) collective-permute-start(bf16[64,1024]{1,0:T(8,128)(2,1)S(1)} %get-tuple-element.166), channel_id=1, source_target_pairs={{0,6},{1,14},{2,22},{3,30},{4,2},{5,10},{6,18},{7,26},{8,7},{9,15}... | collective-permute-start | bytes 393224 | tf_op jit(solution)/shard_map/ppermute | solution.py:139
  54.5 19.0 %collective-permute-start.11 = (bf16[512,768]{1,0:T(8,128)(2,1)S(1)}, bf16[512,768]{1,0:T(8,128)(2,1)S(1)}, u32[]{:S(2)}, u32[]{:S(2)}) collective-permute-start(bf16[512,768]{1,0:T(8,128)(2,1)S(1)} %convolution_convert_fusion.2), channel_id=1, source_target_pairs={{0,4},{4,0},{8,12},{12,8},{16,20},{20,16},{24,28},{28,24},{1,5},{5... | collective-permute-start | bytes 2359304 | tf_op jit(solution)/shard_map/ppermute | solution.py:56
  107.6 17.7 %collective-permute-start.33 = (bf16[64,1024]{1,0:T(8,128)(2,1)S(1)}, bf16[64,1024]{1,0:T(8,128)(2,1)S(1)}, u32[]{:S(2)}, u32[]{:S(2)}) collective-permute-start(bf16[64,1024]{1,0:T(8,128)(2,1)S(1)} %get-tuple-element.76), channel_id=1, source_target_pairs={{0,28},{4,24},{8,20},{12,16},{16,12},{20,8},{24,4},{28,0},{1,29},{... | collective-permute-start | bytes 393224 | tf_op jit(solution)/shard_map/ppermute | solution.py:56
  108.8 16.5 %collective-permute-start.32 = (bf16[64,1024]{1,0:T(8,128)(2,1)S(1)}, bf16[64,1024]{1,0:T(8,128)(2,1)S(1)}, u32[]{:S(2)}, u32[]{:S(2)}) collective-permute-start(bf16[64,1024]{1,0:T(8,128)(2,1)S(1)} %get-tuple-element.77), channel_id=1, source_target_pairs={{0,24},{4,28},{8,16},{12,20},{16,8},{20,12},{24,0},{28,4},{1,25},{... | collective-permute-start | bytes 393224 | tf_op jit(solution)/shard_map/ppermute | solution.py:56
  110.5 14.8 %collective-permute-start.31 = (bf16[64,1024]{1,0:T(8,128)(2,1)S(1)}, bf16[64,1024]{1,0:T(8,128)(2,1)S(1)}, u32[]{:S(2)}, u32[]{:S(2)}) collective-permute-start(bf16[64,1024]{1,0:T(8,128)(2,1)S(1)} %get-tuple-element.78), channel_id=1, source_target_pairs={{0,20},{4,16},{8,28},{12,24},{16,4},{20,0},{24,12},{28,8},{1,21},{... | collective-permute-start | bytes 393224 | tf_op jit(solution)/shard_map/ppermute | solution.py:56
  126.6 14.3 %collective-permute-start.36 = (bf16[2,64,1024]{2,1,0:T(8,128)(2,1)S(1)}, bf16[2,64,1024]{2,1,0:T(8,128)(2,1)S(1)}, u32[]{:S(2)}, u32[]{:S(2)}) collective-permute-start(bf16[2,64,1024]{2,1,0:T(8,128)(2,1)S(1)} %get-tuple-element.74), channel_id=1, source_target_pairs={{0,3},{1,0},{2,1},{3,2},{4,7},{5,4},{6,5},{7,6},{8,11},{9,8},{10,9... | collective-permute-start | bytes 786440 | tf_op jit(solution)/shard_map/ppermute | solution.py:63
  129.3 21.7 %collective-permute-start.35 = (bf16[2,64,1024]{2,1,0:T(8,128)(2,1)S(1)}, bf16[2,64,1024]{2,1,0:T(8,128)(2,1)S(1)}, u32[]{:S(2)}, u32[]{:S(2)}) collective-permute-start(bf16[2,64,1024]{2,1,0:T(8,128)(2,1)S(1)} %get-tuple-element.75), channel_id=1, source_target_pairs={{0,2},{1,3},{2,0},{3,1},{4,6},{5,7},{6,4},{7,5},{8,10},{9,11},{10,... | collective-permute-start | bytes 786440 | tf_op jit(solution)/shard_map/ppermute | solution.py:63
  210.8 15.3 %collective-permute-start.48 = (bf16[512,512]{0,1:T(8,128)(2,1)S(1)}, bf16[512,512]{0,1:T(8,128)(2,1)S(1)}, u32[]{:S(2)}, u32[]{:S(2)}) collective-permute-start(bf16[512,512]{0,1:T(8,128)(2,1)S(1)} %select_select_fusion.1), channel_id=1, source_target_pairs={{3,2},{2,1},{1,0},{4,5},{5,6},{6,7},{11,10},{10,9},{9,8},{12,13},{... | collective-permute-start | bytes 1572872 | tf_op jit(solution)/shard_map/ppermute | solution.py:270
  243.5 15.1 %collective-permute-start.66 = (bf16[512,512]{0,1:T(8,128)(2,1)S(1)}, bf16[512,512]{0,1:T(8,128)(2,1)S(1)}, u32[]{:S(2)}, u32[]{:S(2)}) collective-permute-start(bf16[512,512]{0,1:T(8,128)(2,1)S(1)} %get-tuple-element.149), channel_id=1, source_target_pairs={{3,2},{2,1},{1,0},{4,5},{5,6},{6,7},{11,10},{10,9},{9,8},{12,13},{... | collective-permute-start | bytes 1572872 | tf_op jit(solution)/shard_map/ppermute | solution.py:270
  250.1 18.9 %collective-permute-start.56 = (bf16[512,256]{0,1:T(8,128)(2,1)S(1)}, bf16[512,256]{0,1:T(8,128)(2,1)S(1)}, u32[]{:S(2)}, u32[]{:S(2)}) collective-permute-start(bf16[512,256]{0,1:T(8,128)(2,1)S(1)} %fusion.129), channel_id=1, source_target_pairs={{2,3},{1,2},{0,1},{5,4},{6,5},{7,6},{10,11},{9,10},{8,9},{13,12},{... | collective-permute-start | bytes 786440 | tf_op jit(solution)/shard_map/ppermute | solution.py:279
  253.6 15.0 %collective-permute-start.51 = (bf16[512,512]{0,1:T(8,128)(2,1)S(1)}, bf16[512,512]{0,1:T(8,128)(2,1)S(1)}, u32[]{:S(2)}, u32[]{:S(2)}) collective-permute-start(bf16[512,512]{0,1:T(8,128)(2,1)S(1)} %get-tuple-element.127), channel_id=1, source_target_pairs={{3,2},{2,1},{1,0},{4,5},{5,6},{6,7},{11,10},{10,9},{9,8},{12,13},{... | collective-permute-start | bytes 1572872 | tf_op jit(solution)/shard_map/ppermute | solution.py:270
  259.2 18.9 %collective-permute-start.72 = (bf16[512,256]{0,1:T(8,128)(2,1)S(1)}, bf16[512,256]{0,1:T(8,128)(2,1)S(1)}, u32[]{:S(2)}, u32[]{:S(2)}) collective-permute-start(bf16[512,256]{0,1:T(8,128)(2,1)S(1)} %get-tuple-element.25), channel_id=1, source_target_pairs={{2,3},{1,2},{0,1},{5,4},{6,5},{7,6},{10,11},{9,10},{8,9},{13,12},{... | collective-permute-start | bytes 786440 | tf_op jit(solution)/shard_map/ppermute | solution.py:279
  262.6 15.1 %collective-permute-start.67 = (bf16[512,512]{0,1:T(8,128)(2,1)S(1)}, bf16[512,512]{0,1:T(8,128)(2,1)S(1)}, u32[]{:S(2)}, u32[]{:S(2)}) collective-permute-start(bf16[512,512]{0,1:T(8,128)(2,1)S(1)} %get-tuple-element.147), channel_id=1, source_target_pairs={{3,2},{2,1},{1,0},{4,5},{5,6},{6,7},{11,10},{10,9},{9,8},{12,13},{... | collective-permute-start | bytes 1572872 | tf_op jit(solution)/shard_map/ppermute | solution.py:270
  269.2 17.6 %collective-permute-start.57 = (bf16[512,256]{0,1:T(8,128)(2,1)S(1)}, bf16[512,256]{0,1:T(8,128)(2,1)S(1)}, u32[]{:S(2)}, u32[]{:S(2)}) collective-permute-start(bf16[512,256]{0,1:T(8,128)(2,1)S(1)} %get-tuple-element.35), channel_id=1, source_target_pairs={{2,3},{1,2},{0,1},{5,4},{6,5},{7,6},{10,11},{9,10},{8,9},{13,12},{... | collective-permute-start | bytes 786440 | tf_op jit(solution)/shard_map/ppermute | solution.py:279
  278.3 17.0 %collective-permute-start.73 = (bf16[512,256]{0,1:T(8,128)(2,1)S(1)}, bf16[512,256]{0,1:T(8,128)(2,1)S(1)}, u32[]{:S(2)}, u32[]{:S(2)}) collective-permute-start(bf16[512,256]{0,1:T(8,128)(2,1)S(1)} %get-tuple-element.23), channel_id=1, source_target_pairs={{2,3},{1,2},{0,1},{5,4},{6,5},{7,6},{10,11},{9,10},{8,9},{13,12},{... | collective-permute-start | bytes 786440 | tf_op jit(solution)/shard_map/ppermute | solution.py:279
  287.0 16.7 %collective-permute-start.58 = (bf16[512,256]{0,1:T(8,128)(2,1)S(1)}, bf16[512,256]{0,1:T(8,128)(2,1)S(1)}, u32[]{:S(2)}, u32[]{:S(2)}) collective-permute-start(bf16[512,256]{0,1:T(8,128)(2,1)S(1)} %get-tuple-element.33), channel_id=1, source_target_pairs={{2,3},{1,2},{0,1},{5,4},{6,5},{7,6},{10,11},{9,10},{8,9},{13,12},{... | collective-permute-start | bytes 786440 | tf_op jit(solution)/shard_map/ppermute | solution.py:279
  295.4 16.7 %collective-permute-start.74 = (bf16[512,256]{0,1:T(8,128)(2,1)S(1)}, bf16[512,256]{0,1:T(8,128)(2,1)S(1)}, u32[]{:S(2)}, u32[]{:S(2)}) collective-permute-start(bf16[512,256]{0,1:T(8,128)(2,1)S(1)} %get-tuple-element.21), channel_id=1, source_target_pairs={{2,3},{1,2},{0,1},{5,4},{6,5},{7,6},{10,11},{9,10},{8,9},{13,12},{... | collective-permute-start | bytes 786440 | tf_op jit(solution)/shard_map/ppermute | solution.py:279
  303.9 16.6 %collective-permute-start.59 = (bf16[512,256]{0,1:T(8,128)(2,1)S(1)}, bf16[512,256]{0,1:T(8,128)(2,1)S(1)}, u32[]{:S(2)}, u32[]{:S(2)}) collective-permute-start(bf16[512,256]{0,1:T(8,128)(2,1)S(1)} %get-tuple-element.31), channel_id=1, source_target_pairs={{2,3},{1,2},{0,1},{5,4},{6,5},{7,6},{10,11},{9,10},{8,9},{13,12},{... | collective-permute-start | bytes 786440 | tf_op jit(solution)/shard_map/ppermute | solution.py:279
  312.3 16.5 %collective-permute-start.75 = (bf16[512,256]{0,1:T(8,128)(2,1)S(1)}, bf16[512,256]{0,1:T(8,128)(2,1)S(1)}, u32[]{:S(2)}, u32[]{:S(2)}) collective-permute-start(bf16[512,256]{0,1:T(8,128)(2,1)S(1)} %get-tuple-element.19), channel_id=1, source_target_pairs={{2,3},{1,2},{0,1},{5,4},{6,5},{7,6},{10,11},{9,10},{8,9},{13,12},{... | collective-permute-start | bytes 786440 | tf_op jit(solution)/shard_map/ppermute | solution.py:279
  320.8 17.2 %collective-permute-start.60 = (bf16[512,256]{0,1:T(8,128)(2,1)S(1)}, bf16[512,256]{0,1:T(8,128)(2,1)S(1)}, u32[]{:S(2)}, u32[]{:S(2)}) collective-permute-start(bf16[512,256]{0,1:T(8,128)(2,1)S(1)} %get-tuple-element.29), channel_id=1, source_target_pairs={{2,3},{1,2},{0,1},{5,4},{6,5},{7,6},{10,11},{9,10},{8,9},{13,12},{... | collective-permute-start | bytes 786440 | tf_op jit(solution)/shard_map/ppermute | solution.py:279
  329.1 15.1 %collective-permute-start.76 = (bf16[512,256]{0,1:T(8,128)(2,1)S(1)}, bf16[512,256]{0,1:T(8,128)(2,1)S(1)}, u32[]{:S(2)}, u32[]{:S(2)}) collective-permute-start(bf16[512,256]{0,1:T(8,128)(2,1)S(1)} %get-tuple-element.17), channel_id=1, source_target_pairs={{2,3},{1,2},{0,1},{5,4},{6,5},{7,6},{10,11},{9,10},{8,9},{13,12},{... | collective-permute-start | bytes 786440 | tf_op jit(solution)/shard_map/ppermute | solution.py:279
  341.5 15.4 %collective-permute-start.80 = (bf16[512,512]{0,1:T(8,128)(2,1)S(1)}, bf16[512,512]{0,1:T(8,128)(2,1)S(1)}, u32[]{:S(2)}, u32[]{:S(2)}) collective-permute-start(bf16[512,512]{0,1:T(8,128)(2,1)S(1)} %get-tuple-element.91), channel_id=1, source_target_pairs={{3,2},{2,1},{1,0},{4,5},{5,6},{6,7},{11,10},{10,9},{9,8},{12,13},{... | collective-permute-start | bytes 1572872 | tf_op jit(solution)/shard_map/ppermute | solution.py:270
  342.8 29.9 %collective-permute-start.84 = (bf16[512,512]{0,1:T(8,128)(2,1)S(1)}, bf16[512,512]{0,1:T(8,128)(2,1)S(1)}, u32[]{:S(2)}, u32[]{:S(2)}) collective-permute-start(bf16[512,512]{0,1:T(8,128)(2,1)S(1)} %get-tuple-element.89), channel_id=1, source_target_pairs={{3,2},{2,1},{1,0},{4,5},{5,6},{6,7},{11,10},{10,9},{9,8},{12,13},{... | collective-permute-start | bytes 1572872 | tf_op jit(solution)/shard_map/ppermute | solution.py:270
  344.2 21.0 %collective-permute-start.77 = (bf16[512,256]{0,1:T(8,128)(2,1)S(1)}, bf16[512,256]{0,1:T(8,128)(2,1)S(1)}, u32[]{:S(2)}, u32[]{:S(2)}) collective-permute-start(bf16[512,256]{0,1:T(8,128)(2,1)S(1)} %broadcast_select_fusion.4), channel_id=1, source_target_pairs={{2,3},{1,2},{0,1},{5,4},{6,5},{7,6},{10,11},{9,10},{8,9},{13,12},{... | collective-permute-start | bytes 786440 | tf_op jit(solution)/shard_map/ppermute | solution.py:279
  357.3 27.2 %collective-permute-start.83 = (bf16[512,256]{0,1:T(8,128)(2,1)S(1)}, bf16[512,256]{0,1:T(8,128)(2,1)S(1)}, u32[]{:S(2)}, u32[]{:S(2)}) collective-permute-start(bf16[512,256]{0,1:T(8,128)(2,1)S(1)} %fusion.122), channel_id=1, source_target_pairs={{0,1},{7,6},{8,9},{15,14},{16,17},{23,22},{24,25},{31,30}} | collective-permute-start | bytes 786440 | tf_op jit(solution)/shard_map/ppermute | solution.py:284
  360.6 25.2 %collective-permute-start.82 = (bf16[512,256]{0,1:T(8,128)(2,1)S(1)}, bf16[512,256]{0,1:T(8,128)(2,1)S(1)}, u32[]{:S(2)}, u32[]{:S(2)}) collective-permute-start(bf16[512,256]{0,1:T(8,128)(2,1)S(1)} %fusion.122), channel_id=1, source_target_pairs={{0,2},{7,5},{8,10},{15,13},{16,18},{23,21},{24,26},{31,29}} | collective-permute-start | bytes 786440 | tf_op jit(solution)/shard_map/ppermute | solution.py:284
  361.9 23.9 %collective-permute-start.81 = (bf16[512,256]{0,1:T(8,128)(2,1)S(1)}, bf16[512,256]{0,1:T(8,128)(2,1)S(1)}, u32[]{:S(2)}, u32[]{:S(2)}) collective-permute-start(bf16[512,256]{0,1:T(8,128)(2,1)S(1)} %fusion.122), channel_id=1, source_target_pairs={{0,3},{7,4},{8,11},{15,12},{16,19},{23,20},{24,27},{31,28}} | collective-permute-start | bytes 786440 | tf_op jit(solution)/shard_map/ppermute | solution.py:284
  365.9 16.6 %collective-permute-start.79 = (bf16[512,256]{0,1:T(8,128)(2,1)S(1)}, bf16[512,256]{0,1:T(8,128)(2,1)S(1)}, u32[]{:S(2)}, u32[]{:S(2)}) collective-permute-start(bf16[512,256]{0,1:T(8,128)(2,1)S(1)} %get-tuple-element.157), channel_id=1, source_target_pairs={{2,3},{1,2},{0,1},{5,4},{6,5},{7,6},{10,11},{9,10},{8,9},{13,12},{... | collective-permute-start | bytes 786440 | tf_op jit(solution)/shard_map/ppermute | solution.py:279
  (78 other events, 672.7 us)

commit v7 on v6

--- a/solution.py
+++ b/solution.py
@@ -236,9 +236,10 @@
     products = {}
 
     def part(k):
-        first = k - k % streams
+        alone = k < streams
+        first = k if alone else k - k % streams
         if first not in products:
-            lo, hi = first * width, min(first + streams, count) * width
+            lo, hi = first * width, min(first + (1 if alone else streams), count) * width
             g = jnp.dot(normed, gate_weight[:, lo:hi], preferred_element_type=F32).astype(BF)
             u = jnp.dot(normed, up_weight[:, lo:hi], preferred_element_type=F32).astype(BF)
             products[first] = g, u

time: 433 us -> 436 us (level)
    dot_general x7 -> x8, matrix products: 20.5 us -> 21.8 us  [part(): jnp.dot(normed, gate_weight[:, lo:hi], preferred_element_type=F32)]
    dot_general x7 -> x8, matrix products: 12.8 us -> 13.7 us  [part(): jnp.dot(normed, up_weight[:, lo:hi], preferred_element_type=F32).astype(BF)]
where the time goes in v7:
time: 436 us; the launch traced here: 431 us
  starting transfers between devices  174 us (40%)
  waiting for transfers between devices  150 us (34%)
  matrix products  56.1 us (13%)
  other arithmetic  25 us (6%)
  blocking collectives  12.3 us (3%)
  local copies, waits for them, and re-layouts  11.8 us (3%)
    ppermute x18, waiting for transfers between devices, feed_forward(): got[s] = lax.ppermute(send, ('ctx', 'mp'), inward)  62.2 us
    ppermute x16, starting transfers between devices, feed_forward(): passed[s] = lax.ppermute(send, ('ctx', 'mp'), outward)  56.9 us
    ppermute x39, waiting for transfers between devices, swap(): return lax.ppermute(x, 'ctx', [(i, i ^ b) for i in range(self.C)])  54.7 us
    ppermute x39, starting transfers between devices, swap(): return lax.ppermute(x, 'ctx', [(i, i ^ b) for i in range(self.C)])  45.3 us
    ppermute x18, starting transfers between devices, feed_forward(): got[s] = lax.ppermute(send, ('ctx', 'mp'), inward)  23.3 us
    ppermute x6, waiting for transfers between devices, rotate_mp(): lax.ppermute(block_for(s), 'mp', [(i, (i + s) % self.M) for i in range(se...  22.8 us
    ppermute x8, starting transfers between devices, rows_to_slices(): lax.ppermute(payload[r % self.H], ('ctx', 'mp'), self.flat(pairs))  22 us
    dot_general x8, matrix products, part(): jnp.dot(normed, gate_weight[:, lo:hi], preferred_element_type=F32)  21.8 us
  transfers between devices with their start and end apart: 94, of which 52 were waited for; matrix products, arithmetic and copies ran while one was open for 9% of the time, Pallas kernels for 0%

profile of v7, /device:TPU:0, one launch (start us, length us, event | category | flops | bytes accessed | tf_op | source)
XLA Modules:
  0.0 431.3 jit_solution(8777562464811535989)
XLA Ops:
  7.0 4.8 %all-to-all-start = ((bf16[8,12,2048]{2,1,0:T(8,128)(2,1)}), bf16[8,12,2048]{2,1,0:T(8,128)(2,1)S(1)}, u32[]{:S(2)}, u32[]{:S(2)}) async-start(bf16[8,12,2048]{2,1,0:T(8,128)(2,1)} %reshape.187), calls=%async_computation | async-start | bytes 1048576 | tf_op jit(solution)/shard_map/all_to_all | solution.py:372
  35.6 5.7 %collective-permute-start.7 = (bf16[64,1024]{1,0:T(8,128)(2,1)S(1)}, bf16[64,1024]{1,0:T(8,128)(2,1)S(1)}, u32[]{:S(2)}, u32[]{:S(2)}) collective-permute-start(bf16[64,1024]{1,0:T(8,128)(2,1)S(1)} %get-tuple-element.162), channel_id=1, source_target_pairs={{0,6},{1,14},{2,22},{3,30},{4,2},{5,10},{6,18},{7,26},{8,7},{9,15}... | collective-permute-start | bytes 393224 | tf_op jit(solution)/shard_map/ppermute | solution.py:139
  41.3 4.9 %collective-permute-start.5 = (bf16[64,1024]{1,0:T(8,128)(2,1)S(1)}, bf16[64,1024]{1,0:T(8,128)(2,1)S(1)}, u32[]{:S(2)}, u32[]{:S(2)}) collective-permute-start(bf16[64,1024]{1,0:T(8,128)(2,1)S(1)} %get-tuple-element.162), channel_id=1, source_target_pairs={{0,5},{1,13},{2,21},{3,29},{4,1},{5,9},{6,17},{7,25},{8,4},{9,12},... | collective-permute-start | bytes 393224 | tf_op jit(solution)/shard_map/ppermute | solution.py:139
  46.4 4.6 %collective-permute-start.3 = (bf16[64,1024]{1,0:T(8,128)(2,1)S(1)}, bf16[64,1024]{1,0:T(8,128)(2,1)S(1)}, u32[]{:S(2)}, u32[]{:S(2)}) collective-permute-start(bf16[64,1024]{1,0:T(8,128)(2,1)S(1)} %get-tuple-element.162), channel_id=1, source_target_pairs={{0,4},{1,12},{2,20},{3,28},{4,0},{5,8},{6,16},{7,24},{8,5},{9,13},... | collective-permute-start | bytes 393224 | tf_op jit(solution)/shard_map/ppermute | solution.py:139
  54.7 11.6 %collective-permute-start.17 = (f32[256]{0:T(256)S(1)}, f32[256]{0:T(256)S(1)}, u32[]{:S(2)}, u32[]{:S(2)}) collective-permute-start(f32[256]{0:T(256)S(1)} %get-tuple-element.177), channel_id=1, source_target_pairs={{0,16},{4,20},{8,24},{12,28},{16,0},{20,4},{24,8},{28,12},{1,17},{... | collective-permute-start | bytes 3080 | tf_op jit(solution)/shard_map/ppermute | solution.py:56
  113.2 6.5 %collective-permute-done.28 = bf16[64,1024]{1,0:T(8,128)(2,1)S(1)} collective-permute-done((bf16[64,1024]{1,0:T(8,128)(2,1)S(1)}, bf16[64,1024]{1,0:T(8,128)(2,1)S(1)}, u32[]{:S(2)}, u32[]{:S(2)}) %collective-permute-start.28) | collective-permute-done | bytes 131104 | tf_op jit(solution)/shard_map/ppermute | solution.py:56
  119.6 5.5 %collective-permute-done.29 = bf16[64,1024]{1,0:T(8,128)(2,1)S(1)} collective-permute-done((bf16[64,1024]{1,0:T(8,128)(2,1)S(1)}, bf16[64,1024]{1,0:T(8,128)(2,1)S(1)}, u32[]{:S(2)}, u32[]{:S(2)}) %collective-permute-start.29) | collective-permute-done | bytes 131104 | tf_op jit(solution)/shard_map/ppermute | solution.py:56
  130.0 6.4 %collective-permute-done.34 = bf16[2,64,1024]{2,1,0:T(8,128)(2,1)S(1)} collective-permute-done((bf16[2,64,1024]{2,1,0:T(8,128)(2,1)S(1)}, bf16[2,64,1024]{2,1,0:T(8,128)(2,1)S(1)}, u32[]{:S(2)}, u32[]{:S(2)}) %collective-permute-start.34) | collective-permute-done | bytes 262176 | tf_op jit(solution)/shard_map/ppermute | solution.py:63
  136.5 4.4 %collective-permute-done.36 = bf16[2,64,1024]{2,1,0:T(8,128)(2,1)S(1)} collective-permute-done((bf16[2,64,1024]{2,1,0:T(8,128)(2,1)S(1)}, bf16[2,64,1024]{2,1,0:T(8,128)(2,1)S(1)}, u32[]{:S(2)}, u32[]{:S(2)}) %collective-permute-start.36) | collective-permute-done | bytes 262176 | tf_op jit(solution)/shard_map/ppermute | solution.py:63
  140.9 10.2 %collective-permute-done.35 = bf16[2,64,1024]{2,1,0:T(8,128)(2,1)S(1)} collective-permute-done((bf16[2,64,1024]{2,1,0:T(8,128)(2,1)S(1)}, bf16[2,64,1024]{2,1,0:T(8,128)(2,1)S(1)}, u32[]{:S(2)}, u32[]{:S(2)}) %collective-permute-start.35) | collective-permute-done | bytes 262176 | tf_op jit(solution)/shard_map/ppermute | solution.py:63
  214.5 8.3 %collective-permute-done.63 = bf16[512,512]{0,1:T(8,128)(2,1)S(1)} collective-permute-done((bf16[512,512]{0,1:T(8,128)(2,1)S(1)}, bf16[512,512]{0,1:T(8,128)(2,1)S(1)}, u32[]{:S(2)}, u32[]{:S(2)}) %collective-permute-start.63) | collective-permute-done | bytes 524320 | tf_op jit(solution)/shard_map/ppermute | solution.py:271
  224.3 4.1 collective-permute-done.48
  229.9 4.1 collective-permute-done.64
  235.7 4.0 collective-permute-done.49
  241.3 4.1 collective-permute-done.65
  247.3 4.6 %collective-permute-start.71 = (bf16[512,256]{0,1:T(8,128)(2,1)S(1)}, bf16[512,256]{0,1:T(8,128)(2,1)S(1)}, u32[]{:S(2)}, u32[]{:S(2)}) collective-permute-start(bf16[512,256]{0,1:T(8,128)(2,1)S(1)} %fusion.117), channel_id=1, source_target_pairs={{2,3},{1,2},{0,1},{5,4},{6,5},{7,6},{10,11},{9,10},{8,9},{13,12},{... | collective-permute-start | bytes 786440 | tf_op jit(solution)/shard_map/ppermute | solution.py:280
  257.2 3.7 collective-permute-done.66
  266.4 4.5 %collective-permute-done.51 = bf16[512,512]{0,1:T(8,128)(2,1)S(1)} collective-permute-done((bf16[512,512]{0,1:T(8,128)(2,1)S(1)}, bf16[512,512]{0,1:T(8,128)(2,1)S(1)}, u32[]{:S(2)}, u32[]{:S(2)}) %collective-permute-start.51) | collective-permute-done | bytes 524320 | tf_op jit(solution)/shard_map/ppermute | solution.py:271
  276.3 3.9 collective-permute-done.67
  280.8 3.8 collective-permute-start.73
  289.3 3.7 collective-permute-start.58
  297.8 3.7 collective-permute-start.74
  306.2 3.7 collective-permute-start.59
  314.7 3.7 collective-permute-start.75
  323.1 3.7 collective-permute-start.60
  331.4 4.0 collective-permute-start.76
  335.4 4.6 %collective-permute-done.55 = bf16[512,512]{0,1:T(8,128)(2,1)S(1)} collective-permute-done((bf16[512,512]{0,1:T(8,128)(2,1)S(1)}, bf16[512,512]{0,1:T(8,128)(2,1)S(1)}, u32[]{:S(2)}, u32[]{:S(2)}) %collective-permute-start.55) | collective-permute-done | bytes 524320 | tf_op jit(solution)/shard_map/ppermute | solution.py:271
  346.5 5.2 %collective-permute-start.77 = (bf16[512,256]{0,1:T(8,128)(2,1)S(1)}, bf16[512,256]{0,1:T(8,128)(2,1)S(1)}, u32[]{:S(2)}, u32[]{:S(2)}) collective-permute-start(bf16[512,256]{0,1:T(8,128)(2,1)S(1)} %broadcast_select_fusion.4), channel_id=1, source_target_pairs={{2,3},{1,2},{0,1},{5,4},{6,5},{7,6},{10,11},{9,10},{8,9},{13,12},{... | collective-permute-start | bytes 786440 | tf_op jit(solution)/shard_map/ppermute | solution.py:280
  351.7 3.9 collective-permute-start.62
  380.3 4.4 %collective-permute-start.87 = (bf16[512,256]{0,1:T(8,128)(2,1)S(1)}, bf16[512,256]{0,1:T(8,128)(2,1)S(1)}, u32[]{:S(2)}, u32[]{:S(2)}) collective-permute-start(bf16[512,256]{0,1:T(8,128)(2,1)S(1)} %fusion.115), channel_id=1, source_target_pairs={{0,1},{7,6},{8,9},{15,14},{16,17},{23,22},{24,25},{31,30}} | collective-permute-start | bytes 786440 | tf_op jit(solution)/shard_map/ppermute | solution.py:285
  401.9 6.1 %collective-permute-done.91 = bf16[2,64,1024]{2,1,0:T(8,128)(2,1)S(1)} collective-permute-done((bf16[2,64,1024]{2,1,0:T(8,128)(2,1)S(1)}, bf16[2,64,1024]{2,1,0:T(8,128)(2,1)S(1)}, u32[]{:S(2)}, u32[]{:S(2)}) %collective-permute-start.91) | collective-permute-done | bytes 262176 | tf_op jit(solution)/shard_map/ppermute | solution.py:56
  416.3 12.3 %all_to_all.10 = bf16[8,12,2048]{2,1,0:T(8,128)(2,1)S(1)} all-to-all(bf16[8,12,2048]{2,1,0:T(8,128)(2,1)S(1)} %reshape.196), channel_id=1, replica_groups=mesh['ctx'=8,'mp'=4] {'ctx'}, dimensions={0} | all-to-all | bytes 786432 | tf_op jit(solution)/shard_map/all_to_all | solution.py:491
  (425 shorter events, 259.8 us)
Async XLA Ops:
  0.7 19.5 %collective-permute-start = (f32[1,64]{1,0:T(1,128)S(1)}, f32[1,64]{1,0:T(1,128)S(1)}, u32[]{:S(2)}, u32[]{:S(2)}) collective-permute-start(f32[1,64]{1,0:T(1,128)S(1)} %get-tuple-element.185), channel_id=1, source_target_pairs={{0,4},{4,0},{8,12},{12,8},{16,20},{20,16},{24,28},{28,24},{1,5},{5... | collective-permute-start | bytes 776 | tf_op jit(solution)/shard_map/ppermute | solution.py:56
  7.0 20.8 %all-to-all-start = ((bf16[8,12,2048]{2,1,0:T(8,128)(2,1)}), bf16[8,12,2048]{2,1,0:T(8,128)(2,1)S(1)}, u32[]{:S(2)}, u32[]{:S(2)}) async-start(bf16[8,12,2048]{2,1,0:T(8,128)(2,1)} %reshape.187), calls=%async_computation | async-start | bytes 1048576 | tf_op jit(solution)/shard_map/all_to_all | solution.py:372
  34.5 16.7 %collective-permute-start.6 = (bf16[64,1024]{1,0:T(8,128)(2,1)S(1)}, bf16[64,1024]{1,0:T(8,128)(2,1)S(1)}, u32[]{:S(2)}, u32[]{:S(2)}) collective-permute-start(bf16[64,1024]{1,0:T(8,128)(2,1)S(1)} %get-tuple-element.161), channel_id=1, source_target_pairs={{0,1},{1,9},{2,17},{3,25},{4,5},{5,13},{6,21},{7,29},{8,0},{9,8},{... | collective-permute-start | bytes 393224 | tf_op jit(solution)/shard_map/ppermute | solution.py:139
  34.9 17.3 %collective-permute-start.4 = (bf16[64,1024]{1,0:T(8,128)(2,1)S(1)}, bf16[64,1024]{1,0:T(8,128)(2,1)S(1)}, u32[]{:S(2)}, u32[]{:S(2)}) collective-permute-start(bf16[64,1024]{1,0:T(8,128)(2,1)S(1)} %get-tuple-element.161), channel_id=1, source_target_pairs={{0,0},{1,8},{2,16},{3,24},{4,4},{5,12},{6,20},{7,28},{8,1},{9,9},{... | collective-permute-start | bytes 393224 | tf_op jit(solution)/shard_map/ppermute | solution.py:139
  35.6 15.4 %collective-permute-start.7 = (bf16[64,1024]{1,0:T(8,128)(2,1)S(1)}, bf16[64,1024]{1,0:T(8,128)(2,1)S(1)}, u32[]{:S(2)}, u32[]{:S(2)}) collective-permute-start(bf16[64,1024]{1,0:T(8,128)(2,1)S(1)} %get-tuple-element.162), channel_id=1, source_target_pairs={{0,6},{1,14},{2,22},{3,30},{4,2},{5,10},{6,18},{7,26},{8,7},{9,15}... | collective-permute-start | bytes 393224 | tf_op jit(solution)/shard_map/ppermute | solution.py:139
  54.6 18.9 %collective-permute-start.11 = (bf16[512,768]{1,0:T(8,128)(2,1)S(1)}, bf16[512,768]{1,0:T(8,128)(2,1)S(1)}, u32[]{:S(2)}, u32[]{:S(2)}) collective-permute-start(bf16[512,768]{1,0:T(8,128)(2,1)S(1)} %convolution_convert_fusion.2), channel_id=1, source_target_pairs={{0,4},{4,0},{8,12},{12,8},{16,20},{20,16},{24,28},{28,24},{1,5},{5... | collective-permute-start | bytes 2359304 | tf_op jit(solution)/shard_map/ppermute | solution.py:56
  107.6 17.7 %collective-permute-start.33 = (bf16[64,1024]{1,0:T(8,128)(2,1)S(1)}, bf16[64,1024]{1,0:T(8,128)(2,1)S(1)}, u32[]{:S(2)}, u32[]{:S(2)}) collective-permute-start(bf16[64,1024]{1,0:T(8,128)(2,1)S(1)} %get-tuple-element.76), channel_id=1, source_target_pairs={{0,28},{4,24},{8,20},{12,16},{16,12},{20,8},{24,4},{28,0},{1,29},{... | collective-permute-start | bytes 393224 | tf_op jit(solution)/shard_map/ppermute | solution.py:56
  108.8 16.5 %collective-permute-start.32 = (bf16[64,1024]{1,0:T(8,128)(2,1)S(1)}, bf16[64,1024]{1,0:T(8,128)(2,1)S(1)}, u32[]{:S(2)}, u32[]{:S(2)}) collective-permute-start(bf16[64,1024]{1,0:T(8,128)(2,1)S(1)} %get-tuple-element.77), channel_id=1, source_target_pairs={{0,24},{4,28},{8,16},{12,20},{16,8},{20,12},{24,0},{28,4},{1,25},{... | collective-permute-start | bytes 393224 | tf_op jit(solution)/shard_map/ppermute | solution.py:56
  110.5 14.8 %collective-permute-start.31 = (bf16[64,1024]{1,0:T(8,128)(2,1)S(1)}, bf16[64,1024]{1,0:T(8,128)(2,1)S(1)}, u32[]{:S(2)}, u32[]{:S(2)}) collective-permute-start(bf16[64,1024]{1,0:T(8,128)(2,1)S(1)} %get-tuple-element.78), channel_id=1, source_target_pairs={{0,20},{4,16},{8,28},{12,24},{16,4},{20,0},{24,12},{28,8},{1,21},{... | collective-permute-start | bytes 393224 | tf_op jit(solution)/shard_map/ppermute | solution.py:56
  126.6 14.3 %collective-permute-start.36 = (bf16[2,64,1024]{2,1,0:T(8,128)(2,1)S(1)}, bf16[2,64,1024]{2,1,0:T(8,128)(2,1)S(1)}, u32[]{:S(2)}, u32[]{:S(2)}) collective-permute-start(bf16[2,64,1024]{2,1,0:T(8,128)(2,1)S(1)} %get-tuple-element.74), channel_id=1, source_target_pairs={{0,3},{1,0},{2,1},{3,2},{4,7},{5,4},{6,5},{7,6},{8,11},{9,8},{10,9... | collective-permute-start | bytes 786440 | tf_op jit(solution)/shard_map/ppermute | solution.py:63
  129.3 21.8 %collective-permute-start.35 = (bf16[2,64,1024]{2,1,0:T(8,128)(2,1)S(1)}, bf16[2,64,1024]{2,1,0:T(8,128)(2,1)S(1)}, u32[]{:S(2)}, u32[]{:S(2)}) collective-permute-start(bf16[2,64,1024]{2,1,0:T(8,128)(2,1)S(1)} %get-tuple-element.75), channel_id=1, source_target_pairs={{0,2},{1,3},{2,0},{3,1},{4,6},{5,7},{6,4},{7,5},{8,10},{9,11},{10,... | collective-permute-start | bytes 786440 | tf_op jit(solution)/shard_map/ppermute | solution.py:63
  213.1 15.3 %collective-permute-start.48 = (bf16[512,512]{0,1:T(8,128)(2,1)S(1)}, bf16[512,512]{0,1:T(8,128)(2,1)S(1)}, u32[]{:S(2)}, u32[]{:S(2)}) collective-permute-start(bf16[512,512]{0,1:T(8,128)(2,1)S(1)} %select_select_fusion.1), channel_id=1, source_target_pairs={{3,2},{2,1},{1,0},{4,5},{5,6},{6,7},{11,10},{10,9},{9,8},{12,13},{... | collective-permute-start | bytes 1572872 | tf_op jit(solution)/shard_map/ppermute | solution.py:271
  245.8 15.1 %collective-permute-start.66 = (bf16[512,512]{0,1:T(8,128)(2,1)S(1)}, bf16[512,512]{0,1:T(8,128)(2,1)S(1)}, u32[]{:S(2)}, u32[]{:S(2)}) collective-permute-start(bf16[512,512]{0,1:T(8,128)(2,1)S(1)} %get-tuple-element.145), channel_id=1, source_target_pairs={{3,2},{2,1},{1,0},{4,5},{5,6},{6,7},{11,10},{10,9},{9,8},{12,13},{... | collective-permute-start | bytes 1572872 | tf_op jit(solution)/shard_map/ppermute | solution.py:271
  252.4 18.9 %collective-permute-start.56 = (bf16[512,256]{0,1:T(8,128)(2,1)S(1)}, bf16[512,256]{0,1:T(8,128)(2,1)S(1)}, u32[]{:S(2)}, u32[]{:S(2)}) collective-permute-start(bf16[512,256]{0,1:T(8,128)(2,1)S(1)} %fusion.123), channel_id=1, source_target_pairs={{2,3},{1,2},{0,1},{5,4},{6,5},{7,6},{10,11},{9,10},{8,9},{13,12},{... | collective-permute-start | bytes 786440 | tf_op jit(solution)/shard_map/ppermute | solution.py:280
  255.9 15.0 %collective-permute-start.51 = (bf16[512,512]{0,1:T(8,128)(2,1)S(1)}, bf16[512,512]{0,1:T(8,128)(2,1)S(1)}, u32[]{:S(2)}, u32[]{:S(2)}) collective-permute-start(bf16[512,512]{0,1:T(8,128)(2,1)S(1)} %get-tuple-element.127), channel_id=1, source_target_pairs={{3,2},{2,1},{1,0},{4,5},{5,6},{6,7},{11,10},{10,9},{9,8},{12,13},{... | collective-permute-start | bytes 1572872 | tf_op jit(solution)/shard_map/ppermute | solution.py:271
  261.5 19.1 %collective-permute-start.72 = (bf16[512,256]{0,1:T(8,128)(2,1)S(1)}, bf16[512,256]{0,1:T(8,128)(2,1)S(1)}, u32[]{:S(2)}, u32[]{:S(2)}) collective-permute-start(bf16[512,256]{0,1:T(8,128)(2,1)S(1)} %get-tuple-element.25), channel_id=1, source_target_pairs={{2,3},{1,2},{0,1},{5,4},{6,5},{7,6},{10,11},{9,10},{8,9},{13,12},{... | collective-permute-start | bytes 786440 | tf_op jit(solution)/shard_map/ppermute | solution.py:280
  265.1 15.1 %collective-permute-start.67 = (bf16[512,512]{0,1:T(8,128)(2,1)S(1)}, bf16[512,512]{0,1:T(8,128)(2,1)S(1)}, u32[]{:S(2)}, u32[]{:S(2)}) collective-permute-start(bf16[512,512]{0,1:T(8,128)(2,1)S(1)} %get-tuple-element.143), channel_id=1, source_target_pairs={{3,2},{2,1},{1,0},{4,5},{5,6},{6,7},{11,10},{10,9},{9,8},{12,13},{... | collective-permute-start | bytes 1572872 | tf_op jit(solution)/shard_map/ppermute | solution.py:271
  271.5 17.6 %collective-permute-start.57 = (bf16[512,256]{0,1:T(8,128)(2,1)S(1)}, bf16[512,256]{0,1:T(8,128)(2,1)S(1)}, u32[]{:S(2)}, u32[]{:S(2)}) collective-permute-start(bf16[512,256]{0,1:T(8,128)(2,1)S(1)} %get-tuple-element.35), channel_id=1, source_target_pairs={{2,3},{1,2},{0,1},{5,4},{6,5},{7,6},{10,11},{9,10},{8,9},{13,12},{... | collective-permute-start | bytes 786440 | tf_op jit(solution)/shard_map/ppermute | solution.py:280
  280.8 16.8 %collective-permute-start.73 = (bf16[512,256]{0,1:T(8,128)(2,1)S(1)}, bf16[512,256]{0,1:T(8,128)(2,1)S(1)}, u32[]{:S(2)}, u32[]{:S(2)}) collective-permute-start(bf16[512,256]{0,1:T(8,128)(2,1)S(1)} %get-tuple-element.23), channel_id=1, source_target_pairs={{2,3},{1,2},{0,1},{5,4},{6,5},{7,6},{10,11},{9,10},{8,9},{13,12},{... | collective-permute-start | bytes 786440 | tf_op jit(solution)/shard_map/ppermute | solution.py:280
  289.3 16.7 %collective-permute-start.58 = (bf16[512,256]{0,1:T(8,128)(2,1)S(1)}, bf16[512,256]{0,1:T(8,128)(2,1)S(1)}, u32[]{:S(2)}, u32[]{:S(2)}) collective-permute-start(bf16[512,256]{0,1:T(8,128)(2,1)S(1)} %get-tuple-element.33), channel_id=1, source_target_pairs={{2,3},{1,2},{0,1},{5,4},{6,5},{7,6},{10,11},{9,10},{8,9},{13,12},{... | collective-permute-start | bytes 786440 | tf_op jit(solution)/shard_map/ppermute | solution.py:280
  297.8 16.7 %collective-permute-start.74 = (bf16[512,256]{0,1:T(8,128)(2,1)S(1)}, bf16[512,256]{0,1:T(8,128)(2,1)S(1)}, u32[]{:S(2)}, u32[]{:S(2)}) collective-permute-start(bf16[512,256]{0,1:T(8,128)(2,1)S(1)} %get-tuple-element.21), channel_id=1, source_target_pairs={{2,3},{1,2},{0,1},{5,4},{6,5},{7,6},{10,11},{9,10},{8,9},{13,12},{... | collective-permute-start | bytes 786440 | tf_op jit(solution)/shard_map/ppermute | solution.py:280
  306.2 16.6 %collective-permute-start.59 = (bf16[512,256]{0,1:T(8,128)(2,1)S(1)}, bf16[512,256]{0,1:T(8,128)(2,1)S(1)}, u32[]{:S(2)}, u32[]{:S(2)}) collective-permute-start(bf16[512,256]{0,1:T(8,128)(2,1)S(1)} %get-tuple-element.31), channel_id=1, source_target_pairs={{2,3},{1,2},{0,1},{5,4},{6,5},{7,6},{10,11},{9,10},{8,9},{13,12},{... | collective-permute-start | bytes 786440 | tf_op jit(solution)/shard_map/ppermute | solution.py:280
  314.7 16.5 %collective-permute-start.75 = (bf16[512,256]{0,1:T(8,128)(2,1)S(1)}, bf16[512,256]{0,1:T(8,128)(2,1)S(1)}, u32[]{:S(2)}, u32[]{:S(2)}) collective-permute-start(bf16[512,256]{0,1:T(8,128)(2,1)S(1)} %get-tuple-element.19), channel_id=1, source_target_pairs={{2,3},{1,2},{0,1},{5,4},{6,5},{7,6},{10,11},{9,10},{8,9},{13,12},{... | collective-permute-start | bytes 786440 | tf_op jit(solution)/shard_map/ppermute | solution.py:280
  323.1 17.2 %collective-permute-start.60 = (bf16[512,256]{0,1:T(8,128)(2,1)S(1)}, bf16[512,256]{0,1:T(8,128)(2,1)S(1)}, u32[]{:S(2)}, u32[]{:S(2)}) collective-permute-start(bf16[512,256]{0,1:T(8,128)(2,1)S(1)} %get-tuple-element.29), channel_id=1, source_target_pairs={{2,3},{1,2},{0,1},{5,4},{6,5},{7,6},{10,11},{9,10},{8,9},{13,12},{... | collective-permute-start | bytes 786440 | tf_op jit(solution)/shard_map/ppermute | solution.py:280
  331.4 15.1 %collective-permute-start.76 = (bf16[512,256]{0,1:T(8,128)(2,1)S(1)}, bf16[512,256]{0,1:T(8,128)(2,1)S(1)}, u32[]{:S(2)}, u32[]{:S(2)}) collective-permute-start(bf16[512,256]{0,1:T(8,128)(2,1)S(1)} %get-tuple-element.17), channel_id=1, source_target_pairs={{2,3},{1,2},{0,1},{5,4},{6,5},{7,6},{10,11},{9,10},{8,9},{13,12},{... | collective-permute-start | bytes 786440 | tf_op jit(solution)/shard_map/ppermute | solution.py:280
  343.8 15.4 %collective-permute-start.80 = (bf16[512,512]{0,1:T(8,128)(2,1)S(1)}, bf16[512,512]{0,1:T(8,128)(2,1)S(1)}, u32[]{:S(2)}, u32[]{:S(2)}) collective-permute-start(bf16[512,512]{0,1:T(8,128)(2,1)S(1)} %get-tuple-element.91), channel_id=1, source_target_pairs={{3,2},{2,1},{1,0},{4,5},{5,6},{6,7},{11,10},{10,9},{9,8},{12,13},{... | collective-permute-start | bytes 1572872 | tf_op jit(solution)/shard_map/ppermute | solution.py:271
  345.1 30.0 %collective-permute-start.84 = (bf16[512,512]{0,1:T(8,128)(2,1)S(1)}, bf16[512,512]{0,1:T(8,128)(2,1)S(1)}, u32[]{:S(2)}, u32[]{:S(2)}) collective-permute-start(bf16[512,512]{0,1:T(8,128)(2,1)S(1)} %get-tuple-element.89), channel_id=1, source_target_pairs={{3,2},{2,1},{1,0},{4,5},{5,6},{6,7},{11,10},{10,9},{9,8},{12,13},{... | collective-permute-start | bytes 1572872 | tf_op jit(solution)/shard_map/ppermute | solution.py:271
  346.5 21.1 %collective-permute-start.77 = (bf16[512,256]{0,1:T(8,128)(2,1)S(1)}, bf16[512,256]{0,1:T(8,128)(2,1)S(1)}, u32[]{:S(2)}, u32[]{:S(2)}) collective-permute-start(bf16[512,256]{0,1:T(8,128)(2,1)S(1)} %broadcast_select_fusion.4), channel_id=1, source_target_pairs={{2,3},{1,2},{0,1},{5,4},{6,5},{7,6},{10,11},{9,10},{8,9},{13,12},{... | collective-permute-start | bytes 786440 | tf_op jit(solution)/shard_map/ppermute | solution.py:280
  359.6 27.2 %collective-permute-start.83 = (bf16[512,256]{0,1:T(8,128)(2,1)S(1)}, bf16[512,256]{0,1:T(8,128)(2,1)S(1)}, u32[]{:S(2)}, u32[]{:S(2)}) collective-permute-start(bf16[512,256]{0,1:T(8,128)(2,1)S(1)} %fusion.116), channel_id=1, source_target_pairs={{0,1},{7,6},{8,9},{15,14},{16,17},{23,22},{24,25},{31,30}} | collective-permute-start | bytes 786440 | tf_op jit(solution)/shard_map/ppermute | solution.py:285
  362.9 25.2 %collective-permute-start.82 = (bf16[512,256]{0,1:T(8,128)(2,1)S(1)}, bf16[512,256]{0,1:T(8,128)(2,1)S(1)}, u32[]{:S(2)}, u32[]{:S(2)}) collective-permute-start(bf16[512,256]{0,1:T(8,128)(2,1)S(1)} %fusion.116), channel_id=1, source_target_pairs={{0,2},{7,5},{8,10},{15,13},{16,18},{23,21},{24,26},{31,29}} | collective-permute-start | bytes 786440 | tf_op jit(solution)/shard_map/ppermute | solution.py:285
  364.2 23.9 %collective-permute-start.81 = (bf16[512,256]{0,1:T(8,128)(2,1)S(1)}, bf16[512,256]{0,1:T(8,128)(2,1)S(1)}, u32[]{:S(2)}, u32[]{:S(2)}) collective-permute-start(bf16[512,256]{0,1:T(8,128)(2,1)S(1)} %fusion.116), channel_id=1, source_target_pairs={{0,3},{7,4},{8,11},{15,12},{16,19},{23,20},{24,27},{31,28}} | collective-permute-start | bytes 786440 | tf_op jit(solution)/shard_map/ppermute | solution.py:285
  368.2 16.6 %collective-permute-start.79 = (bf16[512,256]{0,1:T(8,128)(2,1)S(1)}, bf16[512,256]{0,1:T(8,128)(2,1)S(1)}, u32[]{:S(2)}, u32[]{:S(2)}) collective-permute-start(bf16[512,256]{0,1:T(8,128)(2,1)S(1)} %get-tuple-element.153), channel_id=1, source_target_pairs={{2,3},{1,2},{0,1},{5,4},{6,5},{7,6},{10,11},{9,10},{8,9},{13,12},{... | collective-permute-start | bytes 786440 | tf_op jit(solution)/shard_map/ppermute | solution.py:280
  (78 other events, 673.8 us)
